TPU v7x, 32 devices: a whole 2x2x4 slice. The times are simulated.
32 devices in a mesh: px: 8 (over z, y), py: 4 (over x, core).
Axes of the slice: x: 2, y: 2, z: 4, core: 2. Of those that a mesh axis runs over, the one named last changes fastest.
Arguments:
- initial_field: float32 [1, 2048, 2048], P(None, ('px', 'py')), may hold values from -6 to 6
- target_field: float32 [1, 2048, 2048], P(None, ('px', 'py')), may hold values from -6 to 6
- forcing: float32 [2, 2048, 2048], P(None, ('px', 'py')), may hold values from -6 to 6
Outputs:
- next_field: float32 [1, 2048, 2048], P(None, ('px', 'py'))
- objective: float32 [], replicated
- field_grad: float32 [1, 2048, 2048], P(None, ('px', 'py'))
- forcing_grad: float32 [2, 2048, 2048], P(None, ('px', 'py'))
All inputs are finite; a program needn't handle non-finite values.
Results may differ from a plain program's by a relative error of at most 0.00014.
Values sent between devices are 32-bit elements; how exact they have to be, the bound alone decides.
A program may use at most 128 MiB of HBM per device.

v0:
```python
import functools
import math

import jax
import jax.numpy as jnp
import numpy as np
from jax import lax
from jax.experimental import pallas as pl
from jax.experimental.pallas import tpu as pltpu
from jax.sharding import PartitionSpec as P

time_step = 0.25
axes = ("px", "py")
TILE = 128


def split_length(length):
    inner = 256 if length % 256 == 0 else TILE
    return (length // inner, inner)


def small_dft(items, sign):
    count = len(items)
    if count == 1:
        return items
    evens = small_dft(items[0::2], sign)
    odds = small_dft(items[1::2], sign)
    low, high = [], []
    for k in range(count // 2):
        odd_re, odd_im = odds[k]
        if 4 * k == count:
            odd_re, odd_im = (-odd_im, odd_re) if sign > 0 else (odd_im, -odd_re)
        elif k:
            c = math.cos(2.0 * math.pi * k / count)
            s = sign * math.sin(2.0 * math.pi * k / count)
            if abs(abs(c) - abs(s)) < 1e-12:
                sc, ss = math.copysign(1.0, c), math.copysign(1.0, s)
                odd_re, odd_im = (
                    c * (odd_re - sc * ss * odd_im),
                    c * (odd_im + sc * ss * odd_re),
                )
            else:
                odd_re, odd_im = (c * odd_re - s * odd_im, c * odd_im + s * odd_re)
        even_re, even_im = evens[k]
        low.append((even_re + odd_re, even_im + odd_im))
        high.append((even_re - odd_re, even_im - odd_im))
    return low + high


def halves(value):
    top = value.astype(jnp.bfloat16)
    return top, (value - top.astype(jnp.float32)).astype(jnp.bfloat16)


def orders(length, rows):
    inner = split_length(length)[1]
    half = rows // 2
    lane = np.arange(inner)
    natural = lane
    local = lane % (inner // 2)
    line = local % half
    kept = rows * (local // half) + np.where((lane >= inner // 2) & (line == 0), half, line)
    groups = TILE // rows
    tall = rows // groups
    within = lane % (inner // groups)
    lines = rows * (within // tall) + tall * (lane // (inner // groups)) + within % tall
    return natural, kept, lines


def twiddle_table(length, order):
    outer = split_length(length)[0]
    angle = 2.0 * np.pi * np.outer(np.arange(outer), order) / length
    return (np.stack([np.cos(angle), np.sin(angle)]) / math.sqrt(length)).astype(np.float32)


def matrix_table(length, sign, left, right):
    inner = split_length(length)[1]
    angle = 2.0 * np.pi * (np.outer(left, right) % inner) / inner
    c, s = np.cos(angle), np.sin(angle)
    full = np.block([[c, sign * s], [-sign * s, c]])
    top = full.astype(jnp.bfloat16)
    return np.stack([top, (full - top.astype(np.float64)).astype(jnp.bfloat16)])


def mirror_table(length):
    inner = split_length(length)[1]
    lane = np.arange(inner)
    both = np.zeros((2, inner, inner))
    both[0, (inner - lane) % inner, lane] = 1.0
    both[1, inner - 1 - lane, lane] = 1.0
    return both.astype(jnp.bfloat16)


class Pieces:
    def __init__(self, length, rows, turned=None, top=None, low=None, grid_out=None):
        self.length, self.rows, self.half = length, rows, rows // 2
        self.outer, self.inner = split_length(length)
        self.turned, self.top, self.low, self.z = turned, top, low, grid_out
        self.step = math.gcd(rows // 2, 16)

    def chunks(self, lines, body):
        def run(i, carry):
            body(pl.multiple_of(i * self.step, self.step))
            return carry

        lax.fori_loop(0, lines // self.step, run, 0)

    def put(self, k, at, part, value):
        lanes = pl.ds(part * self.inner, self.inner)
        top, low = halves(value)
        self.top[k, at, lanes] = top
        self.low[k, at, lanes] = low

    def get(self, k, at, part):
        return self.z[k, at, pl.ds(part * self.inner, self.inner)]

    def multiply(self, lines, matrix, real_in=False, real_out=False):
        deep = self.inner if real_in else 2 * self.inner
        wide = self.inner if real_out else 2 * self.inner
        count = self.outer * lines
        top = self.top[:, :lines, :deep].reshape(count, deep)
        low = self.low[:, :lines, :deep].reshape(count, deep)
        right_top = matrix[0, :deep, :wide]
        right_low = matrix[1, :deep, :wide]
        dot = functools.partial(jnp.dot, preferred_element_type=jnp.float32)
        total = dot(top, right_top) + dot(low, right_top) + dot(top, right_low)
        self.z[:, :lines, :wide] = total.reshape(self.outer, lines, wide)

    def twist(self, k, pair, sign, twiddle):
        c = twiddle[0, pl.ds(k, 1), :]
        s = twiddle[1, pl.ds(k, 1), :]
        s = s if sign > 0 else -s
        re, im = pair
        return (re * c - im * s, re * s + im * c)

    def turn_full(self, source):
        rows, blocks = self.rows, TILE // self.rows
        for t in range(self.length // TILE):
            tile = source[pl.ds(t * blocks, blocks), :rows, :].reshape(TILE, 2 * rows)
            self.turned[: 2 * rows, pl.ds(t * TILE, TILE)] = tile.T

    def turn_lines(self, source):
        rows = self.rows
        groups = TILE // rows
        blocks, wide = self.inner // rows, self.inner // groups
        for t in range(self.outer):
            tile = source[pl.ds(t * blocks, blocks), :, :].reshape(wide, TILE).T
            for h in range(groups):
                self.turned[:rows, pl.ds(t * self.inner + h * wide, wide)] = tile[h * rows : (h + 1) * rows]

    def kept_lanes(self, j):
        wide = self.inner // 2
        return j * self.inner + (wide if 2 * j >= self.outer else 0), wide

    def clear_other(self, j):
        at, wide = self.kept_lanes(j)
        other = j * self.inner + (0 if 2 * j >= self.outer else wide)
        self.turned[: 2 * self.rows, pl.ds(other, wide)] = jnp.zeros((2 * self.rows, wide), jnp.float32)

    def turn_kept(self, source):
        rows, half, blocks = self.rows, self.half, self.inner // self.rows
        for j in range(self.outer):
            at, wide = self.kept_lanes(j)
            tile = source[pl.ds(j * blocks, blocks), :, :].reshape(wide, 2 * rows)
            self.turned[: 2 * rows, pl.ds(at, wide)] = tile.T
            self.clear_other(j)

    def unpack_middle(self):
        rows, middle = self.rows, (self.outer // 2) * self.inner
        first = self.turned[rows : 2 * rows, :TILE]
        lane0 = lax.broadcasted_iota(jnp.int32, first.shape, 1) == 0
        zero = jnp.zeros_like(first)
        self.turned[:rows, pl.ds(middle, TILE)] += jnp.where(lane0, first, zero)
        self.turned[rows : 2 * rows, :TILE] = jnp.where(lane0, zero, first)

    def incoming(self, lines, sign, twiddle, matrix, real_out=False):
        def body(r0):
            items = []
            for j in range(self.outer):
                lanes = pl.ds(j * self.inner, self.inner)
                items.append((
                    self.turned[pl.ds(r0, self.step), lanes],
                    self.turned[pl.ds(lines + r0, self.step), lanes],
                ))
            for k, pair in enumerate(small_dft(items, sign)):
                re, im = self.twist(k, pair, sign, twiddle)
                self.put(k, pl.ds(r0, self.step), 0, re)
                self.put(k, pl.ds(r0, self.step), 1, im)

        self.chunks(lines, body)
        self.multiply(lines, matrix, real_out=real_out)

    def outgoing(self, lines, sign, twiddle, matrix, real_in, write):
        self.multiply(lines, matrix, real_in=real_in)

        def body(r0):
            at = pl.ds(r0, self.step)
            write(r0, small_dft([
                self.twist(k, (self.get(k, at, 0), self.get(k, at, 1)), sign, twiddle)
                for k in range(self.outer)
            ], sign))

        self.chunks(lines, body)

    def pack_middle(self, items):
        re, im = items[0]
        lane0 = lax.broadcasted_iota(jnp.int32, im.shape, 1) == 0
        return [(re, jnp.where(lane0, items[self.outer // 2][0], im))] + items[1:]

    def write_full(self, result, pack):
        rows = self.rows

        def write(r0, items):
            at = pl.ds(r0, self.step)
            for j, (re, im) in enumerate(self.pack_middle(items) if pack else items):
                for piece in range(self.inner // rows):
                    to = j * (self.inner // rows) + piece
                    lanes = slice(piece * rows, (piece + 1) * rows)
                    result[to, at, pl.ds(0, rows)] = re[:, lanes]
                    result[to, at, pl.ds(rows, rows)] = im[:, lanes]

        return write

    def outgoing_kept(self, twiddle, matrix, result):
        self.multiply(self.rows, matrix, real_in=True)
        rows, half, blocks = self.rows, self.half, self.inner // self.rows
        tall = rows * rows // TILE
        step = math.gcd(rows, 16)
        span = min(tall, step)
        for h in range(rows // max(tall, step)):

            def body(i, carry, h=h):
                r0 = i * step if isinstance(i, int) else pl.multiple_of(i * step, step)
                at = pl.ds(h * max(tall, step) + r0, step)
                items = self.pack_middle(small_dft([
                    self.twist(k, (self.get(k, at, 0), self.get(k, at, 1)), -1.0, twiddle)
                    for k in range(self.outer)
                ], -1.0))
                for j, pair in enumerate(items):
                    base = self.inner // 2 if 2 * j >= self.outer else 0
                    for piece in range(blocks):
                        lanes = slice(base + piece * half, base + (piece + 1) * half)
                        for part, value in enumerate(pair):
                            for sub in range(step // span):
                                group = h * (step // span) + sub
                                to = pl.ds(group * rows + part * half, half)
                                held = value[sub * span : (sub + 1) * span, lanes]
                                result[j * blocks + piece, pl.ds(r0, span), to] = held
                return carry

            if tall > step:
                lax.fori_loop(0, tall // step, body, 0)
            else:
                body(0, 0)

    def mirrored(self, blocks, mirror):
        dot = functools.partial(jnp.dot, preferred_element_type=jnp.float32)

        def flip(values, which):
            top, low = halves(jnp.concatenate(values, axis=0))
            return dot(top, mirror[which]) + dot(low, mirror[which])

        flat = [part for k in range(self.outer) for pair in blocks[k] for part in pair]
        per = 2 * len(blocks[0])
        low = flip(flat[:per], 0)
        high = flip(flat[per:], 1)
        out = []
        for k in range(self.outer):
            part, base = (low, 0) if k == 0 else (high, (self.outer - k - 1) * per)
            take = lambda i: part[(base + i) * 8 : (base + i + 1) * 8]
            out.append([(take(2 * i), -take(2 * i + 1)) for i in range(per // 2)])
        return out

    def spread(self, first, second, strided, result):
        rows, fill = self.rows, TILE - 2 * self.rows
        for t in range(self.length // TILE):
            lanes = pl.ds(t * TILE, TILE)
            parts = [first[:, lanes], second[:, lanes]]
            if fill:
                parts.append(jnp.zeros((fill, TILE), jnp.float32))
            strided[pl.ds(t * TILE, TILE), :] = jnp.concatenate(parts, axis=0).T
        for k in range(self.outer):
            slab = strided[pl.ds(k, self.inner, stride=self.outer), :].T
            result[k] = slab[: 2 * rows, :]

    def collect(self, slabs, strided, results):
        rows = self.rows
        for k in range(self.outer):
            slab = slabs(k)
            fill = TILE - slab.shape[0]
            if fill:
                slab = jnp.concatenate([slab, jnp.zeros((fill, self.inner), jnp.float32)], axis=0)
            strided[pl.ds(k, self.inner, stride=self.outer), :] = slab.T
        for t in range(self.length // TILE):
            block = strided[pl.ds(t * TILE, TILE), :].T
            for i, result in enumerate(results):
                result[:, pl.ds(t * TILE, TILE)] = block[i * rows : (i + 1) * rows, :]


def signed_waves(position, count):
    signed = jnp.where(position < count // 2, position, position - count)
    waves = 4.0 * signed.astype(jnp.float32) / count
    return waves, jnp.where(position == count // 2, jnp.float32(0.0), waves)


def first_waves(piece, k):
    lanes = lax.broadcasted_iota(jnp.int32, (1, piece.inner), 1)
    return signed_waves(piece.outer * lanes + k, piece.length)


def inverse_denominator(wave_first, wave_second):
    square = wave_first * wave_first + wave_second * wave_second
    return 1.0 / (1.0 + time_step * (square * square - square))


def second_wave(piece, position):
    shape = (position.shape[0], piece.inner)
    return jnp.broadcast_to(signed_waves(position, piece.length)[0], shape)


def row_index(count, width):
    return lax.broadcasted_iota(jnp.int32, (count, width), 0)


def start_kernel(length, rows, field, target, twiddle, matrix, out, both_p, *scratch):
    piece = Pieces(length, rows, *scratch[:4])
    piece.spread(field, target, scratch[4], both_p)

    def body(r0):
        at = pl.ds(r0, piece.step)
        for k in range(piece.outer):
            piece.put(k, at, 0, both_p[k, at, :])

    piece.chunks(rows, body)
    piece.outgoing_kept(twiddle, matrix, out)


def slope_second_kernel(length, rows, field_p, twiddle, out_matrix, in_matrix, kept, result, *scratch):
    piece = Pieces(length, rows, *scratch)

    def body(r0):
        at = pl.ds(r0, piece.step)
        for k in range(piece.outer):
            piece.put(k, at, 0, field_p[k, at, :])

    piece.chunks(rows, body)
    for j in range(piece.outer):
        piece.clear_other(j)

    def write(r0, items):
        for j, (re, im) in enumerate(items):
            at, wide = piece.kept_lanes(j)
            base = at - j * piece.inner
            position = j * piece.inner + kept[:, base : base + wide]
            slope = 2.0 * signed_waves(position, length)[1]
            piece.turned[pl.ds(r0, piece.step), pl.ds(at, wide)] = -slope * im[:, base : base + wide]
            piece.turned[pl.ds(rows + r0, piece.step), pl.ds(at, wide)] = slope * re[:, base : base + wide]

    piece.outgoing(rows, -1.0, twiddle, out_matrix, True, write)
    piece.incoming(rows, 1.0, twiddle, in_matrix, real_out=True)
    result[...] = piece.z[:, :, : piece.inner]


def spread_kernel(length, rows, forcing, result, strided):
    Pieces(length, rows).spread(forcing.at[0], forcing.at[1], strided, result)


def collect_kernel(length, rows, slabs, result, strided):
    piece = Pieces(length, rows)
    piece.collect(lambda k: slabs[k], strided, [result.at[i] for i in range(result.shape[0])])


def weight_of(device, r0, step, inner):
    alone = (row_index(step, inner) + r0 + device) == 0
    return jnp.where(alone, jnp.float32(1.0), jnp.float32(2.0))


def slope_kernel(length, rows, device_ref, source, in_twiddle, in_matrix, out_twiddle, out_matrix, out, state, *scratch):
    device = device_ref[0]
    piece = Pieces(length, rows, *scratch)
    half = piece.half
    piece.turn_lines(source)
    piece.incoming(half, -1.0, in_twiddle, in_matrix)

    def body(r0):
        at, also = pl.ds(r0, piece.step), pl.ds(half + r0, piece.step)
        weight = weight_of(device, r0, piece.step, piece.inner)
        for k in range(piece.outer):
            re, im = piece.get(k, at, 0), piece.get(k, at, 1)
            state[k, at, :], state[k, also, :] = re, im
            scale = first_waves(piece, k)[1] * weight
            piece.put(k, at, 0, -scale * im)
            piece.put(k, at, 1, scale * re)

    piece.chunks(half, body)
    piece.outgoing(half, 1.0, out_twiddle, out_matrix, False, piece.write_full(out, False))


def total_kernel(length, rows, device_ref, source, coef, in_twiddle, in_matrix, out_twiddle, out_matrix, out, *scratch):
    device = device_ref[0]
    piece = Pieces(length, rows, *scratch)
    half = piece.half
    piece.turn_lines(source)
    piece.incoming(half, -1.0, in_twiddle, in_matrix)

    def body(r0):
        at, also = pl.ds(r0, piece.step), pl.ds(half + r0, piece.step)
        weight = weight_of(device, r0, piece.step, piece.inner)
        for k in range(piece.outer):
            re, im = piece.get(k, at, 0), piece.get(k, at, 1)
            deriv = first_waves(piece, k)[1]
            scale = 1.0 / time_step
            piece.put(k, at, 0, weight * (scale * coef[k, at, :] - deriv * im))
            piece.put(k, at, 1, weight * (scale * coef[k, also, :] + deriv * re))

    piece.chunks(half, body)
    piece.outgoing(half, 1.0, out_twiddle, out_matrix, False, piece.write_full(out, False))


def edge_inverses(piece, k):
    wave_first = first_waves(piece, k)[0]
    middle = jnp.full((1, 1), piece.length // 2, jnp.int32)
    zero = jnp.zeros((1, 1), jnp.int32)
    return [inverse_denominator(wave_first, signed_waves(p, piece.length)[0]) for p in (zero, middle)]


def next_kernel(length, rows, device_ref, source, state, forcing, in_twiddle, in_matrix, out_twiddle, out_matrix, mirror, out, *scratch):
    device = device_ref[0]
    piece = Pieces(length, rows, *scratch)
    half, step, inner = piece.half, piece.step, piece.inner
    late = device >= (length // rows) // 2
    piece.turn_lines(source)
    piece.incoming(half, -1.0, in_twiddle, in_matrix)

    def body(r0):
        at, also = pl.ds(r0, step), pl.ds(half + r0, step)
        index = row_index(step, 1) + r0
        low_wave = second_wave(piece, device * rows + index)
        high_wave = second_wave(piece, device * rows + half + index)
        moved = jnp.logical_and(row_index(step, inner) + r0 == 0, late)
        weight = weight_of(device, r0, step, inner)
        for k in range(piece.outer):
            wave_first = first_waves(piece, k)[0]
            low = inverse_denominator(wave_first, low_wave)
            high = inverse_denominator(wave_first, high_wave)
            for part in range(2):
                own = state[k, pl.ds(part * half + r0, step), :] + time_step * piece.get(k, at, part)
                own = weight * own
                f_low = time_step * forcing[k, pl.ds(part * rows + r0, step), :]
                f_high = time_step * forcing[k, pl.ds(part * rows + half + r0, step), :]
                piece.put(k, at, part, (f_low + jnp.where(moved, 0.0, own)) * low)
                piece.put(k, also, part, (f_high + jnp.where(moved, own, 0.0)) * high)

    piece.chunks(half, body)

    @pl.when(device == 0)
    def _():
        at = pl.ds(0, 8)
        blocks = []
        for k in range(piece.outer):
            own = tuple(
                state[k, pl.ds(part * half, 8), :] + time_step * piece.get(k, at, part) for part in range(2)
            )
            full = tuple(
                own[part] + time_step * forcing[k, pl.ds(part * rows, 8), :] for part in range(2)
            )
            blocks.append([own, full])
        flipped = piece.mirrored(blocks, mirror)
        rest = pl.ds(0, 16)
        row0 = row_index(16, inner) == 0
        for k in range(piece.outer):
            zero, middle = edge_inverses(piece, k)
            for part in range(2):
                own, full = blocks[k][0][part], blocks[k][1][part]
                own_c, full_c = flipped[k][0][part], flipped[k][1][part]
                value = 0.5 * ((full + full_c) * zero + (own - own_c) * middle)
                replace(piece, k, part, value)

    piece.outgoing(rows, 1.0, out_twiddle, out_matrix, False, piece.write_full(out, False))


def replace(piece, k, part, value):
    lanes = pl.ds(part * piece.inner, piece.inner)
    row0 = row_index(16, piece.inner) == 0
    value = jnp.concatenate([value, value], axis=0)
    for held, new in zip((piece.top, piece.low), halves(value)):
        old = held[k, pl.ds(0, 16), lanes].astype(jnp.float32)
        held[k, pl.ds(0, 16), lanes] = jnp.where(row0, new.astype(jnp.float32), old).astype(jnp.bfloat16)


def misfit_kernel(length, rows, device_ref, source, in_twiddle, in_matrix, out_twiddle, out_matrix, mirror, out, full, coef, total_out, *scratch):
    device = device_ref[0]
    piece = Pieces(length, rows, *scratch)
    half, step, inner = piece.half, piece.step, piece.inner
    late = device >= (length // rows) // 2
    piece.turn_full(source)
    piece.incoming(rows, -1.0, in_twiddle, in_matrix)

    def body(r0):
        at, also = pl.ds(r0, step), pl.ds(half + r0, step)
        index = row_index(step, 1) + r0
        low_wave = second_wave(piece, device * rows + index)
        high_wave = second_wave(piece, device * rows + half + index)
        moved = jnp.logical_and(row_index(step, inner) + r0 == 0, late)
        weight = weight_of(device, r0, step, inner)
        for k in range(piece.outer):
            wave_first = first_waves(piece, k)[0]
            low = time_step * inverse_denominator(wave_first, low_wave)
            high = time_step * inverse_denominator(wave_first, high_wave)
            for part in range(2):
                low_value = piece.get(k, at, part) * low
                high_value = piece.get(k, also, part) * high
                full[k, pl.ds(part * rows + r0, step), :] = low_value
                full[k, pl.ds(part * rows + half + r0, step), :] = high_value
                own = jnp.where(moved, high_value, low_value)
                coef[k, pl.ds(part * half + r0, step), :] = own
                piece.put(k, at, part, weight * own)

    piece.chunks(half, body)

    @pl.when(device == 0)
    def _():
        at = pl.ds(0, 8)
        blocks = [[(piece.get(k, at, 0), piece.get(k, at, 1))] for k in range(piece.outer)]
        flipped = piece.mirrored(blocks, mirror)
        row0 = row_index(8, inner) == 0
        for k in range(piece.outer):
            zero, middle = edge_inverses(piece, k)
            for part in range(2):
                own, own_c = blocks[k][0][part], flipped[k][0][part]
                first = (0.5 * time_step) * (own + own_c) * zero
                value = first + (0.5 * time_step) * (own - own_c) * middle
                at_full, at_coef = pl.ds(part * rows, 8), pl.ds(part * half, 8)
                full[k, at_full, :] = jnp.where(row0, first, full[k, at_full, :])
                coef[k, at_coef, :] = jnp.where(row0, value, coef[k, at_coef, :])
                replace(piece, k, part, value)

    piece.outgoing(half, 1.0, out_twiddle, out_matrix, False, piece.write_full(out, False))
    total_out[...] = jnp.sum(source[:, pl.ds(rows, 8), :], axis=0)


def nonlinear_kernel(length, rows, source, second, twiddle, in_matrix, out_matrix, out, first_out, *scratch):
    piece = Pieces(length, rows, *scratch)
    piece.turn_kept(source)
    piece.unpack_middle()
    piece.incoming(rows, 1.0, twiddle, in_matrix, real_out=True)

    def body(r0):
        at = pl.ds(r0, piece.step)
        for k in range(piece.outer):
            first, other = piece.get(k, at, 0), second[k, at, :]
            first_out[k, at, :] = first
            piece.put(k, at, 0, -0.5 * (first * first + other * other))

    piece.chunks(rows, body)
    piece.outgoing_kept(twiddle, out_matrix, out)


def joint_kernel(length, rows, source, first, second, twiddle, in_matrix, out_matrix, out, second_out, *scratch):
    piece = Pieces(length, rows, *scratch)
    piece.turn_kept(source)
    piece.unpack_middle()
    piece.incoming(rows, 1.0, twiddle, in_matrix, real_out=True)

    def body(r0):
        at = pl.ds(r0, piece.step)
        for k in range(piece.outer):
            value = piece.get(k, at, 0)
            second_out[k, at, :] = value * second[k, at, :]
            piece.put(k, at, 0, value * first[k, at, :])

    piece.chunks(rows, body)
    piece.outgoing_kept(twiddle, out_matrix, out)


def residual_kernel(length, rows, source, both_p, twiddle, in_matrix, out_matrix, out, field_out, *scratch):
    piece = Pieces(length, rows, *scratch[:4])
    strided, total = scratch[4:]
    piece.turn_full(source)
    piece.unpack_middle()
    piece.incoming(rows, 1.0, twiddle, in_matrix, real_out=True)
    piece.collect(lambda k: piece.get(k, pl.ds(0, rows), 0), strided, [field_out])
    total[...] = jnp.zeros_like(total)

    def body(r0):
        at = pl.ds(r0, piece.step)
        for k in range(piece.outer):
            residual = piece.get(k, at, 0) - both_p[k, pl.ds(rows + r0, piece.step), :]
            total[...] += residual * residual
            piece.put(k, at, 0, residual)

    piece.chunks(rows, body)
    piece.outgoing(rows, -1.0, twiddle, out_matrix, True, piece.write_full(out, True))
    value = 0.5 * jnp.sum(total[...])
    out[:, pl.ds(rows, 8), :] = jnp.full((out.shape[0], 8, 2 * rows), value, jnp.float32)


def last_kernel(length, rows, source, second, twiddle, in_matrix, field_out, *scratch):
    piece = Pieces(length, rows, *scratch[:4])
    piece.turn_kept(source)
    piece.unpack_middle()
    piece.incoming(rows, 1.0, twiddle, in_matrix, real_out=True)
    piece.collect(
        lambda k: piece.get(k, pl.ds(0, rows), 0) + second[k], scratch[4], [field_out]
    )


def member_step(device, field, target, forcing_p, devices, rows, length):
    outer, inner = split_length(length)
    half = rows // 2
    float32 = jnp.float32
    shape = lambda *dims: jax.ShapeDtypeStruct(dims, float32)
    kept_blocks = shape(devices, rows * rows // TILE, TILE)
    half_blocks = shape(devices, half, 2 * rows)
    blocks = shape(devices, rows, 2 * rows)
    longer = shape(devices, rows + 8, 2 * rows)
    pair, one = shape(outer, 2 * rows, inner), shape(outer, rows, inner)
    plain = shape(rows, length)
    step = math.gcd(half, 16)
    base = [
        pltpu.VMEM((2 * rows, length), float32),
        pltpu.VMEM((outer, rows, 2 * inner), jnp.bfloat16),
        pltpu.VMEM((outer, rows, 2 * inner), jnp.bfloat16),
        pltpu.VMEM((outer, rows, 2 * inner), float32),
    ]
    strided = pltpu.VMEM((length, TILE), float32)
    total = pltpu.VMEM((step, inner), float32)
    vmem = pl.BlockSpec(memory_space=pltpu.VMEM)
    smem = pl.BlockSpec(memory_space=pltpu.SMEM)

    natural, kept, lines = orders(length, rows)
    tw_natural, tw_kept, tw_lines = [jnp.asarray(twiddle_table(length, o)) for o in (natural, kept, lines)]
    matrix = lambda *args: matrix_table(length, *args)
    forward, backward = matrix(-1.0, natural, natural), matrix(1.0, natural, natural)
    kept_out, kept_in = matrix(-1.0, natural, kept)[:, :inner], matrix(1.0, kept, natural)[:, :, :inner]
    lines_in = matrix(-1.0, lines, natural)
    mirror = jnp.asarray(mirror_table(length))
    kept_lane = jnp.asarray(kept[None, :].astype(np.int32))

    def call(body, outs, scratch, *operands):
        return pl.pallas_call(
            functools.partial(body, length, rows),
            out_shape=outs,
            in_specs=[smem if operand is device else vmem for operand in operands],
            out_specs=jax.tree.map(lambda leaf: vmem, outs),
            scratch_shapes=scratch,
            compiler_params=pltpu.CompilerParams(vmem_limit_bytes=20 * 2**20),
            cost_estimate=pl.CostEstimate(flops=6 * 10**9, bytes_accessed=4 * 2**20, transcendentals=0),
        )(*operands)

    def move(value):
        return lax.all_to_all(value, axes, split_axis=0, concat_axis=0, tiled=True)

    spectral_tables = (tw_lines, lines_in, tw_natural, backward)
    slope_tables = (tw_kept, kept_out, kept_in, kept_lane)
    sent, both_p = call(start_kernel, (kept_blocks, pair), base + [strided], field, target, tw_kept, kept_out)
    second = call(slope_second_kernel, one, base, both_p, *slope_tables)
    sent, state = call(slope_kernel, (half_blocks, one), base, device, move(sent), *spectral_tables)
    sent, first = call(nonlinear_kernel, (kept_blocks, one), base, move(sent), second, tw_kept, kept_in, kept_out)
    sent = call(next_kernel, blocks, base, device, move(sent), state, forcing_p, *spectral_tables, mirror)
    sent, next_field = call(
        residual_kernel, (longer, plain), base + [strided, total],
        move(sent), both_p, tw_natural, backward, forward,
    )
    sent, full, coef, sums = call(
        misfit_kernel, (half_blocks, pair, one, shape(8, 2 * rows)), base,
        device, move(sent), tw_natural, forward, tw_natural, backward, mirror,
    )
    sent, product = call(
        joint_kernel, (kept_blocks, one), base, move(sent), first, second, tw_kept, kept_in, kept_out
    )
    second_part = call(slope_second_kernel, one, base, product, *slope_tables)
    sent = call(total_kernel, half_blocks, base, device, move(sent), coef, *spectral_tables)
    field_grad = call(last_kernel, plain, base + [strided], move(sent), second_part, tw_kept, kept_in)
    return next_field, sums[0, 0], field_grad, full


def per_device(devices, initial_field, target_field, forcing):
    members, rows, length = initial_field.shape
    device = lax.axis_index(axes).astype(jnp.int32).reshape(1)
    outer, inner = split_length(length)
    vmem = pl.BlockSpec(memory_space=pltpu.VMEM)
    strided = pltpu.VMEM((length, TILE), jnp.float32)

    def reorder(body, shape, operand):
        return pl.pallas_call(
            functools.partial(body, length, rows),
            out_shape=jax.ShapeDtypeStruct(shape, jnp.float32),
            in_specs=[vmem],
            out_specs=vmem,
            scratch_shapes=[strided],
        )(operand)

    forcing_p = reorder(spread_kernel, (outer, 2 * rows, inner), forcing)
    results = [
        member_step(device, initial_field[m], target_field[m], forcing_p, devices, rows, length)
        for m in range(members)
    ]
    next_field = jnp.stack([one[0] for one in results])
    objective = sum(one[1] for one in results) / (members * length * length)
    field_grad = jnp.stack([one[2] for one in results])
    forcing_grad = reorder(collect_kernel, (2, rows, length), sum(one[3] for one in results))
    return (next_field, objective, field_grad, forcing_grad)


def solution(mesh):
    devices = mesh.shape["px"] * mesh.shape["py"]
    spec = P(None, axes, None)
    return jax.shard_map(
        functools.partial(per_device, devices),
        mesh=mesh,
        in_specs=(spec, spec, spec),
        out_specs=(spec, P(), spec, spec),
        check_vma=False,
    )
```

profile of v0, /device:TPU:0, one launch (start us, length us, event | category | flops | bytes accessed | tf_op | source)
XLA Modules:
  0.0 220.2 jit_solution(8035481217707644848)
XLA Ops:
  1.7 1.0 copy-done.3
  2.7 1.0 copy-done.8
  4.5 2.9 %shard_map.156 = (f32[32,32,128]{2,1,0:T(8,128)}, f32[8,128,256]{2,1,0:T(8,128)S(1)}) custom-call(f32[64,2048]{1,0:T(8,128)S(1)} %bitcast.6, f32[64,2048]{1,0:T(8,128)S(1)} %bitcast.7, f32[2,8,256]{2,1,0:T(8,128)S(1)} %copy-done.14, bf16[2,256,512]{2,1,0:T(8,128)(2,1)S(1)} %copy-done.8), custom_call_target="tpu_custom_call" | custom-call | flops 6000000000 | bytes 4194304 | tf_op jit(solution)/shard_map/pallas_call | solution.py:641
  8.3 7.3 %all-to-all-start = ((f32[32,32,128]{2,1,0:T(8,128)}), f32[32,32,128]{2,1,0:T(8,128)S(1)}, u32[]{:S(2)}, u32[]{:S(2)}) async-start(f32[32,32,128]{2,1,0:T(8,128)} %get-tuple-element.18), calls=%async_computation | async-start | bytes 1048576 | tf_op jit(solution)/shard_map/all_to_all | solution.py:652
  15.7 15.6 %all-to-all-done.source = f32[32,32,128]{2,1,0:T(8,128)S(1)} async-done(((f32[32,32,128]{2,1,0:T(8,128)}), f32[32,32,128]{2,1,0:T(8,128)S(1)}, u32[]{:S(2)}, u32[]{:S(2)}) %all-to-all-start) | async-done | bytes 524320 | tf_op jit(solution)/shard_map/all_to_all | solution.py:652
  31.3 2.9 %shard_map.157 = (f32[32,32,128]{2,1,0:T(8,128)}, f32[8,64,256]{2,1,0:T(8,128)S(1)}) custom-call(s32[1]{0:T(128)} %bitcast.device_ref, f32[32,32,128]{2,1,0:T(8,128)S(1)} %all-to-all-done.source, f32[2,8,256]{2,1,0:T(8,128)S(1)} %copy-done.17, bf16[2,512,512]{2,1,0:T(8,128)(2,1)S(1)} %copy-done.5, f32[2,8,256]{2,1,0:T(8,128)S(1)} %copy-done.16, ...), custom_call_target="tpu_custom_call" | custom-call | flops 6000000000 | bytes 4194304 | tf_op jit(solution)/shard_map/pallas_call | solution.py:641
  35.0 3.0 %all-to-all-start.1 = ((f32[32,32,128]{2,1,0:T(8,128)}), f32[32,32,128]{2,1,0:T(8,128)S(1)}, u32[]{:S(2)}, u32[]{:S(2)}) async-start(f32[32,32,128]{2,1,0:T(8,128)} %get-tuple-element.19), calls=%async_computation.1 | async-start | bytes 1048576 | tf_op jit(solution)/shard_map/all_to_all | solution.py:652
  39.0 1.2 copy-done.20
  40.3 2.7 %shard_map.158.second = f32[8,64,256]{2,1,0:T(8,128)S(1)} custom-call(f32[8,128,256]{2,1,0:T(8,128)S(1)} %copy-done.20, f32[2,8,256]{2,1,0:T(8,128)S(1)} %copy-done.15, bf16[2,256,512]{2,1,0:T(8,128)(2,1)S(1)} %copy-done.9, bf16[2,512,256]{2,1,0:T(8,128)(2,1)S(1)} %copy-done.7, s32[1,256]{1,0:T(1,128)S(1)} %copy-done.18), custom_call_target="tpu_custom_call" | custom-call | flops 6000000000 | bytes 4194304 | tf_op jit(solution)/shard_map/pallas_call | solution.py:641
  43.8 9.8 %all-to-all-done.1.source = f32[32,32,128]{2,1,0:T(8,128)S(1)} async-done(((f32[32,32,128]{2,1,0:T(8,128)}), f32[32,32,128]{2,1,0:T(8,128)S(1)}, u32[]{:S(2)}, u32[]{:S(2)}) %all-to-all-start.1) | async-done | bytes 524320 | tf_op jit(solution)/shard_map/all_to_all | solution.py:652
  53.6 1.0 copy-done.10
  54.6 1.0 copy-done.25
  55.7 4.2 %shard_map.159 = (f32[32,32,128]{2,1,0:T(8,128)}, f32[8,64,256]{2,1,0:T(8,128)S(1)}) custom-call(f32[32,32,128]{2,1,0:T(8,128)S(1)} %all-to-all-done.1.source, f32[8,64,256]{2,1,0:T(8,128)S(1)} %copy-done.25, f32[2,8,256]{2,1,0:T(8,128)S(1)} %copy-done.15, bf16[2,512,256]{2,1,0:T(8,128)(2,1)S(1)} %copy-done.7, bf16[2,256,512]{2,1,0:T(8,128)(2,1)S(1)} %copy-done.10), custom_call_target="tpu_custom_call" | custom-call | flops 6000000000 | bytes 4194304 | tf_op jit(solution)/shard_map/pallas_call | solution.py:641
  60.7 3.0 %all-to-all-start.2 = ((f32[32,32,128]{2,1,0:T(8,128)}), f32[32,32,128]{2,1,0:T(8,128)S(1)}, u32[]{:S(2)}, u32[]{:S(2)}) async-start(f32[32,32,128]{2,1,0:T(8,128)} %get-tuple-element.21), calls=%async_computation.2 | async-start | bytes 1048576 | tf_op jit(solution)/shard_map/all_to_all | solution.py:652
  63.7 2.9 %shard_map.160.forcing = f32[8,128,256]{2,1,0:T(8,128)} custom-call(f32[2,64,2048]{2,1,0:T(8,128)} %forcing.1), custom_call_target="tpu_custom_call" | custom-call | tf_op jit(solution)/shard_map/pallas_call | solution.py:686
  66.7 12.7 %all-to-all-done.2.source = f32[32,32,128]{2,1,0:T(8,128)S(1)} async-done(((f32[32,32,128]{2,1,0:T(8,128)}), f32[32,32,128]{2,1,0:T(8,128)S(1)}, u32[]{:S(2)}, u32[]{:S(2)}) %all-to-all-start.2) | async-done | bytes 524320 | tf_op jit(solution)/shard_map/all_to_all | solution.py:652
  79.3 1.2 copy-done.1
  80.6 1.0 copy-done.23
  81.6 3.4 %shard_map.161 = f32[32,64,128]{2,1,0:T(8,128)S(1)} custom-call(s32[1]{0:T(128)} %bitcast.device_ref, f32[32,32,128]{2,1,0:T(8,128)S(1)} %all-to-all-done.2.source, f32[8,64,256]{2,1,0:T(8,128)S(1)} %copy-done.23, f32[8,128,256]{2,1,0:T(8,128)S(1)} %copy-done.1, f32[2,8,256]{2,1,0:T(8,128)S(1)} %copy-done.17, bf16[2,512,512]{2,1,0:T(8,128)(2,1)S(1)} %copy-done.5, ...), custom_call_target="tpu_custom_call" | custom-call | flops 6000000000 | bytes 4194304 | tf_op jit(solution)/shard_map/pallas_call | solution.py:641
  85.0 28.7 %all_to_all.40.source = f32[32,64,128]{2,1,0:T(8,128)S(1)} all-to-all(f32[32,64,128]{2,1,0:T(8,128)S(1)} %shard_map.161), channel_id=1, replica_groups=mesh['px'=8,'py'=4] {'px','py'}, dimensions={0} | all-to-all | bytes 2097152 | tf_op jit(solution)/shard_map/all_to_all | solution.py:652
  113.8 4.7 %shard_map.162 = (f32[32,72,128]{2,1,0:T(8,128)S(1)}, f32[64,2048]{1,0:T(8,128)}) custom-call(f32[32,64,128]{2,1,0:T(8,128)S(1)} %all_to_all.40.source, f32[8,128,256]{2,1,0:T(8,128)S(1)} %copy-done.21, f32[2,8,256]{2,1,0:T(8,128)S(1)} %copy-done.16, bf16[2,512,512]{2,1,0:T(8,128)(2,1)S(1)} %copy-done.4, bf16[2,512,512]{2,1,0:T(8,128)(2,1)S(1)} %copy-done.6), custom_call_target="tpu_custom_call" | custom-call | flops 6000000000 | bytes 4194304 | tf_op jit(solution)/shard_map/pallas_call | solution.py:641
  118.5 34.0 %all_to_all.41.source = f32[32,72,128]{2,1,0:T(8,128)S(1)} all-to-all(f32[32,72,128]{2,1,0:T(8,128)S(1)} %get-tuple-element.24), channel_id=1, replica_groups=mesh['px'=8,'py'=4] {'px','py'}, dimensions={0} | all-to-all | bytes 2359296 | tf_op jit(solution)/shard_map/all_to_all | solution.py:652
  152.5 3.5 %shard_map.163 = (f32[32,32,128]{2,1,0:T(8,128)S(1)}, f32[8,128,256]{2,1,0:T(8,128)S(1)}, f32[8,64,256]{2,1,0:T(8,128)S(1)}, f32[8,128]{1,0:T(8,128)S(1)}) custom-call(s32[1]{0:T(128)} %bitcast.device_ref, f32[32,72,128]{2,1,0:T(8,128)S(1)} %all_to_all.41.source, f32[2,8,256]{2,1,0:T(8,128)S(1)} %copy-done.16, bf16[2,512,512]{2,1,0:T(8,128)(2,1)S(1)} %copy-done.6, ...), custom_call_target="tpu_custom_call" | custom-call | flops 6000000000 | bytes 4194304 | tf_op jit(solution)/shard_map/pallas_call | solution.py:641
  156.0 17.3 %all_to_all.42.source = f32[32,32,128]{2,1,0:T(8,128)S(1)} all-to-all(f32[32,32,128]{2,1,0:T(8,128)S(1)} %get-tuple-element.26), channel_id=1, replica_groups=mesh['px'=8,'py'=4] {'px','py'}, dimensions={0} | all-to-all | bytes 1048576 | tf_op jit(solution)/shard_map/all_to_all | solution.py:652
  173.3 3.4 %shard_map.164 = (f32[32,32,128]{2,1,0:T(8,128)S(1)}, f32[8,64,256]{2,1,0:T(8,128)S(1)}) custom-call(f32[32,32,128]{2,1,0:T(8,128)S(1)} %all_to_all.42.source, f32[8,64,256]{2,1,0:T(8,128)S(1)} %copy-done.28, f32[8,64,256]{2,1,0:T(8,128)S(1)} %copy-done.26, f32[2,8,256]{2,1,0:T(8,128)S(1)} %copy-done.15, bf16[2,512,256]{2,1,0:T(8,128)(2,1)S(1)} %copy-done.7, ...), custom_call_target="tpu_custom_call" | custom-call | flops 6000000000 | bytes 4194304 | tf_op jit(solution)/shard_map/pallas_call | solution.py:641
  176.8 18.3 %all_to_all.43.source = f32[32,32,128]{2,1,0:T(8,128)S(1)} all-to-all(f32[32,32,128]{2,1,0:T(8,128)S(1)} %get-tuple-element.28), channel_id=1, replica_groups=mesh['px'=8,'py'=4] {'px','py'}, dimensions={0} | all-to-all | bytes 1048576 | tf_op jit(solution)/shard_map/all_to_all | solution.py:652
  195.1 2.9 %shard_map.165 = f32[32,32,128]{2,1,0:T(8,128)} custom-call(s32[1]{0:T(128)} %bitcast.device_ref, f32[32,32,128]{2,1,0:T(8,128)S(1)} %all_to_all.43.source, f32[8,64,256]{2,1,0:T(8,128)S(1)} %get-tuple-element.29.coef, f32[2,8,256]{2,1,0:T(8,128)S(1)} %copy-done.17, bf16[2,512,512]{2,1,0:T(8,128)(2,1)S(1)} %copy-done.5, f32[2,8,256]{2,1,0:T(8,128)S(1)} %copy-done.16, ...), custom_call_target="tpu_custom_call" | custom-call | flops 6000000000 | bytes 4194304 | tf_op jit(solution)/shard_map/pallas_call | solution.py:641
  198.0 3.0 %all-to-all-start.7 = ((f32[32,32,128]{2,1,0:T(8,128)}), f32[32,32,128]{2,1,0:T(8,128)S(1)}, u32[]{:S(2)}, u32[]{:S(2)}) async-start(f32[32,32,128]{2,1,0:T(8,128)} %shard_map.165), calls=%async_computation.7 | async-start | bytes 1048576 | tf_op jit(solution)/shard_map/all_to_all | solution.py:652
  201.5 2.9 %shard_map.168 = f32[2,64,2048]{2,1,0:T(8,128)} custom-call(f32[8,128,256]{2,1,0:T(8,128)} %copy-done), custom_call_target="tpu_custom_call" | custom-call | tf_op jit(solution)/shard_map/pallas_call | solution.py:686
  205.0 2.8 %shard_map.166.second = f32[8,64,256]{2,1,0:T(8,128)S(1)} custom-call(f32[8,64,256]{2,1,0:T(8,128)S(1)} %copy-done.30, f32[2,8,256]{2,1,0:T(8,128)S(1)} %copy-done.15, bf16[2,256,512]{2,1,0:T(8,128)(2,1)S(1)} %copy-done.12, bf16[2,512,256]{2,1,0:T(8,128)(2,1)S(1)} %copy-done.7, s32[1,256]{1,0:T(1,128)S(1)} %copy-done.18), custom_call_target="tpu_custom_call" | custom-call | flops 6000000000 | bytes 4194304 | tf_op jit(solution)/shard_map/pallas_call | solution.py:641
  207.8 8.8 %all-to-all-done.7.source = f32[32,32,128]{2,1,0:T(8,128)S(1)} async-done(((f32[32,32,128]{2,1,0:T(8,128)}), f32[32,32,128]{2,1,0:T(8,128)S(1)}, u32[]{:S(2)}, u32[]{:S(2)}) %all-to-all-start.7) | async-done | bytes 524320 | tf_op jit(solution)/shard_map/all_to_all | solution.py:652
  216.6 2.5 %shard_map.167 = f32[64,2048]{1,0:T(8,128)} custom-call(f32[32,32,128]{2,1,0:T(8,128)S(1)} %all-to-all-done.7.source, f32[8,64,256]{2,1,0:T(8,128)S(1)} %shard_map.166.second, f32[2,8,256]{2,1,0:T(8,128)S(1)} %copy-done.15, bf16[2,512,256]{2,1,0:T(8,128)(2,1)S(1)} %copy-done.7), custom_call_target="tpu_custom_call" | custom-call | flops 6000000000 | bytes 4194304 | tf_op jit(solution)/shard_map/pallas_call | solution.py:641
  (56 shorter events, 6.8 us)
Async XLA Ops:
  0.6 1.0 copy-start.2
  1.7 1.0 copy-start.3
  2.7 1.0 copy-start.8
  4.5 26.8 %copy-start.4 = (bf16[2,512,512]{2,1,0:T(8,128)(2,1)S(1)}, bf16[2,512,512]{2,1,0:T(8,128)(2,1)}, u32[]{:S(2)}) copy-start(bf16[2,512,512]{2,1,0:T(8,128)(2,1)} %constant.43.clone.out_matrix.in_matrix) | copy-start | bytes 3145732
  4.5 26.8 %copy-start.5 = (bf16[2,512,512]{2,1,0:T(8,128)(2,1)S(1)}, bf16[2,512,512]{2,1,0:T(8,128)(2,1)}, u32[]{:S(2)}) copy-start(bf16[2,512,512]{2,1,0:T(8,128)(2,1)} %constant.42.clone.in_matrix) | copy-start | bytes 3145732
  4.5 26.8 %copy-start.16 = (f32[2,8,256]{2,1,0:T(8,128)S(1)}, f32[2,8,256]{2,1,0:T(8,128)}, u32[]{:S(2)}) copy-start(f32[2,8,256]{2,1,0:T(8,128)} %constant.35.clone.out_twiddle.twiddle.in_twiddle) | copy-start | bytes 49156
  4.5 26.8 %copy-start.17 = (f32[2,8,256]{2,1,0:T(8,128)S(1)}, f32[2,8,256]{2,1,0:T(8,128)}, u32[]{:S(2)}) copy-start(f32[2,8,256]{2,1,0:T(8,128)} %constant.37.clone.in_twiddle) | copy-start | bytes 49156
  7.4 1.0 copy-start.19
  8.3 22.9 %all-to-all-start = ((f32[32,32,128]{2,1,0:T(8,128)}), f32[32,32,128]{2,1,0:T(8,128)S(1)}, u32[]{:S(2)}, u32[]{:S(2)}) async-start(f32[32,32,128]{2,1,0:T(8,128)} %get-tuple-element.18), calls=%async_computation | async-start | bytes 1048576 | tf_op jit(solution)/shard_map/all_to_all | solution.py:652
  31.3 6.7 %copy-start.7 = (bf16[2,512,256]{2,1,0:T(8,128)(2,1)S(1)}, bf16[2,512,256]{2,1,0:T(8,128)(2,1)}, u32[]{:S(2)}) copy-start(bf16[2,512,256]{2,1,0:T(8,128)(2,1)} %constant.41.clone.in_matrix) | copy-start | bytes 1572868
  31.3 6.7 %copy-start.15 = (f32[2,8,256]{2,1,0:T(8,128)S(1)}, f32[2,8,256]{2,1,0:T(8,128)}, u32[]{:S(2)}) copy-start(f32[2,8,256]{2,1,0:T(8,128)} %constant.36.clone.twiddle) | copy-start | bytes 49156
  31.3 6.7 %copy-start.18 = (s32[1,256]{1,0:T(1,128)S(1)}, s32[1,256]{1,0:T(1,128)}, u32[]{:S(2)}) copy-start(s32[1,256]{1,0:T(1,128)} %constant.39.clone.kept) | copy-start | bytes 3076
  35.0 18.6 %all-to-all-start.1 = ((f32[32,32,128]{2,1,0:T(8,128)}), f32[32,32,128]{2,1,0:T(8,128)S(1)}, u32[]{:S(2)}, u32[]{:S(2)}) async-start(f32[32,32,128]{2,1,0:T(8,128)} %get-tuple-element.19), calls=%async_computation.1 | async-start | bytes 1048576 | tf_op jit(solution)/shard_map/all_to_all | solution.py:652
  38.0 1.0 copy-start.9
  39.0 1.2 copy-start.20
  43.0 0.8 copy-start.24
  53.6 1.0 copy-start.10
  54.6 1.0 copy-start.25
  60.7 18.6 %all-to-all-start.2 = ((f32[32,32,128]{2,1,0:T(8,128)}), f32[32,32,128]{2,1,0:T(8,128)S(1)}, u32[]{:S(2)}, u32[]{:S(2)}) async-start(f32[32,32,128]{2,1,0:T(8,128)} %get-tuple-element.21), calls=%async_computation.2 | async-start | bytes 1048576 | tf_op jit(solution)/shard_map/all_to_all | solution.py:652
  63.7 15.6 %copy-start.13 = (bf16[2,256,256]{2,1,0:T(8,128)(2,1)S(1)}, bf16[2,256,256]{2,1,0:T(8,128)(2,1)}, u32[]{:S(2)}) copy-start(bf16[2,256,256]{2,1,0:T(8,128)(2,1)} %constant.38.clone.mirror) | copy-start | bytes 786436
  79.3 1.2 copy-start.1
  80.6 1.0 copy-start.23
  85.0 28.7 %copy-start.6 = (bf16[2,512,512]{2,1,0:T(8,128)(2,1)S(1)}, bf16[2,512,512]{2,1,0:T(8,128)(2,1)}, u32[]{:S(2)}) copy-start(bf16[2,512,512]{2,1,0:T(8,128)(2,1)} %constant.44.clone.out_matrix.in_matrix) | copy-start | bytes 3145732
  85.0 28.7 %copy-start.21 = (f32[8,128,256]{2,1,0:T(8,128)S(1)}, f32[8,128,256]{2,1,0:T(8,128)}, u32[]{:S(2)}) copy-start(f32[8,128,256]{2,1,0:T(8,128)} %copy-done.19) | copy-start | bytes 3145732
  152.5 20.8 %copy-start.11 = (bf16[2,256,512]{2,1,0:T(8,128)(2,1)S(1)}, bf16[2,256,512]{2,1,0:T(8,128)(2,1)}, u32[]{:S(2)}) copy-start(bf16[2,256,512]{2,1,0:T(8,128)(2,1)} %constant.40.clone.matrix.out_matrix) | copy-start | bytes 1572868
  152.5 20.8 %copy-start.26 = (f32[8,64,256]{2,1,0:T(8,128)S(1)}, f32[8,64,256]{2,1,0:T(8,128)}, u32[]{:S(2)}) copy-start(f32[8,64,256]{2,1,0:T(8,128)} %copy-done.24) | copy-start | bytes 1572868
  152.5 20.8 %copy-start.28 = (f32[8,64,256]{2,1,0:T(8,128)S(1)}, f32[8,64,256]{2,1,0:T(8,128)}, u32[]{:S(2)}) copy-start(f32[8,64,256]{2,1,0:T(8,128)} %copy-done.27) | copy-start | bytes 1572868
  156.0 20.8 %copy-start = (f32[8,128,256]{2,1,0:T(8,128)}, f32[8,128,256]{2,1,0:T(8,128)S(1)}, u32[]{:S(2)}) copy-start(f32[8,128,256]{2,1,0:T(8,128)S(1)} %get-tuple-element.31.slabs) | copy-start | bytes 3145732
  176.8 18.3 %copy-start.29 = (f32[8,64,256]{2,1,0:T(8,128)}, f32[8,64,256]{2,1,0:T(8,128)S(1)}, u32[]{:S(2)}) copy-start(f32[8,64,256]{2,1,0:T(8,128)S(1)} %get-tuple-element.30.field_p) | copy-start | bytes 1572868
  198.0 18.6 %all-to-all-start.7 = ((f32[32,32,128]{2,1,0:T(8,128)}), f32[32,32,128]{2,1,0:T(8,128)S(1)}, u32[]{:S(2)}, u32[]{:S(2)}) async-start(f32[32,32,128]{2,1,0:T(8,128)} %shard_map.165), calls=%async_computation.7 | async-start | bytes 1048576 | tf_op jit(solution)/shard_map/all_to_all | solution.py:652
  201.0 4.0 %copy-start.12 = (bf16[2,256,512]{2,1,0:T(8,128)(2,1)S(1)}, bf16[2,256,512]{2,1,0:T(8,128)(2,1)}, u32[]{:S(2)}) copy-start(bf16[2,256,512]{2,1,0:T(8,128)(2,1)} %constant.40.clone.matrix.out_matrix) | copy-start | bytes 1572868
  201.0 4.0 %copy-start.30 = (f32[8,64,256]{2,1,0:T(8,128)S(1)}, f32[8,64,256]{2,1,0:T(8,128)}, u32[]{:S(2)}) copy-start(f32[8,64,256]{2,1,0:T(8,128)} %copy-done.29) | copy-start | bytes 1572868
  (3 other events, 2.3 us)
where the time goes:
time: 221 us; the launch traced here: 220 us
  blocking collectives  98.4 us (45%)
  waiting for transfers between devices  46.8 us (21%)
  Pallas kernels  41.7 us (19%)
  starting transfers between devices  16.2 us (7%)
  local copies, waits for them, and re-layouts  14.4 us (7%)
  between operations  2.67 us (1%)
    all_to_all x4, blocking collectives, move(): return lax.all_to_all(value, axes, split_axis=0, concat_axis=0, tiled=True)  98.4 us
    all_to_all x4, waiting for transfers between devices, move(): return lax.all_to_all(value, axes, split_axis=0, concat_axis=0, tiled=True)  46.8 us
    pallas_call x11, Pallas kernels, call(): pl.pallas_call(functools.partial(body, length, rows), out_shape=outs, in_...  35.9 us
    all_to_all x4, starting transfers between devices, move(): return lax.all_to_all(value, axes, split_axis=0, concat_axis=0, tiled=True)  16.2 us
    unnamed x62, local copies, waits for them, and re-layouts  13.9 us
    pallas_call x2, Pallas kernels, reorder(): pl.pallas_call(functools.partial(body, length, rows), out_shape=jax.Shape...  5.79 us
  transfers between devices with their start and end apart: 4, of which 4 were waited for; matrix products, arithmetic and copies ran while one was open for 0% of the time, Pallas kernels for 5%

commit v1 on v0

--- a/solution.py
+++ b/solution.py
@@ -271,6 +271,27 @@
             out.append([(take(2 * i), -take(2 * i + 1)) for i in range(per // 2)])
         return out
 
+    def pack_columns(self, slabs, result):
+        rows, half, wide = self.rows, self.half, self.inner // 2
+        blocks, groups = self.inner // rows, TILE // rows
+        tall = rows // groups
+        for k in range(self.outer):
+            slab = slabs(k)
+            for s in range(blocks):
+                parts = []
+                for group in range(groups):
+                    for part in range(2):
+                        at = part * wide + s * half
+                        parts.append(slab[group * tall : (group + 1) * tall, at : at + half])
+                result[k * blocks + s] = jnp.concatenate(parts, axis=1)
+
+    def turn_columns(self, source, result):
+        rows, wide, blocks = self.rows, self.inner // 2, self.inner // self.rows
+        for j in range(self.outer):
+            tile = source[pl.ds(j * blocks, blocks), :, :].reshape(wide, 2 * rows).T
+            result[j, :, pl.ds(0, wide)] = tile[:rows]
+            result[j, :, pl.ds(wide, wide)] = tile[rows:]
+
     def spread(self, first, second, strided, result):
         rows, fill = self.rows, TILE - 2 * self.rows
         for t in range(self.length // TILE):
@@ -322,17 +343,10 @@
     return lax.broadcasted_iota(jnp.int32, (count, width), 0)
 
 
-def start_kernel(length, rows, field, target, twiddle, matrix, out, both_p, *scratch):
-    piece = Pieces(length, rows, *scratch[:4])
-    piece.spread(field, target, scratch[4], both_p)
-
-    def body(r0):
-        at = pl.ds(r0, piece.step)
-        for k in range(piece.outer):
-            piece.put(k, at, 0, both_p[k, at, :])
-
-    piece.chunks(rows, body)
-    piece.outgoing_kept(twiddle, matrix, out)
+def start_kernel(length, rows, field, target, out, both_p, *scratch):
+    piece = Pieces(length, rows)
+    piece.spread(field, target, scratch[0], both_p)
+    piece.pack_columns(lambda k: both_p[k, pl.ds(0, rows), :], out)
 
 
 def slope_second_kernel(length, rows, field_p, twiddle, out_matrix, in_matrix, kept, result, *scratch):
@@ -375,43 +389,19 @@
     return jnp.where(alone, jnp.float32(1.0), jnp.float32(2.0))
 
 
-def slope_kernel(length, rows, device_ref, source, in_twiddle, in_matrix, out_twiddle, out_matrix, out, state, *scratch):
-    device = device_ref[0]
+def slope_first_kernel(length, rows, source, in_twiddle, in_matrix, out_twiddle, out_matrix, out, *scratch):
     piece = Pieces(length, rows, *scratch)
     half = piece.half
     piece.turn_lines(source)
     piece.incoming(half, -1.0, in_twiddle, in_matrix)
 
     def body(r0):
-        at, also = pl.ds(r0, piece.step), pl.ds(half + r0, piece.step)
-        weight = weight_of(device, r0, piece.step, piece.inner)
+        at = pl.ds(r0, piece.step)
         for k in range(piece.outer):
             re, im = piece.get(k, at, 0), piece.get(k, at, 1)
-            state[k, at, :], state[k, also, :] = re, im
-            scale = first_waves(piece, k)[1] * weight
+            scale = first_waves(piece, k)[1]
             piece.put(k, at, 0, -scale * im)
             piece.put(k, at, 1, scale * re)
-
-    piece.chunks(half, body)
-    piece.outgoing(half, 1.0, out_twiddle, out_matrix, False, piece.write_full(out, False))
-
-
-def total_kernel(length, rows, device_ref, source, coef, in_twiddle, in_matrix, out_twiddle, out_matrix, out, *scratch):
-    device = device_ref[0]
-    piece = Pieces(length, rows, *scratch)
-    half = piece.half
-    piece.turn_lines(source)
-    piece.incoming(half, -1.0, in_twiddle, in_matrix)
-
-    def body(r0):
-        at, also = pl.ds(r0, piece.step), pl.ds(half + r0, piece.step)
-        weight = weight_of(device, r0, piece.step, piece.inner)
-        for k in range(piece.outer):
-            re, im = piece.get(k, at, 0), piece.get(k, at, 1)
-            deriv = first_waves(piece, k)[1]
-            scale = 1.0 / time_step
-            piece.put(k, at, 0, weight * (scale * coef[k, at, :] - deriv * im))
-            piece.put(k, at, 1, weight * (scale * coef[k, also, :] + deriv * re))
 
     piece.chunks(half, body)
     piece.outgoing(half, 1.0, out_twiddle, out_matrix, False, piece.write_full(out, False))
@@ -424,7 +414,7 @@
     return [inverse_denominator(wave_first, signed_waves(p, piece.length)[0]) for p in (zero, middle)]
 
 
-def next_kernel(length, rows, device_ref, source, state, forcing, in_twiddle, in_matrix, out_twiddle, out_matrix, mirror, out, *scratch):
+def next_kernel(length, rows, device_ref, source, forcing, in_twiddle, in_matrix, out_twiddle, out_matrix, mirror, out, *scratch):
     device = device_ref[0]
     piece = Pieces(length, rows, *scratch)
     half, step, inner = piece.half, piece.step, piece.inner
@@ -444,8 +434,7 @@
             low = inverse_denominator(wave_first, low_wave)
             high = inverse_denominator(wave_first, high_wave)
             for part in range(2):
-                own = state[k, pl.ds(part * half + r0, step), :] + time_step * piece.get(k, at, part)
-                own = weight * own
+                own = weight * piece.get(k, at, part)
                 f_low = time_step * forcing[k, pl.ds(part * rows + r0, step), :]
                 f_high = time_step * forcing[k, pl.ds(part * rows + half + r0, step), :]
                 piece.put(k, at, part, (f_low + jnp.where(moved, 0.0, own)) * low)
@@ -458,9 +447,7 @@
         at = pl.ds(0, 8)
         blocks = []
         for k in range(piece.outer):
-            own = tuple(
-                state[k, pl.ds(part * half, 8), :] + time_step * piece.get(k, at, part) for part in range(2)
-            )
+            own = tuple(piece.get(k, at, part) for part in range(2))
             full = tuple(
                 own[part] + time_step * forcing[k, pl.ds(part * rows, 8), :] for part in range(2)
             )
@@ -488,7 +475,7 @@
         held[k, pl.ds(0, 16), lanes] = jnp.where(row0, new.astype(jnp.float32), old).astype(jnp.bfloat16)
 
 
-def misfit_kernel(length, rows, device_ref, source, in_twiddle, in_matrix, out_twiddle, out_matrix, mirror, out, full, coef, total_out, *scratch):
+def misfit_kernel(length, rows, device_ref, source, in_twiddle, in_matrix, out_twiddle, out_matrix, mirror, out, full, total_out, *scratch):
     device = device_ref[0]
     piece = Pieces(length, rows, *scratch)
     half, step, inner = piece.half, piece.step, piece.inner
@@ -513,7 +500,6 @@
                 full[k, pl.ds(part * rows + r0, step), :] = low_value
                 full[k, pl.ds(part * rows + half + r0, step), :] = high_value
                 own = jnp.where(moved, high_value, low_value)
-                coef[k, pl.ds(part * half + r0, step), :] = own
                 piece.put(k, at, part, weight * own)
 
     piece.chunks(half, body)
@@ -530,47 +516,45 @@
                 own, own_c = blocks[k][0][part], flipped[k][0][part]
                 first = (0.5 * time_step) * (own + own_c) * zero
                 value = first + (0.5 * time_step) * (own - own_c) * middle
-                at_full, at_coef = pl.ds(part * rows, 8), pl.ds(part * half, 8)
+                at_full = pl.ds(part * rows, 8)
                 full[k, at_full, :] = jnp.where(row0, first, full[k, at_full, :])
-                coef[k, at_coef, :] = jnp.where(row0, value, coef[k, at_coef, :])
                 replace(piece, k, part, value)
 
     piece.outgoing(half, 1.0, out_twiddle, out_matrix, False, piece.write_full(out, False))
     total_out[...] = jnp.sum(source[:, pl.ds(rows, 8), :], axis=0)
 
 
-def nonlinear_kernel(length, rows, source, second, twiddle, in_matrix, out_matrix, out, first_out, *scratch):
+def nonlinear_kernel(length, rows, source, both_p, second, twiddle, out_matrix, out, first, *scratch):
+    piece = Pieces(length, rows, *scratch)
+    piece.turn_columns(source, first)
+
+    def body(r0):
+        at = pl.ds(r0, piece.step)
+        for k in range(piece.outer):
+            one, other = first[k, at, :], second[k, at, :]
+            piece.put(k, at, 0, both_p[k, at, :] - (0.5 * time_step) * (one * one + other * other))
+
+    piece.chunks(rows, body)
+    piece.outgoing_kept(twiddle, out_matrix, out)
+
+
+def joint_kernel(length, rows, source, first, second, twiddle, in_matrix, out, value_out, second_out, *scratch):
     piece = Pieces(length, rows, *scratch)
     piece.turn_kept(source)
     piece.unpack_middle()
     piece.incoming(rows, 1.0, twiddle, in_matrix, real_out=True)
+    lanes = pl.ds(0, piece.inner)
 
     def body(r0):
         at = pl.ds(r0, piece.step)
         for k in range(piece.outer):
-            first, other = piece.get(k, at, 0), second[k, at, :]
-            first_out[k, at, :] = first
-            piece.put(k, at, 0, -0.5 * (first * first + other * other))
+            value = piece.get(k, at, 0)
+            value_out[k, at, :] = (1.0 / time_step) * value
+            second_out[k, at, :] = value * second[k, at, :]
+            piece.z[k, at, lanes] = value * first[k, at, :]
 
     piece.chunks(rows, body)
-    piece.outgoing_kept(twiddle, out_matrix, out)
-
-
-def joint_kernel(length, rows, source, first, second, twiddle, in_matrix, out_matrix, out, second_out, *scratch):
-    piece = Pieces(length, rows, *scratch)
-    piece.turn_kept(source)
-    piece.unpack_middle()
-    piece.incoming(rows, 1.0, twiddle, in_matrix, real_out=True)
-
-    def body(r0):
-        at = pl.ds(r0, piece.step)
-        for k in range(piece.outer):
-            value = piece.get(k, at, 0)
-            second_out[k, at, :] = value * second[k, at, :]
-            piece.put(k, at, 0, value * first[k, at, :])
-
-    piece.chunks(rows, body)
-    piece.outgoing_kept(twiddle, out_matrix, out)
+    piece.pack_columns(lambda k: piece.z[k, pl.ds(0, rows), lanes], out)
 
 
 def residual_kernel(length, rows, source, both_p, twiddle, in_matrix, out_matrix, out, field_out, *scratch):
@@ -595,14 +579,10 @@
     out[:, pl.ds(rows, 8), :] = jnp.full((out.shape[0], 8, 2 * rows), value, jnp.float32)
 
 
-def last_kernel(length, rows, source, second, twiddle, in_matrix, field_out, *scratch):
-    piece = Pieces(length, rows, *scratch[:4])
-    piece.turn_kept(source)
-    piece.unpack_middle()
-    piece.incoming(rows, 1.0, twiddle, in_matrix, real_out=True)
-    piece.collect(
-        lambda k: piece.get(k, pl.ds(0, rows), 0) + second[k], scratch[4], [field_out]
-    )
+def last_kernel(length, rows, source, value, second, field_out, strided, first):
+    piece = Pieces(length, rows)
+    piece.turn_columns(source, first)
+    piece.collect(lambda k: first[k] + value[k] + second[k], strided, [field_out])
 
 
 def member_step(device, field, target, forcing_p, devices, rows, length):
@@ -653,25 +633,27 @@
 
     spectral_tables = (tw_lines, lines_in, tw_natural, backward)
     slope_tables = (tw_kept, kept_out, kept_in, kept_lane)
-    sent, both_p = call(start_kernel, (kept_blocks, pair), base + [strided], field, target, tw_kept, kept_out)
+    sent, both_p = call(start_kernel, (kept_blocks, pair), [strided], field, target)
     second = call(slope_second_kernel, one, base, both_p, *slope_tables)
-    sent, state = call(slope_kernel, (half_blocks, one), base, device, move(sent), *spectral_tables)
-    sent, first = call(nonlinear_kernel, (kept_blocks, one), base, move(sent), second, tw_kept, kept_in, kept_out)
-    sent = call(next_kernel, blocks, base, device, move(sent), state, forcing_p, *spectral_tables, mirror)
+    sent = call(slope_first_kernel, half_blocks, base, move(sent), *spectral_tables)
+    sent, first = call(nonlinear_kernel, (kept_blocks, one), base, move(sent), both_p, second, tw_kept, kept_out)
+    sent = call(next_kernel, blocks, base, device, move(sent), forcing_p, *spectral_tables, mirror)
     sent, next_field = call(
         residual_kernel, (longer, plain), base + [strided, total],
         move(sent), both_p, tw_natural, backward, forward,
     )
-    sent, full, coef, sums = call(
-        misfit_kernel, (half_blocks, pair, one, shape(8, 2 * rows)), base,
+    sent, full, sums = call(
+        misfit_kernel, (half_blocks, pair, shape(8, 2 * rows)), base,
         device, move(sent), tw_natural, forward, tw_natural, backward, mirror,
     )
-    sent, product = call(
-        joint_kernel, (kept_blocks, one), base, move(sent), first, second, tw_kept, kept_in, kept_out
+    sent, value, product = call(
+        joint_kernel, (kept_blocks, one, one), base, move(sent), first, second, tw_kept, kept_in
     )
     second_part = call(slope_second_kernel, one, base, product, *slope_tables)
-    sent = call(total_kernel, half_blocks, base, device, move(sent), coef, *spectral_tables)
-    field_grad = call(last_kernel, plain, base + [strided], move(sent), second_part, tw_kept, kept_in)
+    sent = call(slope_first_kernel, half_blocks, base, move(sent), *spectral_tables)
+    field_grad = call(
+        last_kernel, plain, [strided, pltpu.VMEM((outer, rows, inner), float32)], move(sent), value, second_part
+    )
     return next_field, sums[0, 0], field_grad, full
 
 

time: 221 us -> 212 us (0.959)
  blocking collectives: 98.4 us -> 121 us
  waiting for transfers between devices: 46.8 us -> 31.2 us
  starting transfers between devices: 16.2 us -> 8.92 us
  Pallas kernels: 41.7 us -> 35.2 us
  local copies, waits for them, and re-layouts: 14.4 us -> 11.9 us
    all_to_all x4 -> x5, blocking collectives: 98.4 us -> 121 us  [move(): return lax.all_to_all(value, axes, split_axis=0, concat_axis=0, tiled=True)]
    all_to_all x4 -> x3, waiting for transfers between devices: 46.8 us -> 31.2 us  [move(): return lax.all_to_all(value, axes, split_axis=0, concat_axis=0, tiled=True)]
    all_to_all x4 -> x3, starting transfers between devices: 16.2 us -> 8.92 us  [move(): return lax.all_to_all(value, axes, split_axis=0, concat_axis=0, tiled=True)]
    pallas_call x11, Pallas kernels: 35.9 us -> 29.4 us  [call(): pl.pallas_call(functools.partial(body, length, rows), out_shape=outs, in_...]
    unnamed x62 -> x58, local copies, waits for them, and re-layouts: 13.9 us -> 11.3 us
  transfers between devices with their start and end apart: 4 -> 3, of which waited for: 4 -> 3; matrix products, arithmetic and copies ran while one was open for 0% -> 0% of each run, Pallas kernels for 5% -> 5%
where the time goes in v1:
time: 212 us; the launch traced here: 211 us
  blocking collectives  121 us (57%)
  Pallas kernels  35.2 us (17%)
  waiting for transfers between devices  31.2 us (15%)
  local copies, waits for them, and re-layouts  11.9 us (6%)
  starting transfers between devices  8.92 us (4%)
  between operations  2.69 us (1%)
    all_to_all x5, blocking collectives, move(): return lax.all_to_all(value, axes, split_axis=0, concat_axis=0, tiled=True)  121 us
    all_to_all x3, waiting for transfers between devices, move(): return lax.all_to_all(value, axes, split_axis=0, concat_axis=0, tiled=True)  31.2 us
    pallas_call x11, Pallas kernels, call(): pl.pallas_call(functools.partial(body, length, rows), out_shape=outs, in_...  29.4 us
    unnamed x58, local copies, waits for them, and re-layouts  11.3 us
    all_to_all x3, starting transfers between devices, move(): return lax.all_to_all(value, axes, split_axis=0, concat_axis=0, tiled=True)  8.92 us
    pallas_call x2, Pallas kernels, reorder(): pl.pallas_call(functools.partial(body, length, rows), out_shape=jax.Shape...  5.78 us
  transfers between devices with their start and end apart: 3, of which 3 were waited for; matrix products, arithmetic and copies ran while one was open for 0% of the time, Pallas kernels for 5%

profile of v1, /device:TPU:0, one launch (start us, length us, event | category | flops | bytes accessed | tf_op | source)
XLA Modules:
  0.0 211.0 jit_solution(14794956071252501975)
XLA Ops:
  0.6 1.0 copy-done.2
  1.7 1.0 copy-done.3
  2.7 1.1 shard_map.156
  3.8 22.7 %all_to_all.40.source = f32[32,32,128]{2,1,0:T(8,128)S(1)} all-to-all(f32[32,32,128]{2,1,0:T(8,128)S(1)} %get-tuple-element.16), channel_id=1, replica_groups=mesh['px'=8,'py'=4] {'px','py'}, dimensions={0} | all-to-all | bytes 1048576 | tf_op jit(solution)/shard_map/all_to_all | solution.py:632
  26.7 2.8 %shard_map.157 = f32[32,32,128]{2,1,0:T(8,128)} custom-call(f32[32,32,128]{2,1,0:T(8,128)S(1)} %all_to_all.40.source, f32[2,8,256]{2,1,0:T(8,128)S(1)} %copy-done.14, bf16[2,512,512]{2,1,0:T(8,128)(2,1)S(1)} %copy-done.5, f32[2,8,256]{2,1,0:T(8,128)S(1)} %copy-done.13, bf16[2,512,512]{2,1,0:T(8,128)(2,1)S(1)} %copy-done.4), custom_call_target="tpu_custom_call" | custom-call | flops 6000000000 | bytes 4194304 | tf_op jit(solution)/shard_map/pallas_call | solution.py:621
  29.5 3.0 %all-to-all-start.1 = ((f32[32,32,128]{2,1,0:T(8,128)}), f32[32,32,128]{2,1,0:T(8,128)S(1)}, u32[]{:S(2)}, u32[]{:S(2)}) async-start(f32[32,32,128]{2,1,0:T(8,128)} %shard_map.157), calls=%async_computation.1 | async-start | bytes 1048576 | tf_op jit(solution)/shard_map/all_to_all | solution.py:632
  32.5 1.0 copy-done.8
  33.5 1.2 copy-done.17
  34.8 2.7 %shard_map.158.second = f32[8,64,256]{2,1,0:T(8,128)S(1)} custom-call(f32[8,128,256]{2,1,0:T(8,128)S(1)} %copy-done.17, f32[2,8,256]{2,1,0:T(8,128)S(1)} %copy-done.12, bf16[2,256,512]{2,1,0:T(8,128)(2,1)S(1)} %copy-done.8, bf16[2,512,256]{2,1,0:T(8,128)(2,1)S(1)} %copy-done.7, s32[1,256]{1,0:T(1,128)S(1)} %copy-done.15), custom_call_target="tpu_custom_call" | custom-call | flops 6000000000 | bytes 4194304 | tf_op jit(solution)/shard_map/pallas_call | solution.py:621
  38.3 9.8 %all-to-all-done.1.source = f32[32,32,128]{2,1,0:T(8,128)S(1)} async-done(((f32[32,32,128]{2,1,0:T(8,128)}), f32[32,32,128]{2,1,0:T(8,128)S(1)}, u32[]{:S(2)}, u32[]{:S(2)}) %all-to-all-start.1) | async-done | bytes 524320 | tf_op jit(solution)/shard_map/all_to_all | solution.py:632
  48.1 1.0 copy-done.9
  49.1 1.2 copy-done.18
  50.3 1.0 copy-done.21
  51.4 2.5 %shard_map.159 = (f32[32,32,128]{2,1,0:T(8,128)}, f32[8,64,256]{2,1,0:T(8,128)S(1)}) custom-call(f32[32,32,128]{2,1,0:T(8,128)S(1)} %all-to-all-done.1.source, f32[8,128,256]{2,1,0:T(8,128)S(1)} %copy-done.18, f32[8,64,256]{2,1,0:T(8,128)S(1)} %copy-done.21, f32[2,8,256]{2,1,0:T(8,128)S(1)} %copy-done.12, bf16[2,256,512]{2,1,0:T(8,128)(2,1)S(1)} %copy-done.9), custom_call_target="tpu_custom_call" | custom-call | flops 6000000000 | bytes 4194304 | tf_op jit(solution)/shard_map/pallas_call | solution.py:621
  54.7 3.0 %all-to-all-start.2 = ((f32[32,32,128]{2,1,0:T(8,128)}), f32[32,32,128]{2,1,0:T(8,128)S(1)}, u32[]{:S(2)}, u32[]{:S(2)}) async-start(f32[32,32,128]{2,1,0:T(8,128)} %get-tuple-element.18), calls=%async_computation.2 | async-start | bytes 1048576 | tf_op jit(solution)/shard_map/all_to_all | solution.py:632
  57.7 2.9 %shard_map.160.forcing = f32[8,128,256]{2,1,0:T(8,128)} custom-call(f32[2,64,2048]{2,1,0:T(8,128)} %forcing.1), custom_call_target="tpu_custom_call" | custom-call | tf_op jit(solution)/shard_map/pallas_call | solution.py:668
  60.6 12.7 %all-to-all-done.2.source = f32[32,32,128]{2,1,0:T(8,128)S(1)} async-done(((f32[32,32,128]{2,1,0:T(8,128)}), f32[32,32,128]{2,1,0:T(8,128)S(1)}, u32[]{:S(2)}, u32[]{:S(2)}) %all-to-all-start.2) | async-done | bytes 524320 | tf_op jit(solution)/shard_map/all_to_all | solution.py:632
  73.3 1.2 copy-done.1
  74.5 3.4 %shard_map.161 = f32[32,64,128]{2,1,0:T(8,128)S(1)} custom-call(s32[1]{0:T(128)} %bitcast.device_ref, f32[32,32,128]{2,1,0:T(8,128)S(1)} %all-to-all-done.2.source, f32[8,128,256]{2,1,0:T(8,128)S(1)} %copy-done.1, f32[2,8,256]{2,1,0:T(8,128)S(1)} %copy-done.14, bf16[2,512,512]{2,1,0:T(8,128)(2,1)S(1)} %copy-done.5, f32[2,8,256]{2,1,0:T(8,128)S(1)} %copy-done.13, ...), custom_call_target="tpu_custom_call" | custom-call | flops 6000000000 | bytes 4194304 | tf_op jit(solution)/shard_map/pallas_call | solution.py:621
  77.9 28.7 %all_to_all.41.source = f32[32,64,128]{2,1,0:T(8,128)S(1)} all-to-all(f32[32,64,128]{2,1,0:T(8,128)S(1)} %shard_map.161), channel_id=1, replica_groups=mesh['px'=8,'py'=4] {'px','py'}, dimensions={0} | all-to-all | bytes 2097152 | tf_op jit(solution)/shard_map/all_to_all | solution.py:632
  106.6 4.7 %shard_map.162 = (f32[32,72,128]{2,1,0:T(8,128)S(1)}, f32[64,2048]{1,0:T(8,128)}) custom-call(f32[32,64,128]{2,1,0:T(8,128)S(1)} %all_to_all.41.source, f32[8,128,256]{2,1,0:T(8,128)S(1)} %copy-done.19, f32[2,8,256]{2,1,0:T(8,128)S(1)} %copy-done.13, bf16[2,512,512]{2,1,0:T(8,128)(2,1)S(1)} %copy-done.4, bf16[2,512,512]{2,1,0:T(8,128)(2,1)S(1)} %copy-done.6), custom_call_target="tpu_custom_call" | custom-call | flops 6000000000 | bytes 4194304 | tf_op jit(solution)/shard_map/pallas_call | solution.py:621
  111.3 34.0 %all_to_all.42.source = f32[32,72,128]{2,1,0:T(8,128)S(1)} all-to-all(f32[32,72,128]{2,1,0:T(8,128)S(1)} %get-tuple-element.20), channel_id=1, replica_groups=mesh['px'=8,'py'=4] {'px','py'}, dimensions={0} | all-to-all | bytes 2359296 | tf_op jit(solution)/shard_map/all_to_all | solution.py:632
  145.4 3.2 %shard_map.163 = (f32[32,32,128]{2,1,0:T(8,128)S(1)}, f32[8,128,256]{2,1,0:T(8,128)S(1)}, f32[8,128]{1,0:T(8,128)S(1)}) custom-call(s32[1]{0:T(128)} %bitcast.device_ref, f32[32,72,128]{2,1,0:T(8,128)S(1)} %all_to_all.42.source, f32[2,8,256]{2,1,0:T(8,128)S(1)} %copy-done.13, bf16[2,512,512]{2,1,0:T(8,128)(2,1)S(1)} %copy-done.6, ...), custom_call_target="tpu_custom_call" | custom-call | flops 6000000000 | bytes 4194304 | tf_op jit(solution)/shard_map/pallas_call | solution.py:621
  148.6 17.3 %all_to_all.43.source = f32[32,32,128]{2,1,0:T(8,128)S(1)} all-to-all(f32[32,32,128]{2,1,0:T(8,128)S(1)} %get-tuple-element.22), channel_id=1, replica_groups=mesh['px'=8,'py'=4] {'px','py'}, dimensions={0} | all-to-all | bytes 1048576 | tf_op jit(solution)/shard_map/all_to_all | solution.py:632
  166.0 1.8 shard_map.164
  168.6 18.3 %all_to_all.44.source = f32[32,32,128]{2,1,0:T(8,128)S(1)} all-to-all(f32[32,32,128]{2,1,0:T(8,128)S(1)} %get-tuple-element.24), channel_id=1, replica_groups=mesh['px'=8,'py'=4] {'px','py'}, dimensions={0} | all-to-all | bytes 1048576 | tf_op jit(solution)/shard_map/all_to_all | solution.py:632
  186.9 2.8 %shard_map.165 = f32[32,32,128]{2,1,0:T(8,128)} custom-call(f32[32,32,128]{2,1,0:T(8,128)S(1)} %all_to_all.44.source, f32[2,8,256]{2,1,0:T(8,128)S(1)} %copy-done.14, bf16[2,512,512]{2,1,0:T(8,128)(2,1)S(1)} %copy-done.5, f32[2,8,256]{2,1,0:T(8,128)S(1)} %copy-done.13, bf16[2,512,512]{2,1,0:T(8,128)(2,1)S(1)} %copy-done.4), custom_call_target="tpu_custom_call" | custom-call | flops 6000000000 | bytes 4194304 | tf_op jit(solution)/shard_map/pallas_call | solution.py:621
  189.7 3.0 %all-to-all-start.7 = ((f32[32,32,128]{2,1,0:T(8,128)}), f32[32,32,128]{2,1,0:T(8,128)S(1)}, u32[]{:S(2)}, u32[]{:S(2)}) async-start(f32[32,32,128]{2,1,0:T(8,128)} %shard_map.165), calls=%async_computation.7 | async-start | bytes 1048576 | tf_op jit(solution)/shard_map/all_to_all | solution.py:632
  193.2 2.9 %shard_map.168 = f32[2,64,2048]{2,1,0:T(8,128)} custom-call(f32[8,128,256]{2,1,0:T(8,128)} %copy-done), custom_call_target="tpu_custom_call" | custom-call | tf_op jit(solution)/shard_map/pallas_call | solution.py:668
  196.8 2.8 %shard_map.166.second = f32[8,64,256]{2,1,0:T(8,128)S(1)} custom-call(f32[8,64,256]{2,1,0:T(8,128)S(1)} %copy-done.26, f32[2,8,256]{2,1,0:T(8,128)S(1)} %copy-done.12, bf16[2,256,512]{2,1,0:T(8,128)(2,1)S(1)} %copy-done.10, bf16[2,512,256]{2,1,0:T(8,128)(2,1)S(1)} %copy-done.7, s32[1,256]{1,0:T(1,128)S(1)} %copy-done.15), custom_call_target="tpu_custom_call" | custom-call | flops 6000000000 | bytes 4194304 | tf_op jit(solution)/shard_map/pallas_call | solution.py:621
  199.5 8.8 %all-to-all-done.7.source = f32[32,32,128]{2,1,0:T(8,128)S(1)} async-done(((f32[32,32,128]{2,1,0:T(8,128)}), f32[32,32,128]{2,1,0:T(8,128)S(1)}, u32[]{:S(2)}, u32[]{:S(2)}) %all-to-all-start.7) | async-done | bytes 524320 | tf_op jit(solution)/shard_map/all_to_all | solution.py:632
  208.3 1.6 shard_map.167
  (51 shorter events, 3.0 us)
Async XLA Ops:
  0.6 1.0 copy-start.2
  1.7 1.0 copy-start.3
  2.7 23.9 %copy-start.4 = (bf16[2,512,512]{2,1,0:T(8,128)(2,1)S(1)}, bf16[2,512,512]{2,1,0:T(8,128)(2,1)}, u32[]{:S(2)}) copy-start(bf16[2,512,512]{2,1,0:T(8,128)(2,1)} %constant.43.clone.out_matrix.in_matrix) | copy-start | bytes 3145732
  2.7 23.9 %copy-start.5 = (bf16[2,512,512]{2,1,0:T(8,128)(2,1)S(1)}, bf16[2,512,512]{2,1,0:T(8,128)(2,1)}, u32[]{:S(2)}) copy-start(bf16[2,512,512]{2,1,0:T(8,128)(2,1)} %constant.42.clone.in_matrix) | copy-start | bytes 3145732
  2.7 23.9 %copy-start.13 = (f32[2,8,256]{2,1,0:T(8,128)S(1)}, f32[2,8,256]{2,1,0:T(8,128)}, u32[]{:S(2)}) copy-start(f32[2,8,256]{2,1,0:T(8,128)} %constant.35.clone.out_twiddle.twiddle.in_twiddle) | copy-start | bytes 49156
  2.7 23.9 %copy-start.14 = (f32[2,8,256]{2,1,0:T(8,128)S(1)}, f32[2,8,256]{2,1,0:T(8,128)}, u32[]{:S(2)}) copy-start(f32[2,8,256]{2,1,0:T(8,128)} %constant.37.clone.in_twiddle) | copy-start | bytes 49156
  3.8 22.8 %copy-start.16 = (f32[8,128,256]{2,1,0:T(8,128)}, f32[8,128,256]{2,1,0:T(8,128)S(1)}, u32[]{:S(2)}) copy-start(f32[8,128,256]{2,1,0:T(8,128)S(1)} %get-tuple-element.17.field_p.both_p) | copy-start | bytes 3145732
  26.6 5.8 %copy-start.7 = (bf16[2,512,256]{2,1,0:T(8,128)(2,1)S(1)}, bf16[2,512,256]{2,1,0:T(8,128)(2,1)}, u32[]{:S(2)}) copy-start(bf16[2,512,256]{2,1,0:T(8,128)(2,1)} %constant.41.clone.in_matrix) | copy-start | bytes 1572868
  26.6 5.8 %copy-start.12 = (f32[2,8,256]{2,1,0:T(8,128)S(1)}, f32[2,8,256]{2,1,0:T(8,128)}, u32[]{:S(2)}) copy-start(f32[2,8,256]{2,1,0:T(8,128)} %constant.36.clone.twiddle) | copy-start | bytes 49156
  26.6 5.8 %copy-start.15 = (s32[1,256]{1,0:T(1,128)S(1)}, s32[1,256]{1,0:T(1,128)}, u32[]{:S(2)}) copy-start(s32[1,256]{1,0:T(1,128)} %constant.39.clone.kept) | copy-start | bytes 3076
  29.5 18.6 %all-to-all-start.1 = ((f32[32,32,128]{2,1,0:T(8,128)}), f32[32,32,128]{2,1,0:T(8,128)S(1)}, u32[]{:S(2)}, u32[]{:S(2)}) async-start(f32[32,32,128]{2,1,0:T(8,128)} %shard_map.157), calls=%async_computation.1 | async-start | bytes 1048576 | tf_op jit(solution)/shard_map/all_to_all | solution.py:632
  32.5 1.0 copy-start.8
  33.5 1.2 copy-start.17
  37.5 0.8 copy-start.20
  48.1 1.0 copy-start.9
  49.1 1.2 copy-start.18
  50.3 1.0 copy-start.21
  53.9 0.8 copy-start.23
  54.7 18.6 %all-to-all-start.2 = ((f32[32,32,128]{2,1,0:T(8,128)}), f32[32,32,128]{2,1,0:T(8,128)S(1)}, u32[]{:S(2)}, u32[]{:S(2)}) async-start(f32[32,32,128]{2,1,0:T(8,128)} %get-tuple-element.18), calls=%async_computation.2 | async-start | bytes 1048576 | tf_op jit(solution)/shard_map/all_to_all | solution.py:632
  57.7 15.6 %copy-start.11 = (bf16[2,256,256]{2,1,0:T(8,128)(2,1)S(1)}, bf16[2,256,256]{2,1,0:T(8,128)(2,1)}, u32[]{:S(2)}) copy-start(bf16[2,256,256]{2,1,0:T(8,128)(2,1)} %constant.38.clone.mirror) | copy-start | bytes 786436
  73.3 1.2 copy-start.1
  77.9 28.7 %copy-start.6 = (bf16[2,512,512]{2,1,0:T(8,128)(2,1)S(1)}, bf16[2,512,512]{2,1,0:T(8,128)(2,1)}, u32[]{:S(2)}) copy-start(bf16[2,512,512]{2,1,0:T(8,128)(2,1)} %constant.44.clone.out_matrix.in_matrix) | copy-start | bytes 3145732
  77.9 28.7 %copy-start.19 = (f32[8,128,256]{2,1,0:T(8,128)S(1)}, f32[8,128,256]{2,1,0:T(8,128)}, u32[]{:S(2)}) copy-start(f32[8,128,256]{2,1,0:T(8,128)} %copy-done.16) | copy-start | bytes 3145732
  145.4 20.6 %copy-start.22 = (f32[8,64,256]{2,1,0:T(8,128)S(1)}, f32[8,64,256]{2,1,0:T(8,128)}, u32[]{:S(2)}) copy-start(f32[8,64,256]{2,1,0:T(8,128)} %copy-done.20) | copy-start | bytes 1572868
  145.4 20.6 %copy-start.24 = (f32[8,64,256]{2,1,0:T(8,128)S(1)}, f32[8,64,256]{2,1,0:T(8,128)}, u32[]{:S(2)}) copy-start(f32[8,64,256]{2,1,0:T(8,128)} %copy-done.23) | copy-start | bytes 1572868
  148.6 19.1 %copy-start = (f32[8,128,256]{2,1,0:T(8,128)}, f32[8,128,256]{2,1,0:T(8,128)S(1)}, u32[]{:S(2)}) copy-start(f32[8,128,256]{2,1,0:T(8,128)S(1)} %get-tuple-element.27.slabs) | copy-start | bytes 3145732
  167.8 0.8 copy-start.27
  168.6 18.3 %copy-start.25 = (f32[8,64,256]{2,1,0:T(8,128)}, f32[8,64,256]{2,1,0:T(8,128)S(1)}, u32[]{:S(2)}) copy-start(f32[8,64,256]{2,1,0:T(8,128)S(1)} %get-tuple-element.26.field_p) | copy-start | bytes 1572868
  189.7 18.6 %all-to-all-start.7 = ((f32[32,32,128]{2,1,0:T(8,128)}), f32[32,32,128]{2,1,0:T(8,128)S(1)}, u32[]{:S(2)}, u32[]{:S(2)}) async-start(f32[32,32,128]{2,1,0:T(8,128)} %shard_map.165), calls=%async_computation.7 | async-start | bytes 1048576 | tf_op jit(solution)/shard_map/all_to_all | solution.py:632
  192.7 4.0 %copy-start.10 = (bf16[2,256,512]{2,1,0:T(8,128)(2,1)S(1)}, bf16[2,256,512]{2,1,0:T(8,128)(2,1)}, u32[]{:S(2)}) copy-start(bf16[2,256,512]{2,1,0:T(8,128)(2,1)} %constant.40.clone.out_matrix) | copy-start | bytes 1572868
  192.7 4.0 %copy-start.26 = (f32[8,64,256]{2,1,0:T(8,128)S(1)}, f32[8,64,256]{2,1,0:T(8,128)}, u32[]{:S(2)}) copy-start(f32[8,64,256]{2,1,0:T(8,128)} %copy-done.25) | copy-start | bytes 1572868
  196.8 11.6 %copy-start.28 = (f32[8,64,256]{2,1,0:T(8,128)S(1)}, f32[8,64,256]{2,1,0:T(8,128)}, u32[]{:S(2)}) copy-start(f32[8,64,256]{2,1,0:T(8,128)} %copy-done.27) | copy-start | bytes 1572868

commit v2 on v1

--- a/solution.py
+++ b/solution.py
@@ -1,5 +1,6 @@
 import functools
 import math
+from types import SimpleNamespace
 
 import jax
 import jax.numpy as jnp
@@ -221,6 +222,32 @@
 
         return write
 
+    def outgoing_slots(self, twiddle, matrix, kept, other):
+        self.multiply(self.rows, matrix, real_in=True)
+        rows, half, blocks = self.rows, self.half, self.inner // self.rows
+        tall, step = rows * rows // TILE, self.step
+        for h in range(rows // tall):
+
+            def body(i, carry, h=h):
+                r0 = pl.multiple_of(i * step, step)
+                at = pl.ds(h * tall + r0, step)
+                items = self.pack_middle(small_dft([
+                    self.twist(k, (self.get(k, at, 0), self.get(k, at, 1)), -1.0, twiddle)
+                    for k in range(self.outer)
+                ], -1.0))
+                for j, pair in enumerate(items):
+                    for part, value in enumerate(pair):
+                        if 2 * j >= self.outer:
+                            value = exchange_lanes(value, rows)
+                        to = pl.ds(h * rows + part * half, half)
+                        for piece in range(blocks):
+                            for side, result in enumerate((kept, other)):
+                                base = piece * rows + side * half
+                                result[j * blocks + piece, pl.ds(r0, step), to] = value[:, base : base + half]
+                return carry
+
+            lax.fori_loop(0, tall // step, body, 0)
+
     def outgoing_kept(self, twiddle, matrix, result):
         self.multiply(self.rows, matrix, real_in=True)
         rows, half, blocks = self.rows, self.half, self.inner // self.rows
@@ -341,6 +368,71 @@
 
 def row_index(count, width):
     return lax.broadcasted_iota(jnp.int32, (count, width), 0)
+
+
+def exchange_lanes(value, rows):
+    half, wide = rows // 2, value.shape[1]
+    line = lax.broadcasted_iota(jnp.int32, value.shape, 1) % rows
+    up, down = pltpu.roll(value, half, 1), pltpu.roll(value, wide - half, 1)
+    return jnp.where(line == 0, down, jnp.where(line == half, up, value))
+
+
+def exchange_rows(held, first, second, swapped):
+    at, also = first, second
+    one, other = held[at], held[also]
+    top = lax.broadcasted_iota(jnp.int32, one.shape, one.ndim - 2) == 0
+    moved = top if swapped is None else jnp.logical_and(top, swapped)
+    held[at] = jnp.where(moved, other, one)
+    held[also] = jnp.where(moved, one, other)
+
+
+class Links:
+    def __init__(self, devices, fast):
+        self.devices, self.fast = devices, fast
+        self.device = lax.axis_index(axes[0]) * fast + lax.axis_index(axes[1])
+
+    def partner(self, i):
+        total, bit = 0, 1
+        while bit < self.devices:
+            total += bit * lax.rem(lax.div(self.device, bit) + lax.div(i, bit), 2)
+            bit *= 2
+        return total
+
+    def send(self, source, target, sems):
+        send_sem, recv_sem, own_sem = sems
+
+        def go(i, carry):
+            peer = self.partner(self.devices - i)
+            pltpu.make_async_remote_copy(
+                src_ref=source(peer),
+                dst_ref=target(self.device),
+                send_sem=send_sem,
+                recv_sem=recv_sem,
+                device_id=(lax.div(peer, self.fast), lax.rem(peer, self.fast)),
+                device_id_type=pl.DeviceIdType.MESH,
+            ).start()
+            return carry
+
+        lax.fori_loop(1, self.devices, go, 0)
+        pltpu.make_async_copy(source(self.device), target(self.device), own_sem).start()
+
+    def whole(self, source, target, sems):
+        others = pl.ds(0, self.devices - 1)
+        return pltpu.make_async_remote_copy(
+            src_ref=source(others),
+            dst_ref=target(others),
+            send_sem=sems[0],
+            recv_sem=sems[1],
+            device_id=(0, 0),
+            device_id_type=pl.DeviceIdType.MESH,
+        )
+
+    def receive(self, source, target, sems):
+        pltpu.make_async_copy(source(self.device), target(self.device), sems[2]).wait()
+        self.whole(source, target, sems).wait_recv()
+
+    def sent(self, source, target, sems):
+        self.whole(source, target, sems).wait_send()
 
 
 def start_kernel(length, rows, field, target, out, both_p, *scratch):
@@ -583,6 +675,334 @@
     piece = Pieces(length, rows)
     piece.turn_columns(source, first)
     piece.collect(lambda k: first[k] + value[k] + second[k], strided, [field_out])
+
+
+def slots_of(device, late, index, rows, half, other):
+    line = half + index if other else index
+    special = jnp.where(late, 0, half) if other else jnp.where(late, half, 0)
+    return device * rows + jnp.where(index == 0, special, line)
+
+
+def step_kernel(length, rows, devices, fast, inputs, outs, box):
+    links = Links(devices, fast)
+    device, half = links.device, rows // 2
+    late = device >= devices // 2
+    copies, sems = box.copies, box.sems
+    piece = Pieces(length, rows, box.turned, box.top, box.low, box.z)
+    step, inner, outer = piece.step, piece.inner, piece.outer
+    both_p, forcing_p, full = box.both_p, box.forcing_p, box.full
+    first, second, value = box.first, box.second, box.value
+    strided, total = box.strided, box.total
+
+    loads = [
+        pltpu.make_async_copy(ref, held, copies.at[i])
+        for i, (ref, held) in enumerate(zip(inputs.refs, inputs.held))
+    ]
+    for copy in loads:
+        copy.start()
+    waiting = iter(loads)
+
+    def load(count):
+        for i in range(count):
+            next(waiting).wait()
+
+    at_all = lambda ref: lambda e: ref.at[e]
+    at_lines = lambda ref, base, count: lambda e: ref.at[e, pl.ds(base, count)]
+    order = []
+
+    def send(source, target):
+        i = len(order)
+        order.append((source, target, (sems.at[i, 0], sems.at[i, 1], sems.at[i, 2])))
+        links.send(*order[-1])
+        return order[-1]
+
+    def receive(*moves):
+        for move in moves:
+            links.receive(*move)
+
+    def send_all(source, target):
+        return send(at_all(source), at_all(target))
+
+    tables = inputs.twiddles
+    tw_natural, tw_kept, tw_lines = (tables.at[i] for i in range(3))
+    forward, backward, lines_in = inputs.forward, inputs.backward, inputs.lines
+    kept_out, kept_in, kept, mirror = inputs.kept_out, inputs.kept_in, inputs.kept, inputs.mirror
+
+    def slope_first(source, out):
+        slope_first_kernel(
+            length, rows, source, tw_lines, lines_in, tw_natural, backward, out,
+            piece.turned, piece.top, piece.low, piece.z,
+        )
+
+    def slope_second(source, out):
+        slope_second_kernel(
+            length, rows, source, tw_kept, kept_out, kept_in, kept, out,
+            piece.turned, piece.top, piece.low, piece.z,
+        )
+
+    load(2)
+    piece.spread(inputs.field, inputs.target, strided, both_p)
+    piece.pack_columns(lambda k: both_p[k, pl.ds(0, rows), :], box.s_field)
+    m_field = send_all(box.s_field, box.r_field)
+
+    load(4)
+    slope_second(both_p, second)
+    load(1)
+    piece.spread(inputs.forcing.at[0], inputs.forcing.at[1], strided, forcing_p)
+    for k in range(outer):
+        for part in range(2):
+            at, also = (k, pl.ds(part * rows, 8)), (k, pl.ds(part * rows + half, 8))
+            exchange_rows(forcing_p, at, also, late)
+    load(4)
+
+    def rest(r0):
+        at = pl.ds(r0, step)
+        wave = second_wave(piece, slots_of(device, late, row_index(step, 1) + r0, rows, half, True))
+        for k in range(outer):
+            scale = time_step * inverse_denominator(first_waves(piece, k)[0], wave)
+            for part in range(2):
+                piece.put(k, at, part, scale * forcing_p[k, pl.ds(part * rows + half + r0, step), :])
+
+    piece.chunks(half, rest)
+    piece.outgoing(half, 1.0, tw_natural, backward, False, piece.write_full(box.s_rest, False))
+
+    def send_rest(base, count):
+        target = at_lines(box.r_next, half + base, count)
+        return send(at_lines(box.s_rest, base, count), target)
+
+    quarter = half // 4
+    m_rest0 = send_rest(0, quarter)
+
+    receive(m_field)
+    slope_first(box.r_field, box.s_slope)
+    m_slope = send_all(box.s_slope, box.r_slope)
+    m_rest1 = send_rest(quarter, quarter)
+
+    receive(m_slope)
+    nonlinear_kernel(
+        length, rows, box.r_slope, both_p, second, tw_kept, kept_out, box.s_sum, first,
+        piece.turned, piece.top, piece.low, piece.z,
+    )
+    m_sum = send_all(box.s_sum, box.r_sum)
+    m_rest2 = send_rest(2 * quarter, half - 2 * quarter)
+
+    receive(m_sum)
+    piece.turn_lines(box.r_sum)
+    piece.incoming(half, -1.0, tw_lines, lines_in)
+
+    def divide(r0):
+        at = pl.ds(r0, step)
+        wave = second_wave(piece, slots_of(device, late, row_index(step, 1) + r0, rows, half, False))
+        weight = weight_of(device, r0, step, inner)
+        for k in range(outer):
+            scale = inverse_denominator(first_waves(piece, k)[0], wave)
+            for part in range(2):
+                forced = time_step * forcing_p[k, pl.ds(part * rows + r0, step), :]
+                piece.put(k, at, part, (weight * piece.get(k, at, part) + forced) * scale)
+
+    piece.chunks(half, divide)
+
+    @pl.when(device == 0)
+    def _():
+        at = pl.ds(0, 8)
+        blocks = []
+        for k in range(outer):
+            own = tuple(piece.get(k, at, part) for part in range(2))
+            joined = tuple(own[part] + time_step * forcing_p[k, pl.ds(part * rows, 8), :] for part in range(2))
+            blocks.append([own, joined])
+        flipped = piece.mirrored(blocks, mirror)
+        for k in range(outer):
+            zero, middle = edge_inverses(piece, k)
+            for part in range(2):
+                own, joined = blocks[k][0][part], blocks[k][1][part]
+                own_c, joined_c = flipped[k][0][part], flipped[k][1][part]
+                replace(piece, k, part, 0.5 * ((joined + joined_c) * zero + (own - own_c) * middle))
+
+    piece.outgoing(half, 1.0, tw_natural, backward, False, piece.write_full(box.s_next, False))
+    m_next = send(at_all(box.s_next), at_lines(box.r_next, 0, half))
+
+    receive(m_rest0, m_rest1, m_rest2, m_next)
+    turned_late = pl.ds(devices // 2, devices // 2)
+    exchange_rows(box.r_next, (turned_late, pl.ds(0, 8)), (turned_late, pl.ds(half, 8)), None)
+    piece.turn_full(box.r_next)
+    piece.unpack_middle()
+    piece.incoming(rows, 1.0, tw_natural, backward, real_out=True)
+    total[...] = jnp.zeros_like(total)
+    lanes = pl.ds(0, inner)
+
+    def misfit(r0):
+        at = pl.ds(r0, step)
+        for k in range(outer):
+            now = piece.get(k, at, 0)
+            value[k, at, :] = now
+            residual = now - both_p[k, pl.ds(rows + r0, step), :]
+            total[...] += residual * residual
+            piece.put(k, at, 0, residual)
+
+    piece.chunks(rows, misfit)
+    piece.outgoing_slots(tw_natural, forward, box.s_kept, box.s_other)
+    m_kept = send_all(box.s_kept, box.r_kept)
+    count = rows * rows // TILE
+    eighth = count // 4
+
+    def send_other(base, size):
+        return send(at_lines(box.s_other, base, size), at_lines(box.r_other, base, size))
+
+    m_other0 = send_other(0, eighth)
+    box.s_total[...] = jnp.full(box.s_total.shape, 0.5 * jnp.sum(total[...]), jnp.float32)
+    m_total = send(lambda e: box.s_total.at[e], lambda e: box.r_total.at[e])
+    stores = []
+
+    def store(ref, out):
+        stores.append(pltpu.make_async_copy(ref, out, copies.at[len(loads) + len(stores)]))
+        stores[-1].start()
+
+    piece.collect(lambda k: value[k], strided, [box.o_next])
+    store(box.o_next, outs.next)
+
+    receive(m_kept)
+    piece.turn_lines(box.r_kept)
+    piece.incoming(half, -1.0, tw_lines, lines_in)
+
+    def adjoint(r0):
+        at = pl.ds(r0, step)
+        wave = second_wave(piece, slots_of(device, late, row_index(step, 1) + r0, rows, half, False))
+        weight = weight_of(device, r0, step, inner)
+        for k in range(outer):
+            scale = time_step * inverse_denominator(first_waves(piece, k)[0], wave)
+            for part in range(2):
+                own = piece.get(k, at, part) * scale
+                full[k, pl.ds(part * rows + r0, step), :] = own
+                piece.put(k, at, part, weight * own)
+
+    piece.chunks(half, adjoint)
+
+    @pl.when(device == 0)
+    def _():
+        at = pl.ds(0, 8)
+        blocks = [[(piece.get(k, at, 0), piece.get(k, at, 1))] for k in range(outer)]
+        flipped = piece.mirrored(blocks, mirror)
+        row0 = row_index(8, inner) == 0
+        for k in range(outer):
+            zero, middle = edge_inverses(piece, k)
+            for part in range(2):
+                own, own_c = blocks[k][0][part], flipped[k][0][part]
+                line = (0.5 * time_step) * (own + own_c) * zero
+                at_full = pl.ds(part * rows, 8)
+                full[k, at_full, :] = jnp.where(row0, line, full[k, at_full, :])
+                replace(piece, k, part, line + (0.5 * time_step) * (own - own_c) * middle)
+
+    piece.outgoing(half, 1.0, tw_natural, backward, False, piece.write_full(box.s_back, False))
+    m_back = send_all(box.s_back, box.r_back)
+    m_other1 = send_other(eighth, eighth)
+
+    receive(m_back)
+    joint_kernel(
+        length, rows, box.r_back, first, second, tw_kept, kept_in, box.s_product, value, box.product,
+        piece.turned, piece.top, piece.low, piece.z,
+    )
+    m_product = send_all(box.s_product, box.r_product)
+    m_other2 = send_other(2 * eighth, count - 2 * eighth)
+
+    slope_second(box.product, second)
+    for k in range(outer):
+        value[k] = value[k] + second[k]
+
+    receive(m_product)
+    slope_first(box.r_product, box.s_last)
+    m_last = send_all(box.s_last, box.r_last)
+
+    receive(m_other0, m_other1, m_other2, m_total)
+    piece.turn_lines(box.r_other)
+    piece.incoming(half, -1.0, tw_lines, lines_in)
+
+    def others(r0):
+        at = pl.ds(r0, step)
+        wave = second_wave(piece, slots_of(device, late, row_index(step, 1) + r0, rows, half, True))
+        for k in range(outer):
+            scale = time_step * inverse_denominator(first_waves(piece, k)[0], wave)
+            for part in range(2):
+                full[k, pl.ds(part * rows + half + r0, step), :] = piece.get(k, at, part) * scale
+
+    piece.chunks(half, others)
+    for k in range(outer):
+        for part in range(2):
+            at, also = (k, pl.ds(part * rows, 8)), (k, pl.ds(part * rows + half, 8))
+            exchange_rows(full, at, also, late)
+    piece.collect(lambda k: full[k], strided, [box.o_forcing.at[i] for i in range(2)])
+    store(box.o_forcing, outs.forcing)
+    outs.total[...] = jnp.sum(box.r_total[...], axis=0)
+
+    receive(m_last)
+    piece.turn_columns(box.r_last, first)
+    piece.collect(lambda k: first[k] + value[k], strided, [box.o_field])
+    store(box.o_field, outs.field)
+    for move in order:
+        links.sent(*move)
+    for copy in stores:
+        copy.wait()
+
+
+messages = 15
+
+
+def joined_step(field, target, forcing, devices, fast, rows, length):
+    outer, inner = split_length(length)
+    half, step = rows // 2, math.gcd(rows // 2, 16)
+    natural, kept, lines = orders(length, rows)
+    matrix = lambda *args: matrix_table(length, *args)
+    tables = dict(
+        field=field, target=target,
+        twiddles=np.stack([twiddle_table(length, o) for o in (natural, kept, lines)]),
+        kept=kept[None, :].astype(np.int32),
+        kept_out=matrix(-1.0, natural, kept)[:, :inner],
+        kept_in=matrix(1.0, kept, natural)[:, :, :inner],
+        forcing=forcing,
+        backward=matrix(1.0, natural, natural),
+        lines=matrix(-1.0, lines, natural),
+        forward=matrix(-1.0, natural, natural),
+        mirror=mirror_table(length),
+    )
+    operands = [jnp.asarray(table) for table in tables.values()]
+    float32 = jnp.float32
+    held = lambda *dims: pltpu.VMEM(dims, float32)
+    packed, lined = held(devices, rows * rows // TILE, TILE), held(devices, half, 2 * rows)
+    pair, one = held(outer, 2 * rows, inner), held(outer, rows, inner)
+    plain, small = held(rows, length), held(devices, 8, TILE)
+    halved = pltpu.VMEM((outer, rows, 2 * inner), jnp.bfloat16)
+    shapes = dict(
+        turned=held(2 * rows, length), top=halved, low=halved, z=held(outer, rows, 2 * inner),
+        strided=held(length, TILE), total=held(step, inner),
+        both_p=pair, forcing_p=pair, full=pair, first=one, second=one, value=one, product=one,
+        o_next=plain, o_field=plain, o_forcing=held(2, rows, length),
+        s_field=packed, r_field=packed, s_slope=lined, r_slope=lined, s_sum=packed, r_sum=packed,
+        s_rest=lined, s_next=lined, r_next=held(devices, rows, 2 * rows),
+        s_kept=packed, r_kept=packed, s_other=packed, r_other=packed, s_total=small, r_total=small,
+        s_back=lined, r_back=lined, s_product=packed, r_product=packed, s_last=lined, r_last=lined,
+        copies=pltpu.SemaphoreType.DMA((len(operands) + 3,)),
+        sems=pltpu.SemaphoreType.DMA((messages, 3)),
+    )
+    inputs = [pltpu.VMEM(operand.shape, operand.dtype) for operand in operands]
+
+    def body(*refs):
+        a, b = len(operands), len(operands) + 4
+        c = b + len(operands)
+        given = SimpleNamespace(refs=refs[:a], held=refs[b:c], **dict(zip(tables, refs[b:c])))
+        outs = SimpleNamespace(next=refs[a], field=refs[a + 1], forcing=refs[a + 2], total=refs[a + 3])
+        step_kernel(length, rows, devices, fast, given, outs, SimpleNamespace(**dict(zip(shapes, refs[c:]))))
+
+    anywhere = pl.BlockSpec(memory_space=pl.ANY)
+    shape = lambda *dims: jax.ShapeDtypeStruct(dims, float32)
+    next_field, field_grad, forcing_grad, total = pl.pallas_call(
+        body,
+        out_shape=(shape(rows, length), shape(rows, length), shape(2, rows, length), shape(8, TILE)),
+        in_specs=[anywhere] * len(operands),
+        out_specs=(anywhere, anywhere, anywhere, pl.BlockSpec(memory_space=pltpu.VMEM)),
+        scratch_shapes=inputs + list(shapes.values()),
+        compiler_params=pltpu.CompilerParams(vmem_limit_bytes=56 * 2**20, has_side_effects=True),
+        cost_estimate=pl.CostEstimate(flops=6 * 10**10, bytes_accessed=4 * 2**20, transcendentals=0),
+    )(*operands)
+    return next_field, total[0, 0], field_grad, forcing_grad
 
 
 def member_step(device, field, target, forcing_p, devices, rows, length):
@@ -657,7 +1077,7 @@
     return next_field, sums[0, 0], field_grad, full
 
 
-def per_device(devices, initial_field, target_field, forcing):
+def per_device(devices, fast, initial_field, target_field, forcing):
     members, rows, length = initial_field.shape
     device = lax.axis_index(axes).astype(jnp.int32).reshape(1)
     outer, inner = split_length(length)
@@ -673,6 +1093,15 @@
             scratch_shapes=[strided],
         )(operand)
 
+    if rows * rows % (TILE * 32) == 0 and TILE % rows == 0:
+        results = [
+            joined_step(initial_field[m], target_field[m], forcing, devices, fast, rows, length)
+            for m in range(members)
+        ]
+        next_field = jnp.stack([one[0] for one in results])
+        objective = sum(one[1] for one in results) / (members * length * length)
+        field_grad = jnp.stack([one[2] for one in results])
+        return (next_field, objective, field_grad, sum(one[3] for one in results))
     forcing_p = reorder(spread_kernel, (outer, 2 * rows, inner), forcing)
     results = [
         member_step(device, initial_field[m], target_field[m], forcing_p, devices, rows, length)
@@ -689,7 +1118,7 @@
     devices = mesh.shape["px"] * mesh.shape["py"]
     spec = P(None, axes, None)
     return jax.shard_map(
-        functools.partial(per_device, devices),
+        functools.partial(per_device, devices, mesh.shape["py"]),
         mesh=mesh,
         in_specs=(spec, spec, spec),
         out_specs=(spec, P(), spec, spec),

time: 212 us -> 148 us (0.70)
  blocking collectives: 121 us -> 0 us
  Pallas kernels: 35.2 us -> 141 us
  waiting for transfers between devices: 31.2 us -> 0 us
  starting transfers between devices: 8.92 us -> 0 us
  local copies, waits for them, and re-layouts: 11.9 us -> 4.97 us
    all_to_all x5 -> x0, blocking collectives: 121 us -> none  [move(): return lax.all_to_all(value, axes, split_axis=0, concat_axis=0, tiled=True)]
    pallas_call x13 -> x1, Pallas kernels: 35.2 us -> 141 us  [joined_step(): pl.pallas_call(body, out_shape=(shape(rows, length), shape(rows, length),...]
    all_to_all x3 -> x0, waiting for transfers between devices: 31.2 us -> none  [move(): return lax.all_to_all(value, axes, split_axis=0, concat_axis=0, tiled=True)]
    all_to_all x3 -> x0, starting transfers between devices: 8.92 us -> none  [move(): return lax.all_to_all(value, axes, split_axis=0, concat_axis=0, tiled=True)]
    unnamed x58 -> x7, local copies, waits for them, and re-layouts: 11.3 us -> 3.73 us
  transfers between devices with their start and end apart: 3 -> 0, of which waited for: 3 -> 0; matrix products, arithmetic and copies ran while one was open for 0% -> 0% of each run, Pallas kernels for 5% -> 0%
where the time goes in v2:
time: 148 us
  Pallas kernels  141 us (95%)
  local copies, waits for them, and re-layouts  4.97 us (3%)
  between operations  2.44 us (2%)
    pallas_call x1, Pallas kernels, joined_step(): pl.pallas_call(body, out_shape=(shape(rows, length), shape(rows, length),...  141 us
    unnamed x7, local copies, waits for them, and re-layouts  3.73 us

profile of v2, /device:TPU:0, one launch (start us, length us, event | category | flops | bytes accessed | tf_op | source)
XLA Modules:
  0.0 148.1 jit_solution(14738814172568223311)
XLA Ops:
  0.6 140.7 %shard_map.138 = (f32[64,2048]{1,0:T(8,128)}, f32[64,2048]{1,0:T(8,128)}, f32[2,64,2048]{2,1,0:T(8,128)}, f32[8,128]{1,0:T(8,128)}) custom-call(f32[64,2048]{1,0:T(8,128)} %bitcast.7, f32[64,2048]{1,0:T(8,128)} %bitcast.8, f32[3,2,8,256]{3,2,1,0:T(8,128)} %constant.20.clone.refs_2_, s32[1,256]{1,0:T(1,128)} %constant.21.clone.refs_3_, ...), custom_call_target="tpu_custom_call" | custom-call | flops 60000002048 | bytes 4194304 | tf_op jit(solution)/shard_map/pallas_call | solution.py:996
  141.3 0.0 copy-start.1
  141.3 1.2 slice.3
  143.2 0.0 copy-start
  143.2 2.0 %copy.18 = f32[1,64,2048]{2,1,0:T(8,128)} copy(f32[1,64,2048]{2,1,0:T(8,128)} %bitcast.6) | data formatting | bytes 1048576
  145.2 0.0 copy-done.1
  145.2 0.8 copy.19
  146.0 0.0 copy-done
  146.0 1.0 copy.20
Async XLA Ops:
  141.3 3.9 %copy-start.1 = (f32[64,2048]{1,0:T(8,128)S(1)}, f32[64,2048]{1,0:T(8,128)}, u32[]{:S(2)}) copy-start(f32[64,2048]{1,0:T(8,128)} %get-tuple-element.10) | copy-start | bytes 1572868
  143.2 2.8 %copy-start = (f32[2,64,2048]{2,1,0:T(8,128)S(1)}, f32[2,64,2048]{2,1,0:T(8,128)}, u32[]{:S(2)}) copy-start(f32[2,64,2048]{2,1,0:T(8,128)} %get-tuple-element.19) | copy-start | bytes 3145732

commit v3 on v2

--- a/solution.py
+++ b/solution.py
@@ -398,7 +398,7 @@
             bit *= 2
         return total
 
-    def send(self, source, target, sems):
+    def send(self, source, target, sems, share=0, shares=1):
         send_sem, recv_sem, own_sem = sems
 
         def go(i, carry):
@@ -413,8 +413,11 @@
             ).start()
             return carry
 
-        lax.fori_loop(1, self.devices, go, 0)
-        pltpu.make_async_copy(source(self.device), target(self.device), own_sem).start()
+        far, near = self.devices // 2, self.devices // 2 - 1
+        for base, count in ((1, far), (1 + far, near)):
+            lax.fori_loop(base + count * share // shares, base + count * (share + 1) // shares, go, 0)
+        if share == 0:
+            pltpu.make_async_copy(source(self.device), target(self.device), own_sem).start()
 
     def whole(self, source, target, sems):
         others = pl.ds(0, self.devices - 1)
@@ -698,7 +701,7 @@
         pltpu.make_async_copy(ref, held, copies.at[i])
         for i, (ref, held) in enumerate(zip(inputs.refs, inputs.held))
     ]
-    for copy in loads:
+    for copy in loads[:2]:
         copy.start()
     waiting = iter(loads)
 
@@ -710,11 +713,15 @@
     at_lines = lambda ref, base, count: lambda e: ref.at[e, pl.ds(base, count)]
     order = []
 
-    def send(source, target):
+    def plan(source, target):
         i = len(order)
         order.append((source, target, (sems.at[i, 0], sems.at[i, 1], sems.at[i, 2])))
-        links.send(*order[-1])
         return order[-1]
+
+    def send(source, target):
+        move = plan(source, target)
+        links.send(*move)
+        return move
 
     def receive(*moves):
         for move in moves:
@@ -741,6 +748,8 @@
         )
 
     load(2)
+    for copy in loads[2:]:
+        copy.start()
     piece.spread(inputs.field, inputs.target, strided, both_p)
     piece.pack_columns(lambda k: both_p[k, pl.ds(0, rows), :], box.s_field)
     m_field = send_all(box.s_field, box.r_field)
@@ -766,27 +775,23 @@
     piece.chunks(half, rest)
     piece.outgoing(half, 1.0, tw_natural, backward, False, piece.write_full(box.s_rest, False))
 
-    def send_rest(base, count):
-        target = at_lines(box.r_next, half + base, count)
-        return send(at_lines(box.s_rest, base, count), target)
-
-    quarter = half // 4
-    m_rest0 = send_rest(0, quarter)
+    m_rest = plan(at_all(box.s_rest), at_lines(box.r_next, half, half))
 
     receive(m_field)
+    links.send(*m_rest, 0, 3)
     slope_first(box.r_field, box.s_slope)
     m_slope = send_all(box.s_slope, box.r_slope)
-    m_rest1 = send_rest(quarter, quarter)
 
     receive(m_slope)
+    links.send(*m_rest, 1, 3)
     nonlinear_kernel(
         length, rows, box.r_slope, both_p, second, tw_kept, kept_out, box.s_sum, first,
         piece.turned, piece.top, piece.low, piece.z,
     )
     m_sum = send_all(box.s_sum, box.r_sum)
-    m_rest2 = send_rest(2 * quarter, half - 2 * quarter)
 
     receive(m_sum)
+    links.send(*m_rest, 2, 3)
     piece.turn_lines(box.r_sum)
     piece.incoming(half, -1.0, tw_lines, lines_in)
 
@@ -821,7 +826,7 @@
     piece.outgoing(half, 1.0, tw_natural, backward, False, piece.write_full(box.s_next, False))
     m_next = send(at_all(box.s_next), at_lines(box.r_next, 0, half))
 
-    receive(m_rest0, m_rest1, m_rest2, m_next)
+    receive(m_rest, m_next)
     turned_late = pl.ds(devices // 2, devices // 2)
     exchange_rows(box.r_next, (turned_late, pl.ds(0, 8)), (turned_late, pl.ds(half, 8)), None)
     piece.turn_full(box.r_next)
@@ -842,25 +847,13 @@
     piece.chunks(rows, misfit)
     piece.outgoing_slots(tw_natural, forward, box.s_kept, box.s_other)
     m_kept = send_all(box.s_kept, box.r_kept)
-    count = rows * rows // TILE
-    eighth = count // 4
-
-    def send_other(base, size):
-        return send(at_lines(box.s_other, base, size), at_lines(box.r_other, base, size))
-
-    m_other0 = send_other(0, eighth)
+    m_other = plan(at_all(box.s_other), at_all(box.r_other))
     box.s_total[...] = jnp.full(box.s_total.shape, 0.5 * jnp.sum(total[...]), jnp.float32)
     m_total = send(lambda e: box.s_total.at[e], lambda e: box.r_total.at[e])
-    stores = []
-
-    def store(ref, out):
-        stores.append(pltpu.make_async_copy(ref, out, copies.at[len(loads) + len(stores)]))
-        stores[-1].start()
-
-    piece.collect(lambda k: value[k], strided, [box.o_next])
-    store(box.o_next, outs.next)
+    piece.collect(lambda k: value[k], strided, [outs.next])
 
     receive(m_kept)
+    links.send(*m_other, 0, 3)
     piece.turn_lines(box.r_kept)
     piece.incoming(half, -1.0, tw_lines, lines_in)
 
@@ -894,25 +887,25 @@
 
     piece.outgoing(half, 1.0, tw_natural, backward, False, piece.write_full(box.s_back, False))
     m_back = send_all(box.s_back, box.r_back)
-    m_other1 = send_other(eighth, eighth)
 
     receive(m_back)
+    links.send(*m_other, 1, 3)
     joint_kernel(
         length, rows, box.r_back, first, second, tw_kept, kept_in, box.s_product, value, box.product,
         piece.turned, piece.top, piece.low, piece.z,
     )
     m_product = send_all(box.s_product, box.r_product)
-    m_other2 = send_other(2 * eighth, count - 2 * eighth)
 
     slope_second(box.product, second)
     for k in range(outer):
         value[k] = value[k] + second[k]
 
     receive(m_product)
+    links.send(*m_other, 2, 3)
     slope_first(box.r_product, box.s_last)
     m_last = send_all(box.s_last, box.r_last)
 
-    receive(m_other0, m_other1, m_other2, m_total)
+    receive(m_other, m_total)
     piece.turn_lines(box.r_other)
     piece.incoming(half, -1.0, tw_lines, lines_in)
 
@@ -929,21 +922,18 @@
         for part in range(2):
             at, also = (k, pl.ds(part * rows, 8)), (k, pl.ds(part * rows + half, 8))
             exchange_rows(full, at, also, late)
-    piece.collect(lambda k: full[k], strided, [box.o_forcing.at[i] for i in range(2)])
-    store(box.o_forcing, outs.forcing)
-    outs.total[...] = jnp.sum(box.r_total[...], axis=0)
+    piece.collect(lambda k: full[k], strided, [outs.forcing.at[i] for i in range(2)])
+    outs.total[...] = jnp.sum(box.r_total[...], axis=0) / (length * length)
 
     receive(m_last)
     piece.turn_columns(box.r_last, first)
-    piece.collect(lambda k: first[k] + value[k], strided, [box.o_field])
-    store(box.o_field, outs.field)
+    for k in range(outer):
+        outs.field[k] = first[k] + value[k]
     for move in order:
         links.sent(*move)
-    for copy in stores:
-        copy.wait()
-
-
-messages = 15
+
+
+messages = 11
 
 
 def joined_step(field, target, forcing, devices, fast, rows, length):
@@ -968,18 +958,17 @@
     held = lambda *dims: pltpu.VMEM(dims, float32)
     packed, lined = held(devices, rows * rows // TILE, TILE), held(devices, half, 2 * rows)
     pair, one = held(outer, 2 * rows, inner), held(outer, rows, inner)
-    plain, small = held(rows, length), held(devices, 8, TILE)
+    small = held(devices, 8, TILE)
     halved = pltpu.VMEM((outer, rows, 2 * inner), jnp.bfloat16)
     shapes = dict(
         turned=held(2 * rows, length), top=halved, low=halved, z=held(outer, rows, 2 * inner),
         strided=held(length, TILE), total=held(step, inner),
         both_p=pair, forcing_p=pair, full=pair, first=one, second=one, value=one, product=one,
-        o_next=plain, o_field=plain, o_forcing=held(2, rows, length),
         s_field=packed, r_field=packed, s_slope=lined, r_slope=lined, s_sum=packed, r_sum=packed,
         s_rest=lined, s_next=lined, r_next=held(devices, rows, 2 * rows),
         s_kept=packed, r_kept=packed, s_other=packed, r_other=packed, s_total=small, r_total=small,
         s_back=lined, r_back=lined, s_product=packed, r_product=packed, s_last=lined, r_last=lined,
-        copies=pltpu.SemaphoreType.DMA((len(operands) + 3,)),
+        copies=pltpu.SemaphoreType.DMA((len(operands),)),
         sems=pltpu.SemaphoreType.DMA((messages, 3)),
     )
     inputs = [pltpu.VMEM(operand.shape, operand.dtype) for operand in operands]
@@ -992,17 +981,42 @@
         step_kernel(length, rows, devices, fast, given, outs, SimpleNamespace(**dict(zip(shapes, refs[c:]))))
 
     anywhere = pl.BlockSpec(memory_space=pl.ANY)
+    vmem, smem = pl.BlockSpec(memory_space=pltpu.VMEM), pl.BlockSpec(memory_space=pltpu.SMEM)
     shape = lambda *dims: jax.ShapeDtypeStruct(dims, float32)
-    next_field, field_grad, forcing_grad, total = pl.pallas_call(
+    next_field, slabs, forcing_grad, total = pl.pallas_call(
         body,
-        out_shape=(shape(rows, length), shape(rows, length), shape(2, rows, length), shape(8, TILE)),
-        in_specs=[anywhere] * len(operands),
-        out_specs=(anywhere, anywhere, anywhere, pl.BlockSpec(memory_space=pltpu.VMEM)),
+        out_shape=(shape(rows, length), shape(outer, rows, inner), shape(2, rows, length), shape(8, TILE)),
+        in_specs=[pl.BlockSpec(memory_space=pltpu.HBM)] * len(operands),
+        out_specs=(vmem, vmem, vmem, vmem),
         scratch_shapes=inputs + list(shapes.values()),
-        compiler_params=pltpu.CompilerParams(vmem_limit_bytes=56 * 2**20, has_side_effects=True),
+        compiler_params=pltpu.CompilerParams(vmem_limit_bytes=34 * 2**20, has_side_effects=True),
         cost_estimate=pl.CostEstimate(flops=6 * 10**10, bytes_accessed=4 * 2**20, transcendentals=0),
-    )(*operands)
-    return next_field, total[0, 0], field_grad, forcing_grad
+    )(*[pltpu.with_memory_space_constraint(one, pltpu.HBM) for one in operands])
+    return pl.pallas_call(
+        functools.partial(tail_kernel, length, rows),
+        out_shape=(shape(rows, length), shape(rows, length), shape(2, rows, length), shape(1, 1)),
+        in_specs=[vmem] * 4,
+        out_specs=(anywhere, anywhere, anywhere, smem),
+        scratch_shapes=[held(length, TILE), held(rows, length), pltpu.SemaphoreType.DMA((3,))],
+        compiler_params=pltpu.CompilerParams(vmem_limit_bytes=8 * 2**20),
+        cost_estimate=pl.CostEstimate(flops=10**9, bytes_accessed=4 * 2**20, transcendentals=0),
+    )(next_field, slabs, forcing_grad, total)
+
+
+def tail_kernel(length, rows, next_field, slabs, forcing_grad, total, next_out, field_out, forcing_out, total_out, strided, held, sems):
+    piece = Pieces(length, rows)
+    copies = [
+        pltpu.make_async_copy(next_field, next_out, sems.at[0]),
+        pltpu.make_async_copy(forcing_grad, forcing_out, sems.at[1]),
+        pltpu.make_async_copy(held, field_out, sems.at[2]),
+    ]
+    copies[0].start()
+    copies[1].start()
+    total_out[0, 0] = jnp.sum(total[0:1, 0:1])
+    piece.collect(lambda k: slabs[k], strided, [held])
+    copies[2].start()
+    for copy in copies:
+        copy.wait()
 
 
 def member_step(device, field, target, forcing_p, devices, rows, length):
@@ -1099,9 +1113,10 @@
             for m in range(members)
         ]
         next_field = jnp.stack([one[0] for one in results])
-        objective = sum(one[1] for one in results) / (members * length * length)
-        field_grad = jnp.stack([one[2] for one in results])
-        return (next_field, objective, field_grad, sum(one[3] for one in results))
+        field_grad = jnp.stack([one[1] for one in results])
+        forcing_grad = sum(one[2] for one in results)
+        objective = sum(one[3].reshape(()) for one in results) / members
+        return (next_field, objective, field_grad, forcing_grad)
     forcing_p = reorder(spread_kernel, (outer, 2 * rows, inner), forcing)
     results = [
         member_step(device, initial_field[m], target_field[m], forcing_p, devices, rows, length)

time: 148 us -> 140 us (0.946)
  local copies, waits for them, and re-layouts: 4.97 us -> 0 us
  Pallas kernels: 141 us -> 139 us
  between operations: 2.44 us -> 0.8 us
    unnamed x7 -> x0, local copies, waits for them, and re-layouts: 3.73 us -> none
    pallas_call x1 -> x2, Pallas kernels: 141 us -> 139 us  [the longest x1 137 us: joined_step(): pl.pallas_call(body, out_shape=(shape(rows, length), shape(outer, rows, i...]
where the time goes in v3:
time: 140 us
  Pallas kernels  139 us (99%)
    pallas_call x1, Pallas kernels, joined_step(): pl.pallas_call(body, out_shape=(shape(rows, length), shape(outer, rows, i...  137 us

profile of v3, /device:TPU:0, one launch (start us, length us, event | category | flops | bytes accessed | tf_op | source)
XLA Modules:
  0.0 140.2 jit_solution(6840395881873654606)
XLA Ops:
  0.6 137.4 %shard_map.138 = (f32[64,2048]{1,0:T(8,128)S(1)}, f32[8,64,256]{2,1,0:T(8,128)S(1)}, f32[2,64,2048]{2,1,0:T(8,128)S(1)}, f32[8,128]{1,0:T(8,128)S(1)}) custom-call(f32[64,2048]{1,0:T(8,128)} %bitcast.5, f32[64,2048]{1,0:T(8,128)} %bitcast.6, f32[3,2,8,256]{3,2,1,0:T(8,128)} %constant.8.clone.refs_2_, s32[1,256]{1,0:T(1,128)} %constant.18.clone.refs_3_, ...), custom_call_target="tpu_custom_call" | custom-call | flops 60000002048 | bytes 4194304 | tf_op jit(solution)/shard_map/pallas_call | solution.py:986
  138.1 2.0 %shard_map.139 = (f32[64,2048]{1,0:T(8,128)}, f32[64,2048]{1,0:T(8,128)}, f32[2,64,2048]{2,1,0:T(8,128)}, f32[1,1]{1,0:T(1,128)}) custom-call(f32[64,2048]{1,0:T(8,128)S(1)} %get-tuple-element.12.next_field, f32[8,64,256]{2,1,0:T(8,128)S(1)} %get-tuple-element.13.slabs, f32[2,64,2048]{2,1,0:T(8,128)S(1)} %get-tuple-element.14.forcing_grad, ...), custom_call_target="tpu_custom_call" | custom-call | flops 1000000000 | bytes 4194304 | tf_op jit(solution)/shard_map/pallas_call | solution.py:995

commit v4 on v1

--- a/solution.py
+++ b/solution.py
@@ -1,5 +1,6 @@
 import functools
 import math
+from types import SimpleNamespace
 
 import jax
 import jax.numpy as jnp
@@ -47,6 +48,17 @@
     return low + high
 
 
+def half_dft(items, sign):
+    count = 2 * len(items)
+    turned = []
+    for j, (re, im) in enumerate(items):
+        c = math.cos(2.0 * math.pi * j / count)
+        s = sign * math.sin(2.0 * math.pi * j / count)
+        turned.append((re, im) if j == 0 else (c * re - s * im, c * im + s * re))
+    pairs = zip(small_dft(items, sign), small_dft(turned, sign))
+    return [one for pair in pairs for one in pair]
+
+
 def halves(value):
     top = value.astype(jnp.bfloat16)
     return top, (value - top.astype(jnp.float32)).astype(jnp.bfloat16)
@@ -60,11 +72,14 @@
     local = lane % (inner // 2)
     line = local % half
     kept = rows * (local // half) + np.where((lane >= inner // 2) & (line == 0), half, line)
-    groups = TILE // rows
-    tall = rows // groups
-    within = lane % (inner // groups)
-    lines = rows * (within // tall) + tall * (lane // (inner // groups)) + within % tall
-    return natural, kept, lines
+    return natural, kept, line_order(inner, rows, TILE // rows)
+
+
+def line_order(inner, rows, groups):
+    lane = np.arange(inner)
+    tall, wide = rows // groups, inner // groups
+    within = lane % wide
+    return rows * (within // tall) + tall * (lane // wide) + within % tall
 
 
 def twiddle_table(length, order):
@@ -126,9 +141,11 @@
         total = dot(top, right_top) + dot(low, right_top) + dot(top, right_low)
         self.z[:, :lines, :wide] = total.reshape(self.outer, lines, wide)
 
-    def twist(self, k, pair, sign, twiddle):
+    def twist(self, k, pair, sign, twiddle, flip=None):
         c = twiddle[0, pl.ds(k, 1), :]
         s = twiddle[1, pl.ds(k, 1), :]
+        if flip is not None and k % 2:
+            c, s = flip * c, flip * s
         s = s if sign > 0 else -s
         re, im = pair
         return (re * c - im * s, re * s + im * c)
@@ -220,6 +237,107 @@
                     result[to, at, pl.ds(rows, rows)] = im[:, lanes]
 
         return write
+
+    def pack_cut(self, slabs, results):
+        rows, half, wide = self.rows, self.half, self.inner // 2
+        cuts, count = len(results), half // len(results)
+        groups = TILE // (2 * count)
+        tall = rows // groups
+        for k in range(self.outer):
+            slab = slabs(k)
+            for s in range(self.inner // rows):
+                for q, result in enumerate(results):
+                    parts = []
+                    for group in range(groups):
+                        for part in range(2):
+                            at = part * wide + s * half + q * count
+                            parts.append(slab[group * tall : (group + 1) * tall, at : at + count])
+                    result[k * (self.inner // rows) + s] = jnp.concatenate(parts, axis=1)
+
+    def turn_cut(self, source, lines, spans):
+        blocks = self.inner // self.rows
+        groups = TILE // (2 * lines)
+        wide = self.inner // groups
+        for t in range(spans):
+            tile = source[pl.ds(t * blocks, blocks), :, :].reshape(wide, TILE).T
+            for h in range(groups):
+                held = tile[h * 2 * lines : (h + 1) * 2 * lines]
+                self.turned[: 2 * lines, pl.ds(t * self.inner + h * wide, wide)] = held
+
+    def turn_whole(self, source, tiles):
+        rows, blocks = self.rows, TILE // self.rows
+        for t in range(tiles):
+            tile = source[pl.ds(t * blocks, blocks), :rows, :].reshape(TILE, 2 * rows)
+            self.turned[: 2 * rows, pl.ds(t * TILE, TILE)] = tile.T
+
+    def first_imaginary(self, at):
+        rows = self.rows
+        part = self.turned[rows : 2 * rows, pl.ds(at, TILE)]
+        lane0 = lax.broadcasted_iota(jnp.int32, part.shape, 1) == 0
+        self.turned[rows : 2 * rows, pl.ds(at, TILE)] = jnp.where(lane0, 0.0, part)
+        return jnp.where(lane0, part, 0.0)
+
+    def incoming_half(self, lines, sign, twiddle, matrix, flip, extra=None, real_out=False):
+        def body(r0):
+            at = pl.ds(r0, self.step)
+            items = []
+            for j in range(self.outer // 2):
+                lanes = pl.ds(j * self.inner, self.inner)
+                items.append((self.turned[at, lanes], self.turned[pl.ds(lines + r0, self.step), lanes]))
+            for k, (re, im) in enumerate(half_dft(items, sign)):
+                if extra is not None:
+                    re = re - extra[at, :] if k % 2 else re + extra[at, :]
+                re, im = self.twist(k, (re, im), sign, twiddle, flip)
+                self.put(k, at, 0, re)
+                self.put(k, at, 1, im)
+
+        self.chunks(lines, body)
+        self.multiply(lines, matrix, real_out=real_out)
+
+    def outgoing_half(self, lines, sign, twiddle, matrix, flip, write):
+        self.multiply(lines, matrix)
+
+        def body(r0):
+            at = pl.ds(r0, self.step)
+            write(r0, small_dft([
+                self.twist(k, (self.get(k, at, 0), self.get(k, at, 1)), sign, twiddle, flip)
+                for k in range(self.outer)
+            ], sign)[: self.outer // 2])
+
+        self.chunks(lines, body)
+
+    def outgoing_sides(self, twiddle, matrix, sides, late=None):
+        self.multiply(self.rows, matrix, real_in=True)
+        rows, half, blocks, middle = self.rows, self.half, self.inner // self.rows, self.outer // 2
+        tall, step = rows * rows // TILE, self.step
+        for h in range(rows // tall):
+
+            def body(i, carry, h=h):
+                r0 = pl.multiple_of(i * step, step)
+                at = pl.ds(h * tall + r0, step)
+                items = small_dft([
+                    self.twist(k, (self.get(k, at, 0), self.get(k, at, 1)), -1.0, twiddle)
+                    for k in range(self.outer)
+                ], -1.0)
+                (low, low_im), (high, high_im) = items[0], items[middle]
+                lane0 = lax.broadcasted_iota(jnp.int32, low.shape, 1) == 0
+                items[0] = (low, jnp.where(lane0, high, low_im))
+                items[middle] = (high, jnp.where(lane0, low, high_im))
+                if late is not None:
+                    items = [
+                        tuple(jnp.where(late, one, other) for one, other in zip(items[middle + j], items[j]))
+                        for j in range(middle)
+                    ]
+                for j, pair in enumerate(items):
+                    for part, value in enumerate(pair):
+                        to = pl.ds(h * rows + part * half, half)
+                        for piece in range(blocks):
+                            for side, result in enumerate(sides):
+                                base = piece * rows + side * half
+                                result[j * blocks + piece, pl.ds(r0, step), to] = value[:, base : base + half]
+                return carry
+
+            lax.fori_loop(0, tall // step, body, 0)
 
     def outgoing_kept(self, twiddle, matrix, result):
         self.multiply(self.rows, matrix, real_in=True)
@@ -341,6 +459,57 @@
 
 def row_index(count, width):
     return lax.broadcasted_iota(jnp.int32, (count, width), 0)
+
+
+class Links:
+    def __init__(self, devices, fast):
+        self.devices, self.fast = devices, fast
+        self.device = lax.axis_index(axes[0]) * fast + lax.axis_index(axes[1])
+
+    def partner(self, i):
+        total, bit = 0, 1
+        while bit < self.devices:
+            total += bit * lax.rem(lax.div(self.device, bit) + lax.div(i, bit), 2)
+            bit *= 2
+        return total
+
+    def send(self, source, target, sems, count):
+        send_sem, recv_sem, own_sem = sems
+        own = lax.rem(self.device, count)
+
+        def go(i, carry):
+            peer = self.partner(count - i)
+            pltpu.make_async_remote_copy(
+                src_ref=source(lax.rem(peer, count)),
+                dst_ref=target(own),
+                send_sem=send_sem,
+                recv_sem=recv_sem,
+                device_id=(lax.div(peer, self.fast), lax.rem(peer, self.fast)),
+                device_id_type=pl.DeviceIdType.MESH,
+            ).start()
+            return carry
+
+        lax.fori_loop(1, count, go, 0)
+        pltpu.make_async_copy(source(own), target(own), own_sem).start()
+
+    def whole(self, source, target, sems, count):
+        others = pl.ds(0, count - 1)
+        return pltpu.make_async_remote_copy(
+            src_ref=source(others),
+            dst_ref=target(others),
+            send_sem=sems[0],
+            recv_sem=sems[1],
+            device_id=(0, 0),
+            device_id_type=pl.DeviceIdType.MESH,
+        )
+
+    def receive(self, source, target, sems, count):
+        own = lax.rem(self.device, count)
+        pltpu.make_async_copy(source(own), target(own), sems[2]).wait()
+        self.whole(source, target, sems, count).wait_recv()
+
+    def sent(self, source, target, sems, count):
+        self.whole(source, target, sems, count).wait_send()
 
 
 def start_kernel(length, rows, field, target, out, both_p, *scratch):
@@ -583,6 +752,356 @@
     piece = Pieces(length, rows)
     piece.turn_columns(source, first)
     piece.collect(lambda k: first[k] + value[k] + second[k], strided, [field_out])
+
+
+def step_kernel(length, rows, devices, fast, cuts, inputs, outs, box):
+    links = Links(devices, fast)
+    device, half, part_devices = links.device, rows // 2, devices // 2
+    late = device >= part_devices
+    flip = jnp.where(late, -1.0, 1.0).astype(jnp.float32)
+    sides = range(2)
+    copies, sems = box.copies, box.sems
+    work = (box.turned, box.top, box.low, box.z)
+    piece = Pieces(length, rows, *work)
+    step, inner, outer = piece.step, piece.inner, piece.outer
+    both_p, forcing_p, full = box.both_p, box.forcing_p, box.full
+    first, second, value = box.first, box.second, box.value
+    strided, total = box.strided, box.total
+    lanes = pl.ds(0, inner)
+
+    loads = [
+        pltpu.make_async_copy(ref, held, copies.at[i])
+        for i, (ref, held) in enumerate(zip(inputs.refs, inputs.held))
+    ]
+    for copy in loads[:2]:
+        copy.start()
+    waiting = iter(loads)
+
+    def load(count):
+        for i in range(count):
+            next(waiting).wait()
+
+    at_all = lambda ref: lambda e: ref.at[e]
+    at_lines = lambda ref, base, count: lambda e: ref.at[e, pl.ds(base, count)]
+    order = []
+
+    def send(source, target, count=devices):
+        i = len(order)
+        order.append((source, target, (sems.at[i, 0], sems.at[i, 1], sems.at[i, 2]), count))
+        links.send(*order[-1])
+        return order[-1]
+
+    def receive(*moves):
+        for move in moves:
+            links.receive(*move)
+
+    tw_natural, tw_kept, tw_lines, tw_cut = (inputs.twiddles.at[i] for i in range(4))
+    forward, backward, mirror = inputs.forward, inputs.backward, inputs.mirror
+    kept_out, kept_in, kept = inputs.kept_out, inputs.kept_in, inputs.kept
+    lines_in, cut_in = box.lines_in, box.cut_in
+
+    def permute_rows(groups, result):
+        tall, blocks = rows // groups, inner // rows
+        for p in range(2):
+            for part in range(2):
+                for group in range(groups):
+                    for s in range(blocks):
+                        at = part * inner + group * (inner // groups) + s * tall
+                        source = part * inner + s * rows + group * tall
+                        result[p, pl.ds(at, tall), :] = forward[p, pl.ds(source, tall), :]
+
+    def slope_first(source, out, lines):
+        piece.turn_cut(source, lines, outer)
+        piece.incoming(lines, -1.0, tw_cut, cut_in)
+
+        def body(r0):
+            at = pl.ds(r0, step)
+            for k in range(outer):
+                re, im = piece.get(k, at, 0), piece.get(k, at, 1)
+                scale = first_waves(piece, k)[1]
+                piece.put(k, at, 0, -scale * im)
+                piece.put(k, at, 1, scale * re)
+
+        piece.chunks(lines, body)
+        piece.outgoing(lines, 1.0, tw_natural, backward, False, piece.write_full(out, False))
+
+    def slope_second(source, out):
+        slope_second_kernel(length, rows, source, tw_kept, kept_out, kept_in, kept, out, *work)
+
+    def send_columns(source, target):
+        return [send(at_all(source.at[q]), at_all(target.at[q])) for q in range(cuts)]
+
+    def turn_slopes(moves, source, back, target):
+        count, result = half // cuts, []
+        for q, move in enumerate(moves):
+            receive(move)
+            slope_first(source.at[q], back.at[q], count)
+            result.append(send(at_all(back.at[q]), at_lines(target, q * count, count)))
+        return result
+
+    def lines_of(side, r0):
+        line = row_index(step, 1) + r0 + side * half
+        alone = (row_index(step, inner) + r0 + side * half + lax.rem(device, part_devices)) == 0
+        return second_wave(piece, device * rows + line), jnp.where(alone, jnp.float32(1.0), jnp.float32(2.0))
+
+    def edges(k):
+        wave = first_waves(piece, k)[0]
+        middle = jnp.full((1, 1), length // 2, jnp.int32)
+        mine, theirs = jnp.where(late, middle, 0), jnp.where(late, 0, middle)
+        return [inverse_denominator(wave, signed_waves(p, length)[0]) for p in (mine, theirs)]
+
+    load(2)
+    for copy in loads[2:]:
+        copy.start()
+    piece.spread(inputs.field, inputs.target, strided, both_p)
+    piece.pack_cut(lambda k: both_p[k, pl.ds(0, rows), :], [box.s_field.at[q] for q in range(cuts)])
+    m_field = send_columns(box.s_field, box.r_field)
+
+    load(len(loads) - 2)
+    permute_rows(TILE // rows, lines_in)
+    permute_rows(TILE * cuts // rows, cut_in)
+    slope_second(both_p, second)
+    m_slope = turn_slopes(m_field, box.r_field, box.s_slope, box.r_slope)
+    piece.spread(inputs.forcing.at[0], inputs.forcing.at[1], strided, forcing_p)
+
+    receive(*m_slope)
+    piece.turn_columns(box.r_slope, first)
+
+    def nonlinear(r0):
+        at = pl.ds(r0, step)
+        for k in range(outer):
+            one, other = first[k, at, :], second[k, at, :]
+            piece.put(k, at, 0, both_p[k, at, :] - (0.5 * time_step) * (one * one + other * other))
+
+    piece.chunks(rows, nonlinear)
+    piece.outgoing_sides(tw_natural, forward, [box.s_sum.at[side] for side in sides], late)
+    m_sum = [send(at_all(box.s_sum.at[side]), at_all(box.r_sum.at[side]), part_devices) for side in sides]
+
+    def divide(side):
+        def body(r0):
+            at = pl.ds(r0, step)
+            wave, weight = lines_of(side, r0)
+            for k in range(outer):
+                scale = inverse_denominator(first_waves(piece, k)[0], wave)
+                for part in range(2):
+                    forced = time_step * forcing_p[k, pl.ds(part * rows + side * half + r0, step), :]
+                    piece.put(k, at, part, (weight * piece.get(k, at, part) + forced) * scale)
+
+        piece.chunks(half, body)
+        if side:
+            return
+
+        @pl.when(lax.rem(device, part_devices) == 0)
+        def _():
+            at = pl.ds(0, 8)
+            blocks = []
+            for k in range(outer):
+                own = tuple(piece.get(k, at, part) for part in range(2))
+                joined = tuple(own[part] + time_step * forcing_p[k, pl.ds(part * rows, 8), :] for part in range(2))
+                blocks.append([own, joined])
+            flipped = piece.mirrored(blocks, mirror)
+            for k in range(outer):
+                mine, theirs = edges(k)
+                for part in range(2):
+                    own, joined = blocks[k][0][part], blocks[k][1][part]
+                    own_c, joined_c = flipped[k][0][part], flipped[k][1][part]
+                    replace(piece, k, part, 0.5 * ((joined + joined_c) * mine + (own - own_c) * theirs))
+
+    m_next = []
+    for side in sides:
+        receive(m_sum[side])
+        piece.turn_cut(box.r_sum.at[side], half, outer // 2)
+        piece.incoming_half(half, -1.0, tw_lines, lines_in, flip)
+        divide(side)
+        sent = box.s_next.at[side]
+        piece.outgoing(half, 1.0, tw_natural, backward, False, piece.write_full(sent, False))
+        m_next.append(send(at_all(sent), at_lines(box.r_next, side * half, half)))
+
+    receive(*m_next)
+    piece.turn_whole(box.r_next, length // TILE)
+    low, high = piece.first_imaginary(0), piece.first_imaginary(length // 2)
+    piece.turned[:rows, pl.ds(0, TILE)] += high
+    piece.turned[:rows, pl.ds(length // 2, TILE)] += low
+    piece.incoming(rows, 1.0, tw_natural, backward, real_out=True)
+    total[...] = jnp.zeros_like(total)
+
+    def misfit(r0):
+        at = pl.ds(r0, step)
+        for k in range(outer):
+            now = piece.get(k, at, 0)
+            value[k, at, :] = now
+            residual = now - both_p[k, pl.ds(rows + r0, step), :]
+            total[...] += residual * residual
+            piece.put(k, at, 0, residual)
+
+    piece.chunks(rows, misfit)
+    piece.outgoing_sides(tw_natural, forward, [box.s_kept.at[side] for side in sides])
+    m_kept = [send(at_all(box.s_kept.at[side]), at_all(box.r_kept.at[side])) for side in sides]
+    box.s_total[...] = jnp.full(box.s_total.shape, 0.5 * jnp.sum(total[...]), jnp.float32)
+    m_total = send(at_all(box.s_total), at_all(box.r_total))
+    piece.collect(lambda k: value[k], strided, [outs.next])
+
+    def adjoint(side):
+        def body(r0):
+            at = pl.ds(r0, step)
+            wave, weight = lines_of(side, r0)
+            for k in range(outer):
+                scale = time_step * inverse_denominator(first_waves(piece, k)[0], wave)
+                for part in range(2):
+                    own = piece.get(k, at, part) * scale
+                    full[k, pl.ds(part * rows + side * half + r0, step), :] = own
+                    piece.put(k, at, part, weight * own)
+
+        piece.chunks(half, body)
+        if side:
+            return
+
+        @pl.when(lax.rem(device, part_devices) == 0)
+        def _():
+            at = pl.ds(0, 8)
+            blocks = [[(piece.get(k, at, 0), piece.get(k, at, 1))] for k in range(outer)]
+            flipped = piece.mirrored(blocks, mirror)
+            row0 = row_index(8, inner) == 0
+            for k in range(outer):
+                mine, theirs = edges(k)
+                for part in range(2):
+                    own, own_c = blocks[k][0][part], flipped[k][0][part]
+                    line = (0.5 * time_step) * (own + own_c) * mine
+                    at_full = pl.ds(part * rows, 8)
+                    full[k, at_full, :] = jnp.where(row0, line, full[k, at_full, :])
+                    replace(piece, k, part, line + (0.5 * time_step) * (own - own_c) * theirs)
+
+    m_back = []
+    for side in sides:
+        receive(m_kept[side])
+        piece.turn_cut(box.r_kept.at[side], half, outer)
+        piece.incoming(half, -1.0, tw_lines, lines_in)
+        adjoint(side)
+        sent = box.s_back.at[side]
+        piece.outgoing_half(half, 1.0, tw_natural, backward, flip, piece.write_full(sent, False))
+        m_back.append(send(at_all(sent), at_lines(box.r_back, side * half, half), part_devices))
+
+    receive(*m_back)
+    piece.turn_whole(box.r_back, length // (2 * TILE))
+    box.extra[:, pl.ds(0, TILE)] = piece.first_imaginary(0)
+    box.extra[:, pl.ds(TILE, inner - TILE)] = jnp.zeros((rows, inner - TILE), jnp.float32)
+    piece.incoming_half(rows, 1.0, tw_natural, backward, flip, box.extra, real_out=True)
+
+    def products(r0):
+        at = pl.ds(r0, step)
+        for k in range(outer):
+            now = piece.get(k, at, 0)
+            value[k, at, :] = (1.0 / time_step) * now
+            box.product[k, at, :] = now * second[k, at, :]
+            piece.z[k, at, lanes] = now * first[k, at, :]
+
+    piece.chunks(rows, products)
+    piece.pack_cut(lambda k: piece.z[k, pl.ds(0, rows), lanes], [box.s_product.at[q] for q in range(cuts)])
+    m_product = send_columns(box.s_product, box.r_product)
+    slope_second(box.product, second)
+    for k in range(outer):
+        value[k] = value[k] + second[k]
+    m_last = turn_slopes(m_product, box.r_product, box.s_last, box.r_last)
+
+    piece.collect(lambda k: full[k], strided, [outs.forcing.at[i] for i in range(2)])
+    receive(m_total)
+    outs.total[...] = jnp.sum(box.r_total[...], axis=0) / (length * length)
+
+    receive(*m_last)
+    piece.turn_columns(box.r_last, first)
+    for k in range(outer):
+        outs.field[k] = first[k] + value[k]
+    for move in order:
+        links.sent(*move)
+
+
+def joined_step(field, target, forcing, devices, fast, rows, length):
+    outer, inner = split_length(length)
+    half, step, cuts = rows // 2, math.gcd(rows // 2, 16), 2
+    natural, kept, lines = orders(length, rows)
+    cut = line_order(inner, rows, TILE * cuts // rows)
+    matrix = lambda *args: matrix_table(length, *args)
+    tables = dict(
+        field=field, target=target,
+        twiddles=np.stack([twiddle_table(length, o) for o in (natural, kept, lines, cut)]),
+        kept=kept[None, :].astype(np.int32),
+        kept_out=matrix(-1.0, natural, kept)[:, :inner],
+        kept_in=matrix(1.0, kept, natural)[:, :, :inner],
+        forcing=forcing,
+        backward=matrix(1.0, natural, natural),
+        forward=matrix(-1.0, natural, natural),
+        mirror=mirror_table(length),
+    )
+    operands = [jnp.asarray(table) for table in tables.values()]
+    float32 = jnp.float32
+    held = lambda *dims: pltpu.VMEM(dims, float32)
+    packed, lined = held(2, devices, rows * rows // TILE, TILE), held(2, devices, half, 2 * rows)
+    packed_half, lined_half = (held(2, devices // 2, *dims.shape[2:]) for dims in (packed, lined))
+    columns, slopes = held(cuts, devices, rows * rows // (TILE * cuts), TILE), held(cuts, devices, half // cuts, 2 * rows)
+    returned = held(devices, half, 2 * rows)
+    table = pltpu.VMEM((2, 2 * inner, 2 * inner), jnp.bfloat16)
+    pair, one = held(outer, 2 * rows, inner), held(outer, rows, inner)
+    small = held(devices, 8, TILE)
+    halved = pltpu.VMEM((outer, rows, 2 * inner), jnp.bfloat16)
+    shapes = dict(
+        turned=held(2 * rows, length), top=halved, low=halved, z=held(outer, rows, 2 * inner),
+        strided=held(length, TILE), total=held(step, inner),
+        both_p=pair, forcing_p=pair, full=pair, first=one, second=one, value=one, product=one,
+        lines_in=table, cut_in=table, extra=held(rows, inner),
+        s_field=columns, r_field=columns, s_slope=slopes, r_slope=returned,
+        s_sum=packed_half, r_sum=packed_half, s_next=lined, r_next=held(devices, rows, 2 * rows),
+        s_kept=packed, r_kept=packed, s_total=small, r_total=small,
+        s_back=lined_half, r_back=held(devices // 2, rows, 2 * rows),
+        s_product=columns, r_product=columns, s_last=slopes, r_last=returned,
+        copies=pltpu.SemaphoreType.DMA((len(operands),)),
+        sems=pltpu.SemaphoreType.DMA((9 + 4 * cuts, 3)),
+    )
+    inputs = [pltpu.VMEM(operand.shape, operand.dtype) for operand in operands]
+
+    def body(*refs):
+        a, b = len(operands), len(operands) + 4
+        c = b + len(operands)
+        given = SimpleNamespace(refs=refs[:a], held=refs[b:c], **dict(zip(tables, refs[b:c])))
+        outs = SimpleNamespace(next=refs[a], field=refs[a + 1], forcing=refs[a + 2], total=refs[a + 3])
+        step_kernel(length, rows, devices, fast, cuts, given, outs, SimpleNamespace(**dict(zip(shapes, refs[c:]))))
+
+    anywhere = pl.BlockSpec(memory_space=pl.ANY)
+    vmem, smem = pl.BlockSpec(memory_space=pltpu.VMEM), pl.BlockSpec(memory_space=pltpu.SMEM)
+    shape = lambda *dims: jax.ShapeDtypeStruct(dims, float32)
+    next_field, slabs, forcing_grad, total = pl.pallas_call(
+        body,
+        out_shape=(shape(rows, length), shape(outer, rows, inner), shape(2, rows, length), shape(8, TILE)),
+        in_specs=[pl.BlockSpec(memory_space=pltpu.HBM)] * len(operands),
+        out_specs=(vmem, vmem, vmem, vmem),
+        scratch_shapes=inputs + list(shapes.values()),
+        compiler_params=pltpu.CompilerParams(vmem_limit_bytes=34 * 2**20, has_side_effects=True),
+        cost_estimate=pl.CostEstimate(flops=6 * 10**10, bytes_accessed=4 * 2**20, transcendentals=0),
+    )(*[pltpu.with_memory_space_constraint(one, pltpu.HBM) for one in operands])
+    return pl.pallas_call(
+        functools.partial(tail_kernel, length, rows),
+        out_shape=(shape(rows, length), shape(rows, length), shape(2, rows, length), shape(1, 1)),
+        in_specs=[vmem] * 4,
+        out_specs=(anywhere, anywhere, anywhere, smem),
+        scratch_shapes=[held(length, TILE), held(rows, length), pltpu.SemaphoreType.DMA((3,))],
+        compiler_params=pltpu.CompilerParams(vmem_limit_bytes=8 * 2**20),
+        cost_estimate=pl.CostEstimate(flops=10**9, bytes_accessed=4 * 2**20, transcendentals=0),
+    )(next_field, slabs, forcing_grad, total)
+
+
+def tail_kernel(length, rows, next_field, slabs, forcing_grad, total, next_out, field_out, forcing_out, total_out, strided, held, sems):
+    piece = Pieces(length, rows)
+    copies = [
+        pltpu.make_async_copy(next_field, next_out, sems.at[0]),
+        pltpu.make_async_copy(forcing_grad, forcing_out, sems.at[1]),
+        pltpu.make_async_copy(held, field_out, sems.at[2]),
+    ]
+    copies[0].start()
+    copies[1].start()
+    total_out[0, 0] = jnp.sum(total[0:1, 0:1])
+    piece.collect(lambda k: slabs[k], strided, [held])
+    copies[2].start()
+    for copy in copies:
+        copy.wait()
 
 
 def member_step(device, field, target, forcing_p, devices, rows, length):
@@ -657,7 +1176,7 @@
     return next_field, sums[0, 0], field_grad, full
 
 
-def per_device(devices, initial_field, target_field, forcing):
+def per_device(devices, fast, initial_field, target_field, forcing):
     members, rows, length = initial_field.shape
     device = lax.axis_index(axes).astype(jnp.int32).reshape(1)
     outer, inner = split_length(length)
@@ -673,6 +1192,16 @@
             scratch_shapes=[strided],
         )(operand)
 
+    if rows * rows % (TILE * 32) == 0 and TILE % rows == 0:
+        results = [
+            joined_step(initial_field[m], target_field[m], forcing, devices, fast, rows, length)
+            for m in range(members)
+        ]
+        next_field = jnp.stack([one[0] for one in results])
+        field_grad = jnp.stack([one[1] for one in results])
+        forcing_grad = sum(one[2] for one in results)
+        objective = sum(one[3].reshape(()) for one in results) / members
+        return (next_field, objective, field_grad, forcing_grad)
     forcing_p = reorder(spread_kernel, (outer, 2 * rows, inner), forcing)
     results = [
         member_step(device, initial_field[m], target_field[m], forcing_p, devices, rows, length)
@@ -689,7 +1218,7 @@
     devices = mesh.shape["px"] * mesh.shape["py"]
     spec = P(None, axes, None)
     return jax.shard_map(
-        functools.partial(per_device, devices),
+        functools.partial(per_device, devices, mesh.shape["py"]),
         mesh=mesh,
         in_specs=(spec, spec, spec),
         out_specs=(spec, P(), spec, spec),

time: 212 us -> 136 us (0.64)
  blocking collectives: 121 us -> 0 us
  Pallas kernels: 35.2 us -> 135 us
  waiting for transfers between devices: 31.2 us -> 0 us
  local copies, waits for them, and re-layouts: 11.9 us -> 0 us
  starting transfers between devices: 8.92 us -> 0 us
    all_to_all x5 -> x0, blocking collectives: 121 us -> none  [move(): return lax.all_to_all(value, axes, split_axis=0, concat_axis=0, tiled=True)]
    pallas_call x13 -> x2, Pallas kernels: 35.2 us -> 135 us  [the longest x1 133 us: joined_step(): pl.pallas_call(body, out_shape=(shape(rows, length), shape(outer, rows, i...]
    all_to_all x3 -> x0, waiting for transfers between devices: 31.2 us -> none  [move(): return lax.all_to_all(value, axes, split_axis=0, concat_axis=0, tiled=True)]
    unnamed x58 -> x0, local copies, waits for them, and re-layouts: 11.3 us -> none
    all_to_all x3 -> x0, starting transfers between devices: 8.92 us -> none  [move(): return lax.all_to_all(value, axes, split_axis=0, concat_axis=0, tiled=True)]
  transfers between devices with their start and end apart: 3 -> 0, of which waited for: 3 -> 0; matrix products, arithmetic and copies ran while one was open for 0% -> 0% of each run, Pallas kernels for 5% -> 0%
where the time goes in v4:
time: 136 us
  Pallas kernels  135 us (99%)
    pallas_call x1, Pallas kernels, joined_step(): pl.pallas_call(body, out_shape=(shape(rows, length), shape(outer, rows, i...  133 us

profile of v4, /device:TPU:0, one launch (start us, length us, event | category | flops | bytes accessed | tf_op | source)
XLA Modules:
  0.0 135.6 jit_solution(15908564210139401955)
XLA Ops:
  0.6 132.8 %shard_map.129 = (f32[64,2048]{1,0:T(8,128)S(1)}, f32[8,64,256]{2,1,0:T(8,128)S(1)}, f32[2,64,2048]{2,1,0:T(8,128)S(1)}, f32[8,128]{1,0:T(8,128)S(1)}) custom-call(f32[64,2048]{1,0:T(8,128)} %bitcast.5, f32[64,2048]{1,0:T(8,128)} %bitcast.6, f32[4,2,8,256]{3,2,1,0:T(8,128)} %constant.7.clone.refs_2_, s32[1,256]{1,0:T(1,128)} %constant.16.clone.refs_3_, ...), custom_call_target="tpu_custom_call" | custom-call | flops 60000002048 | bytes 4194304 | tf_op jit(solution)/shard_map/pallas_call | solution.py:1071
  133.4 2.0 %shard_map.130 = (f32[64,2048]{1,0:T(8,128)}, f32[64,2048]{1,0:T(8,128)}, f32[2,64,2048]{2,1,0:T(8,128)}, f32[1,1]{1,0:T(1,128)}) custom-call(f32[64,2048]{1,0:T(8,128)S(1)} %get-tuple-element.12.next_field, f32[8,64,256]{2,1,0:T(8,128)S(1)} %get-tuple-element.13.slabs, f32[2,64,2048]{2,1,0:T(8,128)S(1)} %get-tuple-element.14.forcing_grad, ...), custom_call_target="tpu_custom_call" | custom-call | flops 1000000000 | bytes 4194304 | tf_op jit(solution)/shard_map/pallas_call | solution.py:1080

commit v5 on v4

--- a/solution.py
+++ b/solution.py
@@ -473,6 +473,22 @@
             bit *= 2
         return total
 
+    def place(self, peer):
+        return (lax.div(peer, self.fast), lax.rem(peer, self.fast))
+
+    def greet(self):
+        barrier = pltpu.get_barrier_semaphore()
+
+        def go(i, carry):
+            at = self.place(self.partner(self.devices - i))
+            pl.semaphore_signal(barrier, inc=1, device_id=at, device_id_type=pl.DeviceIdType.MESH)
+            return carry
+
+        lax.fori_loop(1, self.devices, go, 0)
+
+    def meet(self):
+        pl.semaphore_wait(pltpu.get_barrier_semaphore(), self.devices - 1)
+
     def send(self, source, target, sems, count):
         send_sem, recv_sem, own_sem = sems
         own = lax.rem(self.device, count)
@@ -484,7 +500,7 @@
                 dst_ref=target(own),
                 send_sem=send_sem,
                 recv_sem=recv_sem,
-                device_id=(lax.div(peer, self.fast), lax.rem(peer, self.fast)),
+                device_id=self.place(peer),
                 device_id_type=pl.DeviceIdType.MESH,
             ).start()
             return carry
@@ -775,6 +791,7 @@
     ]
     for copy in loads[:2]:
         copy.start()
+    links.greet()
     waiting = iter(loads)
 
     def load(count):
@@ -855,6 +872,7 @@
         copy.start()
     piece.spread(inputs.field, inputs.target, strided, both_p)
     piece.pack_cut(lambda k: both_p[k, pl.ds(0, rows), :], [box.s_field.at[q] for q in range(cuts)])
+    links.meet()
     m_field = send_columns(box.s_field, box.r_field)
 
     load(len(loads) - 2)
@@ -1074,7 +1092,7 @@
         in_specs=[pl.BlockSpec(memory_space=pltpu.HBM)] * len(operands),
         out_specs=(vmem, vmem, vmem, vmem),
         scratch_shapes=inputs + list(shapes.values()),
-        compiler_params=pltpu.CompilerParams(vmem_limit_bytes=34 * 2**20, has_side_effects=True),
+        compiler_params=pltpu.CompilerParams(vmem_limit_bytes=34 * 2**20, has_side_effects=True, collective_id=0),
         cost_estimate=pl.CostEstimate(flops=6 * 10**10, bytes_accessed=4 * 2**20, transcendentals=0),
     )(*[pltpu.with_memory_space_constraint(one, pltpu.HBM) for one in operands])
     return pl.pallas_call(

time: 136 us -> 131 us (0.963)
  Pallas kernels: 135 us -> 130 us
    pallas_call x1, Pallas kernels: 133 us -> 128 us  [joined_step(): pl.pallas_call(body, out_shape=(shape(rows, length), shape(outer, rows, i...]
where the time goes in v5:
time: 131 us
  Pallas kernels  130 us (99%)
    pallas_call x1, Pallas kernels, joined_step(): pl.pallas_call(body, out_shape=(shape(rows, length), shape(outer, rows, i...  128 us

profile of v5, /device:TPU:0, one launch (start us, length us, event | category | flops | bytes accessed | tf_op | source)
XLA Modules:
  0.0 130.8 jit_solution(15974056554010982910)
XLA Ops:
  0.6 128.0 %shard_map.129 = (f32[64,2048]{1,0:T(8,128)S(1)}, f32[8,64,256]{2,1,0:T(8,128)S(1)}, f32[2,64,2048]{2,1,0:T(8,128)S(1)}, f32[8,128]{1,0:T(8,128)S(1)}) custom-call(f32[64,2048]{1,0:T(8,128)} %bitcast.5, f32[64,2048]{1,0:T(8,128)} %bitcast.6, f32[4,2,8,256]{3,2,1,0:T(8,128)} %constant.7.clone.refs_2_, s32[1,256]{1,0:T(1,128)} %constant.16.clone.refs_3_, ...), custom_call_target="tpu_custom_call" | custom-call | flops 60000002048 | bytes 4194304 | tf_op jit(solution)/shard_map/pallas_call | solution.py:1089
  128.7 2.0 %shard_map.130 = (f32[64,2048]{1,0:T(8,128)}, f32[64,2048]{1,0:T(8,128)}, f32[2,64,2048]{2,1,0:T(8,128)}, f32[1,1]{1,0:T(1,128)}) custom-call(f32[64,2048]{1,0:T(8,128)S(1)} %get-tuple-element.12.next_field, f32[8,64,256]{2,1,0:T(8,128)S(1)} %get-tuple-element.13.slabs, f32[2,64,2048]{2,1,0:T(8,128)S(1)} %get-tuple-element.14.forcing_grad, ...), custom_call_target="tpu_custom_call" | custom-call | flops 1000000000 | bytes 4194304 | tf_op jit(solution)/shard_map/pallas_call | solution.py:1098

commit v6 on v5

--- a/solution.py
+++ b/solution.py
@@ -308,8 +308,9 @@
 
     def outgoing_sides(self, twiddle, matrix, sides, late=None):
         self.multiply(self.rows, matrix, real_in=True)
-        rows, half, blocks, middle = self.rows, self.half, self.inner // self.rows, self.outer // 2
-        tall, step = rows * rows // TILE, self.step
+        rows, blocks, middle = self.rows, self.inner // self.rows, self.outer // 2
+        lines, step = rows // len(sides), self.step
+        tall = 2 * lines * rows // TILE
         for h in range(rows // tall):
 
             def body(i, carry, h=h):
@@ -330,11 +331,11 @@
                     ]
                 for j, pair in enumerate(items):
                     for part, value in enumerate(pair):
-                        to = pl.ds(h * rows + part * half, half)
+                        to = pl.ds((2 * h + part) * lines, lines)
                         for piece in range(blocks):
                             for side, result in enumerate(sides):
-                                base = piece * rows + side * half
-                                result[j * blocks + piece, pl.ds(r0, step), to] = value[:, base : base + half]
+                                base = piece * rows + side * lines
+                                result[j * blocks + piece, pl.ds(r0, step), to] = value[:, base : base + lines]
                 return carry
 
             lax.fori_loop(0, tall // step, body, 0)
@@ -465,6 +466,28 @@
     def __init__(self, devices, fast):
         self.devices, self.fast = devices, fast
         self.device = lax.axis_index(axes[0]) * fast + lax.axis_index(axes[1])
+        self.near = min(8, devices // 2)
+        self.steps = []
+        for low in range(self.near):
+            step, bit = 0, 1
+            while bit < self.near:
+                if low // bit % 2:
+                    step += bit * (1 - 2 * lax.rem(lax.div(self.device, bit), 2))
+                bit *= 2
+            self.steps.append(step)
+
+    def visit(self, count, body):
+        near = self.near
+
+        def far(i, carry):
+            base = self.partner(count - near * i)
+            for low in reversed(range(near)):
+                body(base + self.steps[low])
+            return carry
+
+        lax.fori_loop(1, count // near, far, 0)
+        for low in reversed(range(1, near)):
+            body(self.device + self.steps[low])
 
     def partner(self, i):
         total, bit = 0, 1
@@ -479,12 +502,11 @@
     def greet(self):
         barrier = pltpu.get_barrier_semaphore()
 
-        def go(i, carry):
-            at = self.place(self.partner(self.devices - i))
+        def go(peer):
+            at = self.place(peer)
             pl.semaphore_signal(barrier, inc=1, device_id=at, device_id_type=pl.DeviceIdType.MESH)
-            return carry
-
-        lax.fori_loop(1, self.devices, go, 0)
+
+        self.visit(self.devices, go)
 
     def meet(self):
         pl.semaphore_wait(pltpu.get_barrier_semaphore(), self.devices - 1)
@@ -493,19 +515,17 @@
         send_sem, recv_sem, own_sem = sems
         own = lax.rem(self.device, count)
 
-        def go(i, carry):
-            peer = self.partner(count - i)
+        def go(peer):
             pltpu.make_async_remote_copy(
-                src_ref=source(lax.rem(peer, count)),
+                src_ref=source(peer if count == self.devices else lax.rem(peer, count)),
                 dst_ref=target(own),
                 send_sem=send_sem,
                 recv_sem=recv_sem,
                 device_id=self.place(peer),
                 device_id_type=pl.DeviceIdType.MESH,
             ).start()
-            return carry
-
-        lax.fori_loop(1, count, go, 0)
+
+        self.visit(count, go)
         pltpu.make_async_copy(source(own), target(own), own_sem).start()
 
     def whole(self, source, target, sems, count):
@@ -770,12 +790,12 @@
     piece.collect(lambda k: first[k] + value[k] + second[k], strided, [field_out])
 
 
-def step_kernel(length, rows, devices, fast, cuts, inputs, outs, box):
+def step_kernel(length, rows, devices, fast, cuts, parts, inputs, outs, box):
     links = Links(devices, fast)
     device, half, part_devices = links.device, rows // 2, devices // 2
     late = device >= part_devices
     flip = jnp.where(late, -1.0, 1.0).astype(jnp.float32)
-    sides = range(2)
+    sides, count = range(parts), rows // parts
     copies, sems = box.copies, box.sems
     work = (box.turned, box.top, box.low, box.z)
     piece = Pieces(length, rows, *work)
@@ -816,6 +836,8 @@
     forward, backward, mirror = inputs.forward, inputs.backward, inputs.mirror
     kept_out, kept_in, kept = inputs.kept_out, inputs.kept_in, inputs.kept
     lines_in, cut_in = box.lines_in, box.cut_in
+    if parts == 2 * cuts:
+        tw_lines, lines_in = tw_cut, cut_in
 
     def permute_rows(groups, result):
         tall, blocks = rows // groups, inner // rows
@@ -849,16 +871,16 @@
         return [send(at_all(source.at[q]), at_all(target.at[q])) for q in range(cuts)]
 
     def turn_slopes(moves, source, back, target):
-        count, result = half // cuts, []
+        size, result = half // cuts, []
         for q, move in enumerate(moves):
             receive(move)
-            slope_first(source.at[q], back.at[q], count)
-            result.append(send(at_all(back.at[q]), at_lines(target, q * count, count)))
+            slope_first(source.at[q], back.at[q], size)
+            result.append(send(at_all(back.at[q]), at_lines(target, q * size, size)))
         return result
 
     def lines_of(side, r0):
-        line = row_index(step, 1) + r0 + side * half
-        alone = (row_index(step, inner) + r0 + side * half + lax.rem(device, part_devices)) == 0
+        line = row_index(step, 1) + r0 + side * count
+        alone = (row_index(step, inner) + r0 + side * count + lax.rem(device, part_devices)) == 0
         return second_wave(piece, device * rows + line), jnp.where(alone, jnp.float32(1.0), jnp.float32(2.0))
 
     def edges(k):
@@ -876,7 +898,8 @@
     m_field = send_columns(box.s_field, box.r_field)
 
     load(len(loads) - 2)
-    permute_rows(TILE // rows, lines_in)
+    if parts != 2 * cuts:
+        permute_rows(TILE * parts // (2 * rows), lines_in)
     permute_rows(TILE * cuts // rows, cut_in)
     slope_second(both_p, second)
     m_slope = turn_slopes(m_field, box.r_field, box.s_slope, box.r_slope)
@@ -902,10 +925,10 @@
             for k in range(outer):
                 scale = inverse_denominator(first_waves(piece, k)[0], wave)
                 for part in range(2):
-                    forced = time_step * forcing_p[k, pl.ds(part * rows + side * half + r0, step), :]
+                    forced = time_step * forcing_p[k, pl.ds(part * rows + side * count + r0, step), :]
                     piece.put(k, at, part, (weight * piece.get(k, at, part) + forced) * scale)
 
-        piece.chunks(half, body)
+        piece.chunks(count, body)
         if side:
             return
 
@@ -928,12 +951,12 @@
     m_next = []
     for side in sides:
         receive(m_sum[side])
-        piece.turn_cut(box.r_sum.at[side], half, outer // 2)
-        piece.incoming_half(half, -1.0, tw_lines, lines_in, flip)
+        piece.turn_cut(box.r_sum.at[side], count, outer // 2)
+        piece.incoming_half(count, -1.0, tw_lines, lines_in, flip)
         divide(side)
         sent = box.s_next.at[side]
-        piece.outgoing(half, 1.0, tw_natural, backward, False, piece.write_full(sent, False))
-        m_next.append(send(at_all(sent), at_lines(box.r_next, side * half, half)))
+        piece.outgoing(count, 1.0, tw_natural, backward, False, piece.write_full(sent, False))
+        m_next.append(send(at_all(sent), at_lines(box.r_next, side * count, count)))
 
     receive(*m_next)
     piece.turn_whole(box.r_next, length // TILE)
@@ -967,10 +990,10 @@
                 scale = time_step * inverse_denominator(first_waves(piece, k)[0], wave)
                 for part in range(2):
                     own = piece.get(k, at, part) * scale
-                    full[k, pl.ds(part * rows + side * half + r0, step), :] = own
+                    full[k, pl.ds(part * rows + side * count + r0, step), :] = own
                     piece.put(k, at, part, weight * own)
 
-        piece.chunks(half, body)
+        piece.chunks(count, body)
         if side:
             return
 
@@ -992,12 +1015,12 @@
     m_back = []
     for side in sides:
         receive(m_kept[side])
-        piece.turn_cut(box.r_kept.at[side], half, outer)
-        piece.incoming(half, -1.0, tw_lines, lines_in)
+        piece.turn_cut(box.r_kept.at[side], count, outer)
+        piece.incoming(count, -1.0, tw_lines, lines_in)
         adjoint(side)
         sent = box.s_back.at[side]
-        piece.outgoing_half(half, 1.0, tw_natural, backward, flip, piece.write_full(sent, False))
-        m_back.append(send(at_all(sent), at_lines(box.r_back, side * half, half), part_devices))
+        piece.outgoing_half(count, 1.0, tw_natural, backward, flip, piece.write_full(sent, False))
+        m_back.append(send(at_all(sent), at_lines(box.r_back, side * count, count), part_devices))
 
     receive(*m_back)
     piece.turn_whole(box.r_back, length // (2 * TILE))
@@ -1036,7 +1059,9 @@
 def joined_step(field, target, forcing, devices, fast, rows, length):
     outer, inner = split_length(length)
     half, step, cuts = rows // 2, math.gcd(rows // 2, 16), 2
-    natural, kept, lines = orders(length, rows)
+    parts = 2
+    natural, kept = orders(length, rows)[:2]
+    lines = line_order(inner, rows, TILE * parts // (2 * rows))
     cut = line_order(inner, rows, TILE * cuts // rows)
     matrix = lambda *args: matrix_table(length, *args)
     tables = dict(
@@ -1053,13 +1078,14 @@
     operands = [jnp.asarray(table) for table in tables.values()]
     float32 = jnp.float32
     held = lambda *dims: pltpu.VMEM(dims, float32)
-    packed, lined = held(2, devices, rows * rows // TILE, TILE), held(2, devices, half, 2 * rows)
-    packed_half, lined_half = (held(2, devices // 2, *dims.shape[2:]) for dims in (packed, lined))
+    packed = held(parts, devices, 2 * rows * rows // (parts * TILE), TILE)
+    lined = held(parts, devices, rows // parts, 2 * rows)
+    packed_half, lined_half = (held(parts, devices // 2, *dims.shape[2:]) for dims in (packed, lined))
     columns, slopes = held(cuts, devices, rows * rows // (TILE * cuts), TILE), held(cuts, devices, half // cuts, 2 * rows)
     returned = held(devices, half, 2 * rows)
     table = pltpu.VMEM((2, 2 * inner, 2 * inner), jnp.bfloat16)
     pair, one = held(outer, 2 * rows, inner), held(outer, rows, inner)
-    small = held(devices, 8, TILE)
+    small = held(devices, 1, TILE)
     halved = pltpu.VMEM((outer, rows, 2 * inner), jnp.bfloat16)
     shapes = dict(
         turned=held(2 * rows, length), top=halved, low=halved, z=held(outer, rows, 2 * inner),
@@ -1072,7 +1098,7 @@
         s_back=lined_half, r_back=held(devices // 2, rows, 2 * rows),
         s_product=columns, r_product=columns, s_last=slopes, r_last=returned,
         copies=pltpu.SemaphoreType.DMA((len(operands),)),
-        sems=pltpu.SemaphoreType.DMA((9 + 4 * cuts, 3)),
+        sems=pltpu.SemaphoreType.DMA((1 + 4 * parts + 4 * cuts, 3)),
     )
     inputs = [pltpu.VMEM(operand.shape, operand.dtype) for operand in operands]
 
@@ -1081,14 +1107,14 @@
         c = b + len(operands)
         given = SimpleNamespace(refs=refs[:a], held=refs[b:c], **dict(zip(tables, refs[b:c])))
         outs = SimpleNamespace(next=refs[a], field=refs[a + 1], forcing=refs[a + 2], total=refs[a + 3])
-        step_kernel(length, rows, devices, fast, cuts, given, outs, SimpleNamespace(**dict(zip(shapes, refs[c:]))))
+        step_kernel(length, rows, devices, fast, cuts, parts, given, outs, SimpleNamespace(**dict(zip(shapes, refs[c:]))))
 
     anywhere = pl.BlockSpec(memory_space=pl.ANY)
     vmem, smem = pl.BlockSpec(memory_space=pltpu.VMEM), pl.BlockSpec(memory_space=pltpu.SMEM)
     shape = lambda *dims: jax.ShapeDtypeStruct(dims, float32)
     next_field, slabs, forcing_grad, total = pl.pallas_call(
         body,
-        out_shape=(shape(rows, length), shape(outer, rows, inner), shape(2, rows, length), shape(8, TILE)),
+        out_shape=(shape(rows, length), shape(outer, rows, inner), shape(2, rows, length), shape(1, TILE)),
         in_specs=[pl.BlockSpec(memory_space=pltpu.HBM)] * len(operands),
         out_specs=(vmem, vmem, vmem, vmem),
         scratch_shapes=inputs + list(shapes.values()),

time: 131 us -> 129 us (0.985)
  Pallas kernels: 130 us -> 128 us
    pallas_call x1, Pallas kernels: 128 us -> 126 us  [joined_step(): pl.pallas_call(body, out_shape=(shape(rows, length), shape(outer, rows, i...]
where the time goes in v6:
time: 129 us
  Pallas kernels  128 us (99%)
    pallas_call x1, Pallas kernels, joined_step(): pl.pallas_call(body, out_shape=(shape(rows, length), shape(outer, rows, i...  126 us

profile of v6, /device:TPU:0, one launch (start us, length us, event | category | flops | bytes accessed | tf_op | source)
XLA Modules:
  0.0 128.8 jit_solution(1115872072653724097)
XLA Ops:
  0.6 126.0 %shard_map.129 = (f32[64,2048]{1,0:T(8,128)S(1)}, f32[8,64,256]{2,1,0:T(8,128)S(1)}, f32[2,64,2048]{2,1,0:T(8,128)S(1)}, f32[1,128]{1,0:T(1,128)S(1)}) custom-call(f32[64,2048]{1,0:T(8,128)} %bitcast.5, f32[64,2048]{1,0:T(8,128)} %bitcast.6, f32[4,2,8,256]{3,2,1,0:T(8,128)} %constant.7.clone.refs_2_, s32[1,256]{1,0:T(1,128)} %constant.16.clone.refs_3_, ...), custom_call_target="tpu_custom_call" | custom-call | flops 60000002048 | bytes 4194304 | tf_op jit(solution)/shard_map/pallas_call | solution.py:1115
  126.6 2.0 %shard_map.130 = (f32[64,2048]{1,0:T(8,128)}, f32[64,2048]{1,0:T(8,128)}, f32[2,64,2048]{2,1,0:T(8,128)}, f32[1,1]{1,0:T(1,128)}) custom-call(f32[64,2048]{1,0:T(8,128)S(1)} %get-tuple-element.12.next_field, f32[8,64,256]{2,1,0:T(8,128)S(1)} %get-tuple-element.13.slabs, f32[2,64,2048]{2,1,0:T(8,128)S(1)} %get-tuple-element.14.forcing_grad, ...), custom_call_target="tpu_custom_call" | custom-call | flops 1000000000 | bytes 4194304 | tf_op jit(solution)/shard_map/pallas_call | solution.py:1124

commit v7 on v6

--- a/solution.py
+++ b/solution.py
@@ -250,7 +250,7 @@
                     parts = []
                     for group in range(groups):
                         for part in range(2):
-                            at = part * wide + s * half + q * count
+                            at = part * wide + (q * (self.inner // rows) + s) * count
                             parts.append(slab[group * tall : (group + 1) * tall, at : at + count])
                     result[k * (self.inner // rows) + s] = jnp.concatenate(parts, axis=1)
 
@@ -269,6 +269,52 @@
         for t in range(tiles):
             tile = source[pl.ds(t * blocks, blocks), :rows, :].reshape(TILE, 2 * rows)
             self.turned[: 2 * rows, pl.ds(t * TILE, TILE)] = tile.T
+
+    def turn_side(self, source, base, lines, spans):
+        blocks = self.inner // self.rows
+        for j in range(spans):
+            tile = source[pl.ds(j * blocks, blocks), pl.ds(base, lines), :].reshape(blocks * lines, 2 * self.rows)
+            self.turned[: 2 * self.rows, pl.ds(j * self.inner, blocks * lines)] = tile.T
+
+    def turn_part(self, source, base, lines, result):
+        rows, wide, blocks = self.rows, self.inner // 2, self.inner // self.rows
+        count = blocks * lines
+        for j in range(self.outer):
+            tile = source[pl.ds(j * blocks, blocks), pl.ds(base, lines), :].reshape(count, 2 * rows).T
+            result[j, :, pl.ds(base * blocks, count)] = tile[:rows]
+            result[j, :, pl.ds(wide + base * blocks, count)] = tile[rows:]
+
+    def incoming_side(self, side, spans, twiddle, matrix, flip=None, extra=None):
+        rows, inner = self.rows, self.inner
+        wide = matrix.shape[2] // 2
+        held = twiddle.at[:, :, pl.ds(side * wide, wide)]
+        transform = small_dft if spans == self.outer else half_dft
+
+        def body(r0):
+            at = pl.ds(r0, self.step)
+            items = []
+            for j in range(spans):
+                lanes = pl.ds(j * inner, wide)
+                items.append((self.turned[at, lanes], self.turned[pl.ds(rows + r0, self.step), lanes]))
+            for k, (re, im) in enumerate(transform(items, 1.0)):
+                if extra is not None:
+                    re = re - extra[at, :wide] if k % 2 else re + extra[at, :wide]
+                for part, value in enumerate(self.twist(k, (re, im), 1.0, held, flip)):
+                    top, low = halves(value)
+                    self.top[k, at, pl.ds(part * wide, wide)] = top
+                    self.low[k, at, pl.ds(part * wide, wide)] = low
+
+        self.chunks(rows, body)
+        deep, count = 2 * wide, self.outer * rows
+        top = self.top[:, :rows, :deep].reshape(count, deep)
+        low = self.low[:, :rows, :deep].reshape(count, deep)
+        right_top, right_low = matrix[0, side], matrix[1, side]
+        dot = functools.partial(jnp.dot, preferred_element_type=jnp.float32)
+        total = dot(top, right_top) + dot(low, right_top) + dot(top, right_low)
+        total = total.reshape(self.outer, rows, inner)
+        if side:
+            total = self.z[:, :rows, :inner] + total
+        self.z[:, :rows, :inner] = total
 
     def first_imaginary(self, at):
         rows = self.rows
@@ -832,7 +878,7 @@
         for move in moves:
             links.receive(*move)
 
-    tw_natural, tw_kept, tw_lines, tw_cut = (inputs.twiddles.at[i] for i in range(4))
+    tw_natural, tw_kept, tw_lines, tw_cut, tw_sided = (inputs.twiddles.at[i] for i in range(5))
     forward, backward, mirror = inputs.forward, inputs.backward, inputs.mirror
     kept_out, kept_in, kept = inputs.kept_out, inputs.kept_in, inputs.kept
     lines_in, cut_in = box.lines_in, box.cut_in
@@ -901,12 +947,20 @@
     if parts != 2 * cuts:
         permute_rows(TILE * parts // (2 * rows), lines_in)
     permute_rows(TILE * cuts // rows, cut_in)
+    for side in sides:
+        for p in range(2):
+            for part in range(2):
+                for s in range(inner // rows):
+                    at = part * (inner // parts) + s * count
+                    source = part * inner + s * rows + side * count
+                    box.sided[p, side, pl.ds(at, count), :] = backward[p, pl.ds(source, count), :inner]
     slope_second(both_p, second)
     m_slope = turn_slopes(m_field, box.r_field, box.s_slope, box.r_slope)
     piece.spread(inputs.forcing.at[0], inputs.forcing.at[1], strided, forcing_p)
 
-    receive(*m_slope)
-    piece.turn_columns(box.r_slope, first)
+    for q in range(cuts):
+        receive(m_slope[q])
+        piece.turn_part(box.r_slope, q * half // cuts, half // cuts, first)
 
     def nonlinear(r0):
         at = pl.ds(r0, step)
@@ -958,12 +1012,14 @@
         piece.outgoing(count, 1.0, tw_natural, backward, False, piece.write_full(sent, False))
         m_next.append(send(at_all(sent), at_lines(box.r_next, side * count, count)))
 
-    receive(*m_next)
-    piece.turn_whole(box.r_next, length // TILE)
-    low, high = piece.first_imaginary(0), piece.first_imaginary(length // 2)
-    piece.turned[:rows, pl.ds(0, TILE)] += high
-    piece.turned[:rows, pl.ds(length // 2, TILE)] += low
-    piece.incoming(rows, 1.0, tw_natural, backward, real_out=True)
+    for side in sides:
+        receive(m_next[side])
+        piece.turn_side(box.r_next, side * count, count, outer)
+        if side == 0:
+            low, high = piece.first_imaginary(0), piece.first_imaginary(length // 2)
+            piece.turned[:rows, pl.ds(0, TILE)] += high
+            piece.turned[:rows, pl.ds(length // 2, TILE)] += low
+        piece.incoming_side(side, outer, tw_sided, box.sided)
     total[...] = jnp.zeros_like(total)
 
     def misfit(r0):
@@ -1022,11 +1078,12 @@
         piece.outgoing_half(count, 1.0, tw_natural, backward, flip, piece.write_full(sent, False))
         m_back.append(send(at_all(sent), at_lines(box.r_back, side * count, count), part_devices))
 
-    receive(*m_back)
-    piece.turn_whole(box.r_back, length // (2 * TILE))
-    box.extra[:, pl.ds(0, TILE)] = piece.first_imaginary(0)
-    box.extra[:, pl.ds(TILE, inner - TILE)] = jnp.zeros((rows, inner - TILE), jnp.float32)
-    piece.incoming_half(rows, 1.0, tw_natural, backward, flip, box.extra, real_out=True)
+    for side in sides:
+        receive(m_back[side])
+        piece.turn_side(box.r_back, side * count, count, outer // 2)
+        if side == 0:
+            box.extra[...] = piece.first_imaginary(0)
+        piece.incoming_side(side, outer // 2, tw_sided, box.sided, flip, None if side else box.extra)
 
     def products(r0):
         at = pl.ds(r0, step)
@@ -1048,8 +1105,9 @@
     receive(m_total)
     outs.total[...] = jnp.sum(box.r_total[...], axis=0) / (length * length)
 
-    receive(*m_last)
-    piece.turn_columns(box.r_last, first)
+    for q in range(cuts):
+        receive(m_last[q])
+        piece.turn_part(box.r_last, q * half // cuts, half // cuts, first)
     for k in range(outer):
         outs.field[k] = first[k] + value[k]
     for move in order:
@@ -1063,10 +1121,11 @@
     natural, kept = orders(length, rows)[:2]
     lines = line_order(inner, rows, TILE * parts // (2 * rows))
     cut = line_order(inner, rows, TILE * cuts // rows)
+    sided = natural.reshape(inner // rows, parts, rows // parts).transpose(1, 0, 2).reshape(inner)
     matrix = lambda *args: matrix_table(length, *args)
     tables = dict(
         field=field, target=target,
-        twiddles=np.stack([twiddle_table(length, o) for o in (natural, kept, lines, cut)]),
+        twiddles=np.stack([twiddle_table(length, o) for o in (natural, kept, lines, cut, sided)]),
         kept=kept[None, :].astype(np.int32),
         kept_out=matrix(-1.0, natural, kept)[:, :inner],
         kept_in=matrix(1.0, kept, natural)[:, :, :inner],
@@ -1091,7 +1150,7 @@
         turned=held(2 * rows, length), top=halved, low=halved, z=held(outer, rows, 2 * inner),
         strided=held(length, TILE), total=held(step, inner),
         both_p=pair, forcing_p=pair, full=pair, first=one, second=one, value=one, product=one,
-        lines_in=table, cut_in=table, extra=held(rows, inner),
+        lines_in=table, cut_in=table, extra=held(rows, TILE), sided=pltpu.VMEM((2, parts, 2 * inner // parts, inner), jnp.bfloat16),
         s_field=columns, r_field=columns, s_slope=slopes, r_slope=returned,
         s_sum=packed_half, r_sum=packed_half, s_next=lined, r_next=held(devices, rows, 2 * rows),
         s_kept=packed, r_kept=packed, s_total=small, r_total=small,

time: 129 us -> 128 us (level)
  no operation moved by 1% of the time
where the time goes in v7:
time: 128 us
  Pallas kernels  127 us (99%)
    pallas_call x1, Pallas kernels, joined_step(): pl.pallas_call(body, out_shape=(shape(rows, length), shape(outer, rows, i...  125 us

profile of v7, /device:TPU:0, one launch (start us, length us, event | category | flops | bytes accessed | tf_op | source)
XLA Modules:
  0.0 127.8 jit_solution(16713979680147283725)
XLA Ops:
  0.6 125.0 %shard_map.129 = (f32[64,2048]{1,0:T(8,128)S(1)}, f32[8,64,256]{2,1,0:T(8,128)S(1)}, f32[2,64,2048]{2,1,0:T(8,128)S(1)}, f32[1,128]{1,0:T(1,128)S(1)}) custom-call(f32[64,2048]{1,0:T(8,128)} %bitcast.5, f32[64,2048]{1,0:T(8,128)} %bitcast.6, f32[5,2,8,256]{3,2,1,0:T(8,128)} %constant.7.clone.refs_2_, s32[1,256]{1,0:T(1,128)} %constant.16.clone.refs_3_, ...), custom_call_target="tpu_custom_call" | custom-call | flops 60000002048 | bytes 4194304 | tf_op jit(solution)/shard_map/pallas_call | solution.py:1174
  125.6 2.0 %shard_map.130 = (f32[64,2048]{1,0:T(8,128)}, f32[64,2048]{1,0:T(8,128)}, f32[2,64,2048]{2,1,0:T(8,128)}, f32[1,1]{1,0:T(1,128)}) custom-call(f32[64,2048]{1,0:T(8,128)S(1)} %get-tuple-element.12.next_field, f32[8,64,256]{2,1,0:T(8,128)S(1)} %get-tuple-element.13.slabs, f32[2,64,2048]{2,1,0:T(8,128)S(1)} %get-tuple-element.14.forcing_grad, ...), custom_call_target="tpu_custom_call" | custom-call | flops 1000000000 | bytes 4194304 | tf_op jit(solution)/shard_map/pallas_call | solution.py:1183

commit v8 on v7

--- a/solution.py
+++ b/solution.py
@@ -284,7 +284,7 @@
             result[j, :, pl.ds(base * blocks, count)] = tile[:rows]
             result[j, :, pl.ds(wide + base * blocks, count)] = tile[rows:]
 
-    def incoming_side(self, side, spans, twiddle, matrix, flip=None, extra=None):
+    def incoming_side(self, side, spans, twiddle, matrix, add, flip=None, extra=None):
         rows, inner = self.rows, self.inner
         wide = matrix.shape[2] // 2
         held = twiddle.at[:, :, pl.ds(side * wide, wide)]
@@ -312,7 +312,7 @@
         dot = functools.partial(jnp.dot, preferred_element_type=jnp.float32)
         total = dot(top, right_top) + dot(low, right_top) + dot(top, right_low)
         total = total.reshape(self.outer, rows, inner)
-        if side:
+        if add:
             total = self.z[:, :rows, :inner] + total
         self.z[:, :rows, :inner] = total
 
@@ -469,6 +469,29 @@
             slab = strided[pl.ds(k, self.inner, stride=self.outer), :].T
             result[k] = slab[: 2 * rows, :]
 
+    def spread_one(self, source, strided, result, base):
+        rows, wide = self.rows, self.inner // 2
+        tiles = self.length // (2 * TILE)
+        for t in range(tiles):
+            pair = [source[:, pl.ds(at * TILE, TILE)] for at in (t, t + tiles)]
+            strided[pl.ds(t * TILE, TILE), :] = jnp.concatenate(pair, axis=0).T
+        for k in range(self.outer):
+            slab = strided[pl.ds(k, wide, stride=self.outer), :].T
+            result[k, pl.ds(base, rows), pl.ds(0, wide)] = slab[:rows]
+            result[k, pl.ds(base, rows), pl.ds(wide, wide)] = slab[rows:]
+
+    def collect_one(self, slabs, strided, result):
+        rows, wide = self.rows, self.inner // 2
+        tiles = self.length // (2 * TILE)
+        for k in range(self.outer):
+            slab = slabs(k)
+            pair = jnp.concatenate([slab[:, :wide], slab[:, wide:]], axis=0)
+            strided[pl.ds(k, wide, stride=self.outer), :] = pair.T
+        for t in range(tiles):
+            block = strided[pl.ds(t * TILE, TILE), :].T
+            result[:, pl.ds(t * TILE, TILE)] = block[:rows]
+            result[:, pl.ds((t + tiles) * TILE, TILE)] = block[rows:]
+
     def collect(self, slabs, strided, results):
         rows = self.rows
         for k in range(self.outer):
@@ -855,8 +878,7 @@
         pltpu.make_async_copy(ref, held, copies.at[i])
         for i, (ref, held) in enumerate(zip(inputs.refs, inputs.held))
     ]
-    for copy in loads[:2]:
-        copy.start()
+    loads[0].start()
     links.greet()
     waiting = iter(loads)
 
@@ -935,15 +957,16 @@
         mine, theirs = jnp.where(late, middle, 0), jnp.where(late, 0, middle)
         return [inverse_denominator(wave, signed_waves(p, length)[0]) for p in (mine, theirs)]
 
-    load(2)
-    for copy in loads[2:]:
+    load(1)
+    for copy in loads[1:]:
         copy.start()
-    piece.spread(inputs.field, inputs.target, strided, both_p)
+    piece.spread_one(inputs.field, strided, both_p, 0)
     piece.pack_cut(lambda k: both_p[k, pl.ds(0, rows), :], [box.s_field.at[q] for q in range(cuts)])
     links.meet()
     m_field = send_columns(box.s_field, box.r_field)
 
-    load(len(loads) - 2)
+    load(len(loads) - 1)
+    piece.spread_one(inputs.target, strided, both_p, rows)
     if parts != 2 * cuts:
         permute_rows(TILE * parts // (2 * rows), lines_in)
     permute_rows(TILE * cuts // rows, cut_in)
@@ -970,7 +993,8 @@
 
     piece.chunks(rows, nonlinear)
     piece.outgoing_sides(tw_natural, forward, [box.s_sum.at[side] for side in sides], late)
-    m_sum = [send(at_all(box.s_sum.at[side]), at_all(box.r_sum.at[side]), part_devices) for side in sides]
+    backwards = sides[::-1]
+    m_sum = [send(at_all(box.s_sum.at[side]), at_all(box.r_sum.at[side]), part_devices) for side in backwards]
 
     def divide(side):
         def body(r0):
@@ -1003,8 +1027,8 @@
                     replace(piece, k, part, 0.5 * ((joined + joined_c) * mine + (own - own_c) * theirs))
 
     m_next = []
-    for side in sides:
-        receive(m_sum[side])
+    for side, move in zip(backwards, m_sum):
+        receive(move)
         piece.turn_cut(box.r_sum.at[side], count, outer // 2)
         piece.incoming_half(count, -1.0, tw_lines, lines_in, flip)
         divide(side)
@@ -1012,14 +1036,14 @@
         piece.outgoing(count, 1.0, tw_natural, backward, False, piece.write_full(sent, False))
         m_next.append(send(at_all(sent), at_lines(box.r_next, side * count, count)))
 
-    for side in sides:
-        receive(m_next[side])
+    for side, move in zip(backwards, m_next):
+        receive(move)
         piece.turn_side(box.r_next, side * count, count, outer)
         if side == 0:
             low, high = piece.first_imaginary(0), piece.first_imaginary(length // 2)
             piece.turned[:rows, pl.ds(0, TILE)] += high
             piece.turned[:rows, pl.ds(length // 2, TILE)] += low
-        piece.incoming_side(side, outer, tw_sided, box.sided)
+        piece.incoming_side(side, outer, tw_sided, box.sided, side != backwards[0])
     total[...] = jnp.zeros_like(total)
 
     def misfit(r0):
@@ -1035,8 +1059,7 @@
     piece.outgoing_sides(tw_natural, forward, [box.s_kept.at[side] for side in sides])
     m_kept = [send(at_all(box.s_kept.at[side]), at_all(box.r_kept.at[side])) for side in sides]
     box.s_total[...] = jnp.full(box.s_total.shape, 0.5 * jnp.sum(total[...]), jnp.float32)
-    m_total = send(at_all(box.s_total), at_all(box.r_total))
-    piece.collect(lambda k: value[k], strided, [outs.next])
+    piece.collect_one(lambda k: value[k], strided, outs.next)
 
     def adjoint(side):
         def body(r0):
@@ -1078,12 +1101,13 @@
         piece.outgoing_half(count, 1.0, tw_natural, backward, flip, piece.write_full(sent, False))
         m_back.append(send(at_all(sent), at_lines(box.r_back, side * count, count), part_devices))
 
+    m_total = send(at_all(box.s_total), at_all(box.r_total))
     for side in sides:
         receive(m_back[side])
         piece.turn_side(box.r_back, side * count, count, outer // 2)
         if side == 0:
             box.extra[...] = piece.first_imaginary(0)
-        piece.incoming_side(side, outer // 2, tw_sided, box.sided, flip, None if side else box.extra)
+        piece.incoming_side(side, outer // 2, tw_sided, box.sided, side > 0, flip, None if side else box.extra)
 
     def products(r0):
         at = pl.ds(r0, step)
@@ -1201,7 +1225,7 @@
     copies[0].start()
     copies[1].start()
     total_out[0, 0] = jnp.sum(total[0:1, 0:1])
-    piece.collect(lambda k: slabs[k], strided, [held])
+    piece.collect_one(lambda k: slabs[k], strided, held)
     copies[2].start()
     for copy in copies:
         copy.wait()
@@ -1295,7 +1319,7 @@
             scratch_shapes=[strided],
         )(operand)
 
-    if rows * rows % (TILE * 32) == 0 and TILE % rows == 0:
+    if 2 * rows == TILE and inner == 2 * TILE:
         results = [
             joined_step(initial_field[m], target_field[m], forcing, devices, fast, rows, length)
             for m in range(members)

time: 128 us -> 128 us (level)
  no operation moved by 1% of the time
where the time goes in v8:
time: 128 us
  Pallas kernels  127 us (99%)
    pallas_call x1, Pallas kernels, joined_step(): pl.pallas_call(body, out_shape=(shape(rows, length), shape(outer, rows, i...  125 us

profile of v8, /device:TPU:0, one launch (start us, length us, event | category | flops | bytes accessed | tf_op | source)
XLA Modules:
  0.0 127.5 jit_solution(18271622522825279496)
XLA Ops:
  0.6 124.8 %shard_map.129 = (f32[64,2048]{1,0:T(8,128)S(1)}, f32[8,64,256]{2,1,0:T(8,128)S(1)}, f32[2,64,2048]{2,1,0:T(8,128)S(1)}, f32[1,128]{1,0:T(1,128)S(1)}) custom-call(f32[64,2048]{1,0:T(8,128)} %bitcast.5, f32[64,2048]{1,0:T(8,128)} %bitcast.6, f32[5,2,8,256]{3,2,1,0:T(8,128)} %constant.7.clone.refs_2_, s32[1,256]{1,0:T(1,128)} %constant.16.clone.refs_3_, ...), custom_call_target="tpu_custom_call" | custom-call | flops 60000002048 | bytes 4194304 | tf_op jit(solution)/shard_map/pallas_call | solution.py:1198
  125.5 1.9 %shard_map.130 = (f32[64,2048]{1,0:T(8,128)}, f32[64,2048]{1,0:T(8,128)}, f32[2,64,2048]{2,1,0:T(8,128)}, f32[1,1]{1,0:T(1,128)}) custom-call(f32[64,2048]{1,0:T(8,128)S(1)} %get-tuple-element.12.next_field, f32[8,64,256]{2,1,0:T(8,128)S(1)} %get-tuple-element.13.slabs, f32[2,64,2048]{2,1,0:T(8,128)S(1)} %get-tuple-element.14.forcing_grad, ...), custom_call_target="tpu_custom_call" | custom-call | flops 1000000000 | bytes 4194304 | tf_op jit(solution)/shard_map/pallas_call | solution.py:1207
